TPU v7x, 8 devices: a whole 2x2x1 slice. The times are simulated.
8 devices in a mesh: dp: 1 (over z), kv: 8 (over y, x, core).
Axes of the slice: x: 2, y: 2, z: 1, core: 2. Of those that a mesh axis runs over, the one named last changes fastest.
Arguments:
- x_in: bfloat16 [512, 1152], P('dp')
- positions: int32 [512], P('dp')
- k_cache: bfloat16 [512, 512, 256], P('dp', 'kv')
- v_cache: bfloat16 [512, 512, 256], P('dp', 'kv')
- slot_pos: int32 [512, 512], P('dp', 'kv')
- norm_scale: bfloat16 [1152], replicated
- w_q: bfloat16 [1152, 1024], replicated
- w_k: bfloat16 [1152, 256], replicated
- w_v: bfloat16 [1152, 256], replicated
- w_o: bfloat16 [1024, 1152], replicated
- b_o: bfloat16 [1152], replicated
Outputs:
- output 1: bfloat16 [512, 1152], P('dp')
- output 2: bfloat16 [512, 512, 256], P('dp', 'kv')
- output 3: bfloat16 [512, 512, 256], P('dp', 'kv')
- output 4: int32 [512, 512], P('dp', 'kv')
All inputs are finite; a program needn't handle non-finite values.
Results may differ from a plain program's by a relative error of at most 0.00589974.
Values sent between devices are 32-bit elements.
A program may use at most 1 GiB of HBM per device.

v0:
```python
import jax
import jax.numpy as jnp
from jax import lax
from jax.sharding import PartitionSpec as P

HEAD_DIM = 256
ROPE_DIM = 128
ROPE_BASE = 10000.0
EPS = 1e-6
NEG_LARGE = -1e30
SCORE_SCALE = HEAD_DIM ** -0.5


def rms_norm(x_in, norm_scale):
    x_f32 = x_in.astype(jnp.float32)
    mean_sq = jnp.mean(x_f32 * x_f32, axis=-1, keepdims=True)
    return (x_f32 * lax.rsqrt(mean_sq + EPS) * (1.0 + norm_scale.astype(jnp.float32))).astype(jnp.bfloat16)


def rope_tables(positions):
    rope_half = ROPE_DIM // 2
    inv_freq = ROPE_BASE ** (-jnp.arange(rope_half, dtype=jnp.float32) / rope_half)
    angles = positions.astype(jnp.float32)[:, None] * inv_freq[None, :]
    return jnp.cos(angles), jnp.sin(angles)


def rotate(tensor, cos_t, sin_t):
    rope_half = ROPE_DIM // 2
    rot_first = tensor[..., :rope_half]
    rot_second = tensor[..., rope_half:ROPE_DIM]
    return jnp.concatenate([rot_first * cos_t - rot_second * sin_t, rot_second * cos_t + rot_first * sin_t, tensor[..., ROPE_DIM:]], axis=-1)


def project_query(normed, cos_t, sin_t, w_q):
    q_full = jnp.dot(normed, w_q, preferred_element_type=jnp.float32)
    q_full = q_full.reshape(normed.shape[0], w_q.shape[1] // HEAD_DIM, HEAD_DIM)
    return rotate(q_full, cos_t[:, None, :], sin_t[:, None, :]).astype(jnp.bfloat16)


def project_kv(normed, cos_t, sin_t, w_k, w_v):
    k_new = rotate(jnp.dot(normed, w_k, preferred_element_type=jnp.float32), cos_t, sin_t).astype(jnp.bfloat16)
    v_new = jnp.dot(normed, w_v, preferred_element_type=jnp.float32).astype(jnp.bfloat16)
    return k_new, v_new


def write_slots(k_cache, v_cache, slot_pos, k_new, v_new, positions, slot_offset, window):
    slot_ids = slot_offset + jnp.arange(k_cache.shape[1], dtype=jnp.int32)
    hit_mask = slot_ids[None, :] == jnp.mod(positions, window)[:, None]
    k_out = jnp.where(hit_mask[:, :, None], k_new[:, None, :], k_cache)
    v_out = jnp.where(hit_mask[:, :, None], v_new[:, None, :], v_cache)
    slot_pos_out = jnp.where(hit_mask, positions[:, None], slot_pos)
    return k_out, v_out, slot_pos_out


def usable_slots(slot_pos_out, positions, window):
    slot_age = positions[:, None] - slot_pos_out
    return (slot_pos_out >= 0) & (slot_age >= 0) & (slot_age < window)


def partial_attention(q_rot, k_out, v_out, usable):
    scores = jnp.einsum('bhd,bsd->bhs', q_rot, k_out, preferred_element_type=jnp.float32) * SCORE_SCALE
    scores = jnp.where(usable[:, None, :], scores, NEG_LARGE)
    local_max = jnp.max(scores, axis=-1)
    weights = jnp.where(usable[:, None, :], jnp.exp(scores - local_max[..., None]), 0.0)
    local_sum = jnp.sum(weights, axis=-1)
    local_acc = jnp.einsum('bhs,bsd->bhd', weights.astype(jnp.bfloat16), v_out, preferred_element_type=jnp.float32)
    return local_max, local_sum, local_acc


def residual_out(x_in, attn_rows, w_o, b_o):
    return (x_in.astype(jnp.float32) + jnp.dot(attn_rows, w_o, preferred_element_type=jnp.float32) + b_o.astype(jnp.float32)).astype(jnp.bfloat16)


def solution(mesh):
    kv_size = mesh.shape['kv']
    row_spec = P('dp', None)
    cache_spec = P('dp', 'kv', None)
    slot_spec = P('dp', 'kv')
    vec_spec = P(None)
    mat_spec = P(None, None)

    def local_step(x_in, positions, k_cache, v_cache, slot_pos, norm_scale, w_q, w_k, w_v, w_o, b_o):
        local_slots = k_cache.shape[1]
        window = local_slots * kv_size
        slot_offset = lax.axis_index('kv') * local_slots
        normed = rms_norm(x_in, norm_scale)
        cos_t, sin_t = rope_tables(positions)
        q_rot = project_query(normed, cos_t, sin_t, w_q)
        k_new, v_new = project_kv(normed, cos_t, sin_t, w_k, w_v)
        k_out, v_out, slot_pos_out = write_slots(k_cache, v_cache, slot_pos, k_new, v_new, positions, slot_offset, window)
        usable = usable_slots(slot_pos_out, positions, window)
        local_max, local_sum, local_acc = partial_attention(q_rot, k_out, v_out, usable)
        global_max = lax.pmax(local_max, 'kv')
        factor = jnp.exp(local_max - global_max)
        total_sum, total_acc = lax.psum((local_sum * factor, local_acc * factor[..., None]), 'kv')
        attn_rows = (total_acc / total_sum[..., None]).astype(jnp.bfloat16).reshape(x_in.shape[0], w_q.shape[1])
        x_out = residual_out(x_in, attn_rows, w_o, b_o)
        return x_out, k_out, v_out, slot_pos_out

    return jax.shard_map(
        local_step,
        mesh=mesh,
        in_specs=(row_spec, P('dp'), cache_spec, cache_spec, slot_spec, vec_spec, mat_spec, mat_spec, mat_spec, mat_spec, vec_spec),
        out_specs=(row_spec, cache_spec, cache_spec, slot_spec),
        check_vma=False)
```

profile of v0, /device:TPU:0, one launch (start us, length us, event | category | flops | bytes accessed | tf_op | source)
XLA Modules:
  0.0 175.7 jit_solution(16976141253911541922)
XLA Ops:
  7.2 0.0 copy-start
  7.2 0.0 all-reduce.2.cloned.1.call-start
  7.2 0.5 multiply_power_fusion
  7.8 0.0 copy-start.2
  7.8 1.7 fusion.2
  9.5 0.8 fusion.26
  10.2 0.7 convert_add_fusion.1
  10.9 1.7 compare_and_fusion
  12.7 1.5 copy.15
  14.2 1.5 copy.18
  15.7 0.0 copy-start.10
  15.7 2.7 %convolution_convert_fusion = bf16[512,256]{1,0:T(8,128)(2,1)} fusion(bf16[1152,256]{1,0:T(8,128)(2,1)} %param.19, bf16[512,1152]{1,0:T(8,128)(2,1)} %param.11, f32[1152]{0:T(1024)S(1)} %convert_add_fusion.1, f32[512]{0:T(512)S(1)} %add_rsqrt_fusion), kind=kOutput, calls=%fused_computation.14 | convolution fusion | flops 304480256 | bytes 2038272 | tf_op jit(solution)/shard_map/dot_general | solution.py:42
  18.4 0.0 copy-done.2
  18.4 0.0 copy-done.10
  18.4 0.7 fusion.21
  19.1 0.7 slice.43
  19.8 0.0 copy-done.9
  19.8 1.3 multiply_cosine_fusion
  21.1 1.7 copy.16
  22.8 1.7 pad_maximum_fusion
  24.4 1.8 %copy.19 = bf16[512,256]{1,0:T(8,128)(2,1)} copy(bf16[512,256]{0,1:T(8,128)(2,1)} %pad_maximum_fusion) | data formatting | bytes 524288 | tf_op jit(solution)/shard_map/concatenate | solution.py:31
  26.2 1.7 copy.17
  28.0 4.5 %fusion.23 = f32[512,1024]{1,0:T(8,128)} fusion(bf16[1152,1024]{1,0:T(8,128)(2,1)} %param.17, bf16[512,1152]{1,0:T(8,128)(2,1)S(1)} %copy-done.2, f32[1152]{0:T(1024)S(1)} %convert_add_fusion.1, f32[512]{0:T(512)S(1)} %add_rsqrt_fusion), kind=kOutput, calls=%fused_computation.50 | convolution fusion | flops 1210318848 | bytes 5642752 | tf_op jit(solution)/shard_map/dot_general | solution.py:35
  32.5 3.2 %reshape.134 = f32[512,4,256]{2,1,0:T(4,128)} reshape(f32[512,1024]{1,0:T(8,128)} %fusion.23) | data formatting | bytes 4194304 | tf_op jit(solution)/shard_map/reshape | solution.py:36
  35.7 2.2 %slice.42 = bf16[512,4,128]{2,1,0:T(4,128)(2,1)} slice(f32[512,4,256]{2,1,0:T(4,128)} %reshape.134), slice={[0:512], [0:4], [128:256]} | slice | bytes 1048576 | tf_op jit(solution)/shard_map/slice | solution.py:31
  38.0 0.0 copy-done.5
  38.0 3.3 %subtract_convert_fusion = (bf16[512,4,64]{2,1,0:T(4,128)(2,1)S(1)}, bf16[512,4,64]{2,1,0:T(4,128)(2,1)}) fusion(f32[512,4,256]{2,1,0:T(4,128)} %reshape.134, f32[512,64]{1,0:T(8,128)} %copy.17, f32[512,64]{1,0:T(8,128)S(1)} %copy-done.5), kind=kLoop, calls=%fused_computation.23 | loop fusion | flops 1048576 | bytes 1835008 | tf_op jit(solution)/shard_map/convert.4
  41.2 0.0 copy-done.4
  41.2 0.0 copy-done.7
  41.3 22.8 %broadcast_select_fusion.1 = (bf16[512,64,256]{2,1,0:T(8,128)(2,1)}, bf16[512,64,256]{2,1,0:T(8,128)(2,1)}) fusion(bf16[512,64,256]{2,1,0:T(8,128)(2,1)} %param.13, pred[512,64]{1,0:T(8,128)(4,1)S(1)} %copy-done.7, bf16[512,256]{1,0:T(8,128)(2,1)S(1)} %copy-done.4, bf16[512,64,256]{2,1,0:T(8,128)(2,1)} %param.14, bf16[512,256]{1,0:T(8,128)(2,1)} %convolution_convert_fusion), kind=kLoop, calls=%fused_computation.1 | loop fusion | flops 16777216 | bytes 67665920 | tf_op jit(solution)/shard_map/jit(_where)/select_n | solution.py:49
  64.1 0.0 copy-done.6
  64.1 9.4 %fusion.27 = (f32[512,4]{1,0:T(8,128)S(1)}, f32[512,4,64]{2,1,0:T(4,128)}) fusion(bf16[512,64,256]{2,1,0:T(8,128)(2,1)} %get-tuple-element.12, bf16[512,4,128]{2,1,0:T(4,128)(2,1)} %slice.42, bf16[512,4,64]{2,1,0:T(4,128)(2,1)} %get-tuple-element.9, bf16[512,4,64]{2,1,0:T(4,128)(2,1)S(1)} %get-tuple-element.8, pred[512,64]{1,0:T(8,128)(4,1)S(1)} %copy-done.6), kind=kOutput, calls=%fused_computation.53 | convolution fusion | flops 70645760 | bytes 18391040 | tf_op jit(solution)/shard_map/bhd,bsd->bhs/dot_general | solution.py:61
  73.4 27.8 %pmax.7 = f32[512,4]{1,0:T(8,128)S(1)} all-reduce(f32[512,4]{1,0:T(8,128)S(1)} %get-tuple-element.21), channel_id=1, replica_groups=mesh['dp'=1,'kv'=8] {'kv'}, use_global_device_ids=true, to_apply=%region_2.3 | all-reduce | flops 2048 | bytes 16384 | tf_op jit(solution)/shard_map/pmax | solution.py:93
  101.2 0.0 copy-start.1
  101.2 2.7 %fusion.11 = f32[512,4]{1,0:T(8,128)S(1)} fusion(f32[512,4,64]{2,1,0:T(4,128)} %get-tuple-element.22, f32[512,4]{1,0:T(8,128)S(1)} %get-tuple-element.21, pred[512,64]{1,0:T(8,128)(4,1)S(1)} %copy-done.6), kind=kLoop, calls=%fused_computation.24 | loop fusion | flops 391168 | bytes 573440 | tf_op jit(solution)/shard_map/reduce_sum | solution.py:65
  103.9 0.1 fusion.25
  104.0 0.0 copy-done.1
  104.0 0.0 copy-start.8
  104.0 8.2 %convolution_multiply_fusion = f32[512,4,256]{2,1,0:T(4,128)} fusion(bf16[512,64,256]{2,1,0:T(8,128)(2,1)} %get-tuple-element.13, f32[512,4]{1,0:T(8,128)S(1)} %get-tuple-element.5, f32[512,4,64]{2,1,0:T(4,128)S(1)} %copy-done.1, f32[512,4]{1,0:T(8,128)S(1)} %get-tuple-element.21, pred[512,64]{1,0:T(8,128)(4,1)S(1)} %copy-done.6), kind=kOutput, calls=%fused_computation.11 | convolution fusion | flops 68026368 | bytes 19447808 | tf_op jit(solution)/shard_map/bhs,bsd->bhd/dot_general | solution.py:66
  112.2 0.0 all-reduce.2.cloned.1.call-update
  112.2 0.0 copy-done.8
  112.3 27.4 %psum.15 = f32[512,4]{1,0:T(8,128)} all-reduce(f32[512,4]{1,0:T(8,128)S(1)} %get-tuple-element.4), channel_id=1, replica_groups=mesh['dp'=1,'kv'=8] {'kv'}, use_global_device_ids=true, to_apply=%region_5.6 | all-reduce | flops 2048 | bytes 16384 | tf_op jit(solution)/shard_map/psum | solution.py:95
  139.6 24.5 %all-reduce.2.cloned.1.call-done = f32[512,4,256]{2,1,0:T(4,128)} async-done(((f32[512,4,256]{2,1,0:T(4,128)}), f32[512,4,256]{2,1,0:T(4,128)}) %all-reduce.2.cloned.1.call-update) | async-done | bytes 2097168 | tf_op jit(solution)/shard_map/psum | solution.py:95
  164.1 2.0 %divide_convert_fusion = bf16[512,4,256]{2,1,0:T(4,128)(2,1)S(1)} fusion(f32[512,4,256]{2,1,0:T(4,128)} %all-reduce.2.cloned.1.call-done, f32[512,4]{1,0:T(8,128)} %psum.15), kind=kLoop, calls=%fused_computation.10 | loop fusion | flops 1048576 | bytes 3153920 | tf_op jit(solution)/shard_map/convert_element_type | solution.py:96
  166.1 0.2 copy.20
  166.3 0.0 copy-done
  166.3 0.0 copy-done.3
  166.3 2.6 %fusion.1 = bf16[512,1152]{1,0:T(8,128)(2,1)} fusion(bf16[512,1024]{1,0:T(8,128)(2,1)S(1)} %bitcast.10, bf16[1024,1152]{1,0:T(8,128)(2,1)S(1)} %copy-done, bf16[512,1152]{1,0:T(8,128)(2,1)S(1)} %copy-done.3, f32[1152]{0:T(1024)S(1)} %convert_element_type.41), kind=kOutput, calls=%fused_computation.6 | convolution fusion | flops 1210318848 | bytes 5771776 | tf_op jit(solution)/shard_map/dot_general | solution.py:71
  (9 shorter events, 0.0 us)
Async XLA Ops:
  7.2 159.2 %copy-start = (bf16[1024,1152]{1,0:T(8,128)(2,1)S(1)}, bf16[1024,1152]{1,0:T(8,128)(2,1)}, u32[]{:S(2)}) copy-start(bf16[1024,1152]{1,0:T(8,128)(2,1)} %param.20) | copy-start | bytes 7077892
  7.2 156.9 %all-reduce.2.cloned.1.call-start = ((), (), s32[]{:S(2)}) async-start(), calls=%async_computation | async-start | bytes 4194304 | tf_op jit(solution)/shard_map/psum | solution.py:95
  7.8 10.7 %copy-start.2 = (bf16[512,1152]{1,0:T(8,128)(2,1)S(1)}, bf16[512,1152]{1,0:T(8,128)(2,1)}, u32[]{:S(2)}) copy-start(bf16[512,1152]{1,0:T(8,128)(2,1)} %param.11) | copy-start | bytes 3538948
  15.7 2.7 %copy-start.10 = (bf16[1152,256]{1,0:T(8,128)(2,1)S(1)}, bf16[1152,256]{1,0:T(8,128)(2,1)}, u32[]{:S(2)}) copy-start(bf16[1152,256]{1,0:T(8,128)(2,1)} %param.18) | copy-start | bytes 1769476
  18.4 1.4 copy-start.9
  32.5 5.4 %copy-start.5 = (f32[512,64]{1,0:T(8,128)S(1)}, f32[512,64]{1,0:T(8,128)}, u32[]{:S(2)}) copy-start(f32[512,64]{1,0:T(8,128)} %copy.16) | copy-start | bytes 393220
  35.7 5.5 %copy-start.4 = (bf16[512,256]{1,0:T(8,128)(2,1)S(1)}, bf16[512,256]{1,0:T(8,128)(2,1)}, u32[]{:S(2)}) copy-start(bf16[512,256]{1,0:T(8,128)(2,1)} %copy.19) | copy-start | bytes 786436
  35.7 5.5 %copy-start.7 = (pred[512,64]{1,0:T(8,128)(4,1)S(1)}, pred[512,64]{1,0:T(8,128)(4,1)}, u32[]{:S(2)}) copy-start(pred[512,64]{1,0:T(8,128)(4,1)} %copy.18) | copy-start | bytes 98308
  41.2 22.8 %copy-start.6 = (pred[512,64]{1,0:T(8,128)(4,1)S(1)}, pred[512,64]{1,0:T(8,128)(4,1)}, u32[]{:S(2)}) copy-start(pred[512,64]{1,0:T(8,128)(4,1)} %copy.15) | copy-start | bytes 98308
  101.2 2.8 %copy-start.1 = (f32[512,4,64]{2,1,0:T(4,128)S(1)}, f32[512,4,64]{2,1,0:T(4,128)}, u32[]{:S(2)}) copy-start(f32[512,4,64]{2,1,0:T(4,128)} %get-tuple-element.22) | copy-start | bytes 1572868
  104.0 8.2 %copy-start.8 = (bf16[1152]{0:T(1024)(128)(2,1)S(1)}, bf16[1152]{0:T(1024)(128)(2,1)}, u32[]{:S(2)}) copy-start(bf16[1152]{0:T(1024)(128)(2,1)} %param.21) | copy-start | bytes 6916
  139.6 26.7 %copy-start.3 = (bf16[512,1152]{1,0:T(8,128)(2,1)S(1)}, bf16[512,1152]{1,0:T(8,128)(2,1)}, u32[]{:S(2)}) copy-start(bf16[512,1152]{1,0:T(8,128)(2,1)} %param.11) | copy-start | bytes 3538948
Sparse Core Ops, SparseCore 0:
  112.4 51.7 all-reduce.1
where the time goes:
time: 176 us
  blocking collectives  55.1 us (31%)
  other arithmetic  39.1 us (22%)
  matrix products  28.1 us (16%)
  waiting for transfers between devices  24.5 us (14%)
  local copies, waits for them, and re-layouts  14.7 us (8%)
  between operations  14.2 us (8%)
    pmax x1, blocking collectives, local_step(): global_max = lax.pmax(local_max, 'kv')  27.8 us
    psum x1, blocking collectives, local_step(): lax.psum((local_sum * factor, local_acc * factor[..., None]), 'kv')  27.4 us
    psum x1, waiting for transfers between devices, local_step(): lax.psum((local_sum * factor, local_acc * factor[..., None]), 'kv')  24.5 us
    select_n x1, other arithmetic, write_slots(): k_out = jnp.where(hit_mask[:, :, None], k_new[:, None, :], k_cache)  22.8 us
    dot_general x1, matrix products, partial_attention(): jnp.einsum('bhd,bsd->bhs', q_rot, k_out, preferred_element_type=jnp.float32)  9.36 us
    dot_general x1, matrix products, partial_attention(): jnp.einsum('bhs,bsd->bhd', weights.astype(jnp.bfloat16), v_out, preferred...  8.19 us
    dot_general x1, matrix products, project_query(): q_full = jnp.dot(normed, w_q, preferred_element_type=jnp.float32)  4.55 us
  transfers between devices with their start and end apart: 1, of which 1 were waited for; matrix products, arithmetic and copies ran while one was open for 0% of the time, Pallas kernels for 0%

commit v1 on v0

v1 whole, which is shorter than its diff:
```python
import functools

import jax
import jax.numpy as jnp
import numpy as np
from jax import lax
from jax.experimental import pallas as pl
from jax.experimental.pallas import tpu as pltpu
from jax.sharding import PartitionSpec as P

HEADS = 4
HEAD_DIM = 256
ROPE_DIM = 128
ROPE_HALF = ROPE_DIM // 2
ROPE_BASE = 10000.0
EPS = 1e-6
SCORE_SCALE = HEAD_DIM ** -0.5
NEG_LARGE = float(np.finfo(np.float32).min)
FAR = 1e9
F32 = jnp.float32
BF16 = jnp.bfloat16

BATCH = 512
D_MODEL = 1152
SLOTS = 64
QW = HEADS * HEAD_DIM
PW = QW + 128
GROUP = 8
STEP = 32
LOADS = BATCH // STEP
CHUNK = 64
NCHUNK = BATCH // CHUNK
ROWS = 256


def sin_cos(theta):
    k = jnp.floor(theta * np.float32(2.0 / np.pi) + 0.5)
    r = theta - k * np.float32(1.5703125)
    r = r - k * np.float32(4.83751296997070312e-4)
    r = r - k * np.float32(7.54978995489188e-8)
    r2 = r * r
    s = r + r * r2 * (-1.6666654611e-1 + r2 * (8.3321608736e-3 + r2 * -1.9515295891e-4))
    c = 1.0 - 0.5 * r2 + r2 * r2 * (4.166664568298827e-2 + r2 * (-1.388731625493765e-3 + r2 * 2.443315711809948e-5))
    q = k - 4.0 * jnp.floor(k * 0.25)
    swap = (q == 1.0) | (q == 3.0)
    sin_v = jnp.where(swap, c, s)
    cos_v = jnp.where(swap, s, c)
    sin_v = jnp.where(q >= 2.0, -sin_v, sin_v)
    cos_v = jnp.where((q == 1.0) | (q == 2.0), -cos_v, cos_v)
    return sin_v, cos_v


def inv_freq_row():
    i = np.arange(ROPE_DIM) % ROPE_HALF
    return (ROPE_BASE ** (-i / ROPE_HALF)).astype(np.float32).reshape(1, ROPE_DIM)


def attn_kernel(pos_row, freq_ref, sp_ref, ns_ref, x_hbm, wq_hbm, wk_hbm, wv_hbm, k_hbm, v_hbm,
                part_ref, sp_out, k_out, v_out,
                kbuf, vbuf, x_v, wq_v, wk_v, wv_v, n_v, q_v, kn_v, vn_v, p_col, js_col, cos_v, sin_v,
                w_sem, k_sem, v_sem, ko_sem, vo_sem):
    off = lax.axis_index('kv') * SLOTS
    weights = ((x_hbm, x_v), (wk_hbm, wk_v), (wv_hbm, wv_v), (wq_hbm, wq_v))
    for n, (src, dst) in enumerate(weights):
        pltpu.make_async_copy(src, dst, w_sem.at[n]).start()

    def rows_of(c):
        return pl.ds(pl.multiple_of(c * STEP, STEP), STEP)

    def k_in(c):
        return pltpu.make_async_copy(k_hbm.at[rows_of(c)], kbuf.at[rows_of(c)], k_sem.at[c])

    def v_in(c):
        return pltpu.make_async_copy(v_hbm.at[rows_of(c)], vbuf.at[rows_of(c)], v_sem.at[c])

    def k_back(c):
        return pltpu.make_async_copy(kbuf.at[rows_of(c)], k_out.at[rows_of(c)], ko_sem.at[c])

    def v_back(c):
        return pltpu.make_async_copy(vbuf.at[rows_of(c)], v_out.at[rows_of(c)], vo_sem.at[c])

    @pl.loop(0, LOADS)
    def _(c):
        k_in(c).start()
        v_in(c).start()

    offf = off.astype(F32)
    for t in range(BATCH // 128):
        row = jnp.broadcast_to(pos_row[:, t * 128:(t + 1) * 128].astype(F32), (128, 128))
        col = row.T
        p_col[pl.ds(t * 128, 128), :] = col
        js = col - 512.0 * jnp.floor(col * (1.0 / 512.0)) - offf
        js_col[pl.ds(t * 128, 128), :] = jnp.where((js >= 0.0) & (js < float(SLOTS)), js, -1.0)
        s, c = sin_cos(col * freq_ref[...])
        lane = lax.broadcasted_iota(jnp.int32, (128, 128), 1)
        sin_v[pl.ds(t * 128, 128), :] = jnp.where(lane < ROPE_HALF, -s, s)
        cos_v[pl.ds(t * 128, 128), :] = c

    p_all = pos_row[...]
    slot_ids = off + lax.broadcasted_iota(jnp.int32, (SLOTS, BATCH), 0)
    sp_out[...] = jnp.where(slot_ids == (p_all & 511), p_all, sp_ref[...])

    def rotate(t, rows):
        r = t[:, :ROPE_DIM]
        r = r * cos_v[rows, :] + pltpu.roll(r, ROPE_HALF, 1) * sin_v[rows, :]
        return jnp.concatenate([r, t[:, ROPE_DIM:]], axis=1)

    for n in range(3):
        src, dst = weights[n]
        pltpu.make_async_copy(src, dst, w_sem.at[n]).wait()

    @pl.loop(0, BATCH // ROWS)
    def _(i):
        rows = pl.ds(pl.multiple_of(i * ROWS, ROWS), ROWS)
        xf = x_v[rows, :].astype(F32)
        mean_sq = jnp.sum(xf * xf, axis=1, keepdims=True) * (1.0 / D_MODEL)
        n_v[rows, :] = (xf * lax.rsqrt(mean_sq + EPS) * (1.0 + ns_ref[...].astype(F32))).astype(BF16)
        kn = jnp.dot(n_v[rows, :], wk_v[...], preferred_element_type=F32)
        kn_v[rows, :] = rotate(kn, rows)
        vn_v[rows, :] = jnp.dot(n_v[rows, :], wv_v[...], preferred_element_type=F32)

    pltpu.make_async_copy(wq_hbm, wq_v, w_sem.at[3]).wait()

    @pl.loop(0, BATCH // ROWS)
    def _(i):
        rows = pl.ds(pl.multiple_of(i * ROWS, ROWS), ROWS)

        @pl.loop(0, HEADS)
        def _(h):
            cols = pl.ds(pl.multiple_of(h * HEAD_DIM, HEAD_DIM), HEAD_DIM)
            qh = jnp.dot(n_v[rows, :], wq_v[:, cols], preferred_element_type=F32)
            q_v[rows, cols] = rotate(qh, rows) * SCORE_SCALE

    sub = lax.broadcasted_iota(jnp.int32, (GROUP, 128), 0)
    lane = lax.broadcasted_iota(jnp.int32, (GROUP, 128), 1)
    slot_c = jnp.where((lane // SLOTS) == (sub % 2), (lane % SLOTS).astype(F32) + offf, FAR)
    pick = [(sub // 2) == cc for cc in range(4)]
    iotas = [(lax.broadcasted_iota(jnp.int32, (16, HEAD_DIM), 0) + 16 * t).astype(F32).astype(BF16) for t in range(SLOTS // 16)]

    def refresh(buf, new_ref, b, hits):
        fresh = jnp.broadcast_to(new_ref[pl.ds(b, 1), :], (16, HEAD_DIM)).astype(BF16)
        out = []
        for t in range(SLOTS // 16):
            piece = jnp.where(hits[t], fresh, buf[b, pl.ds(16 * t, 16), :])
            buf[b, pl.ds(16 * t, 16), :] = piece
            out.append(piece)
        return out

    def group(r0):
        ks, vs = [], []
        for i in range(GROUP):
            b = r0 + i
            js = jnp.broadcast_to(js_col[pl.ds(b, 1), :], (16, 128)).astype(BF16)
            js = jnp.concatenate([js, js], axis=1)
            hits = [io == js for io in iotas]
            ks += refresh(kbuf, kn_v, b, hits)
            vs += refresh(vbuf, vn_v, b, hits)
        rows = pl.ds(r0, GROUP)
        q = jnp.concatenate([q_v[rows, h * HEAD_DIM:(h + 1) * HEAD_DIM] for h in range(HEADS)], axis=0).astype(BF16)
        kmat = jnp.concatenate(ks, axis=0)
        vmat = jnp.concatenate(vs, axis=0)
        s = lax.dot_general(q, kmat, (((1,), (1,)), ((), ())), preferred_element_type=F32)
        valid = slot_c <= p_col[rows, :]
        stats = jnp.zeros((GROUP, 128), F32)
        ps = []
        for h in range(HEADS):
            sh = s[h * GROUP:(h + 1) * GROUP, :]
            c = sh[:, 384:512]
            for cc in range(3):
                c = jnp.where(pick[cc], sh[:, cc * 128:(cc + 1) * 128], c)
            c = jnp.where(valid, c, NEG_LARGE)
            m = jnp.max(c, axis=1, keepdims=True)
            e = jnp.where(valid, jnp.exp(c - m), 0.0)
            l = jnp.sum(e, axis=1, keepdims=True)
            stats = jnp.where(lane == h, m, stats)
            stats = jnp.where(lane == HEADS + h, l, stats)
            ps.append(jnp.concatenate([jnp.where(pick[cc], e, 0.0) for cc in range(4)], axis=1))
        pm = jnp.concatenate(ps, axis=0).astype(BF16)
        o = jnp.dot(pm, vmat, preferred_element_type=F32)
        for h in range(HEADS):
            part_ref[rows, h * HEAD_DIM:(h + 1) * HEAD_DIM] = o[h * GROUP:(h + 1) * GROUP, :]
        part_ref[rows, QW:PW] = stats

    @pl.loop(0, LOADS)
    def _(c):
        k_in(c).wait()
        v_in(c).wait()
        for g in range(STEP // GROUP):
            group(pl.multiple_of(c * STEP + g * GROUP, GROUP))
        k_back(c).start()
        v_back(c).start()

    @pl.loop(0, LOADS)
    def _(c):
        k_back(c).wait()
        v_back(c).wait()


def merge_rows(a_rows, b_rows):
    sa, sb = a_rows[1], b_rows[1]
    lane = lax.broadcasted_iota(jnp.int32, sa.shape, 1)
    ma, mb = sa, sb
    mm = jnp.maximum(ma, mb)
    fa, fb = jnp.exp(ma - mm), jnp.exp(mb - mm)
    fa_l = pltpu.roll(fa, HEADS, 1)
    fb_l = pltpu.roll(fb, HEADS, 1)
    stats = jnp.where(lane < HEADS, mm, sa * fa_l + sb * fb_l)
    vals = []
    for h in range(HEADS):
        va = a_rows[0][:, h * HEAD_DIM:(h + 1) * HEAD_DIM]
        vb = b_rows[0][:, h * HEAD_DIM:(h + 1) * HEAD_DIM]
        vals.append(va * fa[:, h:h + 1] + vb * fb[:, h:h + 1])
    return jnp.concatenate(vals, axis=1), stats


class Places:
    def __init__(self):
        me = lax.axis_index('kv')
        self.core = me % 2
        self.x = (me // 2) % 2
        self.y = me // 4
        self.mate = me + 1 - 2 * self.core
        self.x_peer = me + 2 - 4 * self.x
        self.y_peer = me + 4 - 8 * self.y

    def first(self, c):
        odd = c % 2
        return self.x_peer + odd * (self.y_peer - self.x_peer), self.x + odd * (self.y - self.x)

    def second(self, c):
        odd = c % 2
        return self.y_peer + odd * (self.x_peer - self.y_peer), self.y + odd * (self.x - self.y)


def enter(pl_):
    barrier = pltpu.get_barrier_semaphore()
    for peer in (pl_.mate, pl_.x_peer, pl_.y_peer):
        pl.semaphore_signal(barrier, inc=1, device_id={'kv': peer}, device_id_type=pl.DeviceIdType.MESH)
    pl.semaphore_wait(barrier, 3)


def send(src, dst, ss, rs, peer):
    return pltpu.make_async_remote_copy(src_ref=src, dst_ref=dst, send_sem=ss, recv_sem=rs,
                                        device_id={'kv': peer}, device_id_type=pl.DeviceIdType.MESH)


def al(v, m=8):
    return pl.multiple_of(v, m)


class Reduce:
    def __init__(self, places, part, r0, r1, r2, own, sems):
        self.p = places
        self.part, self.r0, self.r1, self.r2, self.own = part, r0, r1, r2, own
        self.s0s, self.s0r, self.s1s, self.s1r, self.s2s, self.s2r = sems

    def copy0(self, c):
        src = al(c * CHUNK + 32 * (1 - self.p.core))
        return send(self.part.at[pl.ds(src, 32)], self.r0.at[pl.ds(al(c * 32), 32)], self.s0s.at[c], self.s0r.at[c], self.p.mate)

    def copy1(self, c):
        peer, k = self.p.first(c)
        src = al(c * CHUNK + 32 * self.p.core + 16 * (1 - k))
        return send(self.part.at[pl.ds(src, 16)], self.r1.at[pl.ds(al(c * 16), 16)], self.s1s.at[c], self.s1r.at[c], peer)

    def copy2(self, c):
        peer, k2 = self.p.second(c)
        k1 = self.p.first(c)[1]
        src = al(c * CHUNK + 32 * self.p.core + 16 * k1 + 8 * (1 - k2))
        return send(self.part.at[pl.ds(src, 8)], self.r2.at[pl.ds(al(c * 8), 8)], self.s2s.at[c], self.s2r.at[c], peer)

    def merge(self, mine, other_ref, theirs):
        a = self.part[pl.ds(mine, 8), :]
        b = other_ref[pl.ds(theirs, 8), :]
        return merge_rows((a[:, :QW], a[:, QW:]), (b[:, :QW], b[:, QW:]))

    def step0(self, c):
        self.copy0(c).wait_recv()
        base = c * CHUNK + 32 * self.p.core
        for t in range(4):
            v, s = self.merge(al(base + 8 * t), self.r0, al(c * 32 + 8 * t))
            self.part[pl.ds(al(base + 8 * t), 8), :] = jnp.concatenate([v, s], axis=1)

    def step1(self, c):
        self.copy1(c).wait_recv()
        base = c * CHUNK + 32 * self.p.core + 16 * self.p.first(c)[1]
        for t in range(2):
            v, s = self.merge(al(base + 8 * t), self.r1, al(c * 16 + 8 * t))
            self.part[pl.ds(al(base + 8 * t), 8), :] = jnp.concatenate([v, s], axis=1)

    def step2(self, c):
        self.copy2(c).wait_recv()
        base = c * CHUNK + 32 * self.p.core + 16 * self.p.first(c)[1] + 8 * self.p.second(c)[1]
        v, s = self.merge(al(base), self.r2, al(c * 8))
        outs = [v[:, h * HEAD_DIM:(h + 1) * HEAD_DIM] / s[:, HEADS + h:HEADS + h + 1] for h in range(HEADS)]
        self.own[pl.ds(al(base), 8), :] = jnp.concatenate(outs, axis=1)

    def drain(self, c):
        self.copy0(c).wait_send()
        self.copy1(c).wait_send()
        self.copy2(c).wait_send()


class Gather:
    def __init__(self, places, g, sems):
        self.p, self.g = places, g
        self.s0s, self.s0r, self.s1s, self.s1r, self.s2s, self.s2r = sems

    def copy0(self, c):
        peer, k2 = self.p.second(c)
        k1 = self.p.first(c)[1]
        rows = pl.ds(al(c * CHUNK + 32 * self.p.core + 16 * k1 + 8 * k2), 8)
        return send(self.g.at[rows], self.g.at[rows], self.s0s.at[c], self.s0r.at[c], peer)

    def copy1(self, c):
        peer, k1 = self.p.first(c)
        rows = pl.ds(al(c * CHUNK + 32 * self.p.core + 16 * k1), 16)
        return send(self.g.at[rows], self.g.at[rows], self.s1s.at[c], self.s1r.at[c], peer)

    def copy2(self, c):
        rows = pl.ds(al(c * CHUNK + 32 * self.p.core), 32)
        return send(self.g.at[rows], self.g.at[rows], self.s2s.at[c], self.s2r.at[c], self.p.mate)

    def drain(self, c):
        self.copy0(c).wait_send()
        self.copy1(c).wait_send()
        self.copy2(c).wait_send()


def comm_kernel(part_in, x_ref, wo_ref, b_ref, out_ref, part, r0, r1, r2, g, lsem, rsems, gsems):
    p = Places()
    cp = pltpu.make_async_copy(part_in, part, lsem)
    cp.start()
    cp.wait()
    enter(p)
    red = Reduce(p, part, r0, r1, r2, g, [rsems.at[i] for i in range(6)])
    gat = Gather(p, g, [gsems.at[i] for i in range(6)])

    @pl.loop(0, NCHUNK)
    def _(c):
        red.copy0(c).start()

    @pl.loop(0, NCHUNK)
    def _(c):
        red.step0(c)
        red.copy1(c).start()

    @pl.loop(0, NCHUNK)
    def _(c):
        red.step1(c)
        red.copy2(c).start()

    @pl.loop(0, NCHUNK)
    def _(c):
        red.step2(c)
        gat.copy0(c).start()

    @pl.loop(0, NCHUNK)
    def _(c):
        gat.copy0(c).wait_recv()
        gat.copy1(c).start()

    @pl.loop(0, NCHUNK)
    def _(c):
        gat.copy1(c).wait_recv()
        gat.copy2(c).start()

    @pl.loop(0, NCHUNK // 2)
    def _(i):
        gat.copy2(2 * i).wait_recv()
        gat.copy2(2 * i + 1).wait_recv()
        rows = pl.ds(al(i * 2 * CHUNK, 2 * CHUNK), 2 * CHUNK)
        o = g[rows, :].astype(BF16)
        y = x_ref[rows, :].astype(F32) + jnp.dot(o, wo_ref[...], preferred_element_type=F32) + b_ref[...].astype(F32)
        out_ref[rows, :] = y.astype(BF16)

    @pl.loop(0, NCHUNK)
    def _(c):
        red.drain(c)
        gat.drain(c)


def solution(mesh):
    row_spec = P('dp', None)
    cache_spec = P('dp', 'kv', None)
    slot_spec = P('dp', 'kv')
    vec_spec = P(None)
    mat_spec = P(None, None)
    hbm = pl.BlockSpec(memory_space=pltpu.HBM)
    vmem = pl.BlockSpec(memory_space=pltpu.VMEM)

    def local_step(x_in, positions, k_cache, v_cache, slot_pos, norm_scale, w_q, w_k, w_v, w_o, b_o):
        part, sp_t, k_out, v_out = pl.pallas_call(
            attn_kernel,
            out_shape=(jax.ShapeDtypeStruct((BATCH, PW), F32),
                       jax.ShapeDtypeStruct((SLOTS, BATCH), jnp.int32),
                       jax.ShapeDtypeStruct(k_cache.shape, BF16),
                       jax.ShapeDtypeStruct(v_cache.shape, BF16)),
            in_specs=[vmem, vmem, vmem, vmem, hbm, hbm, hbm, hbm, hbm, hbm],
            out_specs=(vmem, vmem, hbm, hbm),
            scratch_shapes=[
                pltpu.VMEM((BATCH, SLOTS, HEAD_DIM), BF16),
                pltpu.VMEM((BATCH, SLOTS, HEAD_DIM), BF16),
                pltpu.VMEM((BATCH, D_MODEL), BF16),
                pltpu.VMEM((D_MODEL, QW), BF16),
                pltpu.VMEM((D_MODEL, HEAD_DIM), BF16),
                pltpu.VMEM((D_MODEL, HEAD_DIM), BF16),
                pltpu.VMEM((BATCH, D_MODEL), BF16),
                pltpu.VMEM((BATCH, QW), F32),
                pltpu.VMEM((BATCH, HEAD_DIM), F32),
                pltpu.VMEM((BATCH, HEAD_DIM), F32),
                pltpu.VMEM((BATCH, 128), F32),
                pltpu.VMEM((BATCH, 128), F32),
                pltpu.VMEM((BATCH, 128), F32),
                pltpu.VMEM((BATCH, 128), F32),
                pltpu.SemaphoreType.DMA((4,)),
                pltpu.SemaphoreType.DMA((LOADS,)),
                pltpu.SemaphoreType.DMA((LOADS,)),
                pltpu.SemaphoreType.DMA((LOADS,)),
                pltpu.SemaphoreType.DMA((LOADS,)),
            ],
            cost_estimate=pl.CostEstimate(flops=4_000_000_000, bytes_accessed=72_000_000, transcendentals=200_000),
            compiler_params=pltpu.CompilerParams(vmem_limit_bytes=60 * 1024 * 1024),
        )(positions.reshape(1, BATCH), jnp.asarray(inv_freq_row()), slot_pos.T, norm_scale.reshape(1, D_MODEL),
          x_in, w_q, w_k, w_v, k_cache, v_cache)
        x_out = pl.pallas_call(
            comm_kernel,
            out_shape=jax.ShapeDtypeStruct((BATCH, D_MODEL), BF16),
            in_specs=[pl.BlockSpec(memory_space=pl.ANY), vmem, vmem, vmem],
            out_specs=vmem,
            scratch_shapes=[
                pltpu.VMEM((BATCH, PW), F32),
                pltpu.VMEM((NCHUNK * 32, PW), F32),
                pltpu.VMEM((NCHUNK * 16, PW), F32),
                pltpu.VMEM((NCHUNK * 8, PW), F32),
                pltpu.VMEM((BATCH, QW), F32),
                pltpu.SemaphoreType.DMA,
                pltpu.SemaphoreType.DMA((6, NCHUNK)),
                pltpu.SemaphoreType.DMA((6, NCHUNK)),
            ],
            cost_estimate=pl.CostEstimate(flops=1_200_000_000, bytes_accessed=6_000_000, transcendentals=0),
            compiler_params=pltpu.CompilerParams(collective_id=0, has_side_effects=True, vmem_limit_bytes=32 * 1024 * 1024),
        )(part, x_in, w_o, b_o.reshape(1, D_MODEL))
        return x_out, k_out, v_out, sp_t.T

    return jax.shard_map(
        local_step,
        mesh=mesh,
        in_specs=(row_spec, P('dp'), cache_spec, cache_spec, slot_spec, vec_spec, mat_spec, mat_spec, mat_spec, mat_spec, vec_spec),
        out_specs=(row_spec, cache_spec, cache_spec, slot_spec),
        check_vma=False)
```

time: 176 us -> 66.9 us (0.38)
  Pallas kernels: 0 us -> 61.4 us
  blocking collectives: 55.1 us -> 0 us
  other arithmetic: 39.1 us -> 0 us
  matrix products: 28.1 us -> 0 us
  waiting for transfers between devices: 24.5 us -> 0 us
  between operations: 14.2 us -> 0.68 us
  local copies, waits for them, and re-layouts: 14.7 us -> 4.66 us
    pallas_call x0 -> x2, Pallas kernels: none -> 61.4 us  [the longest x1 32.4 us: local_step(): pl.pallas_call(attn_kernel, out_shape=(jax.ShapeDtypeStruct((BATCH, PW),...]
    dot_general x6 -> x0, matrix products: 28.1 us -> none  [the longest x1 9.36 us: partial_attention(): jnp.einsum('bhd,bsd->bhs', q_rot, k_out, preferred_element_type=jnp.float32)]
    pmax x1 -> x0, blocking collectives: 27.8 us -> none  [local_step(): global_max = lax.pmax(local_max, 'kv')]
    psum x1 -> x0, blocking collectives: 27.4 us -> none  [local_step(): lax.psum((local_sum * factor, local_acc * factor[..., None]), 'kv')]
    psum x1 -> x0, waiting for transfers between devices: 24.5 us -> none  [local_step(): lax.psum((local_sum * factor, local_acc * factor[..., None]), 'kv')]
    select_n x1 -> x0, other arithmetic: 22.8 us -> none  [write_slots(): k_out = jnp.where(hit_mask[:, :, None], k_new[:, None, :], k_cache)]
    reduce_sum x2 -> x0, other arithmetic: 4.41 us -> none  [the longest x1 2.71 us: partial_attention(): local_sum = jnp.sum(weights, axis=-1)]
    another operation x1 -> x0, other arithmetic: 3.27 us -> none
  transfers between devices with their start and end apart: 1 -> 0, of which waited for: 1 -> 0; matrix products, arithmetic and copies ran while one was open for 0% -> 0% of each run, Pallas kernels for 0% -> 0%
where the time goes in v1:
time: 66.9 us; the launch traced here: 66.7 us
  Pallas kernels  61.4 us (92%)
  local copies, waits for them, and re-layouts  4.66 us (7%)
  between operations  0.68 us (1%)
    pallas_call x1, Pallas kernels, local_step(): pl.pallas_call(attn_kernel, out_shape=(jax.ShapeDtypeStruct((BATCH, PW),...  32.4 us
    pallas_call x1, Pallas kernels, local_step(): pl.pallas_call(comm_kernel, out_shape=jax.ShapeDtypeStruct((BATCH, D_MODE...  28.9 us
    unnamed x7, local copies, waits for them, and re-layouts  2.68 us

profile of v1, /device:TPU:0, one launch (start us, length us, event | category | flops | bytes accessed | tf_op | source)
XLA Modules:
  0.0 66.7 jit_solution(10881470137041277491)
XLA Ops:
  0.6 1.3 %reshape.18.ns_ref = bf16[1,1152]{1,0:T(2,128)(2,1)} reshape(bf16[1152]{0:T(1024)(128)(2,1)} %param.17) | data formatting | bytes 4608 | tf_op jit(solution)/shard_map/reshape | solution.py:424
  1.9 0.7 %reshape.19.b_ref = bf16[1,1152]{1,0:T(2,128)(2,1)S(1)} reshape(bf16[1152]{0:T(1024)(128)(2,1)} %param.22) | data formatting | bytes 4608 | tf_op jit(solution)/shard_map/reshape | solution.py:443
  2.6 0.0 copy-start
  2.6 0.0 copy-start.1
  2.6 32.4 %shard_map.147 = (f32[512,1152]{1,0:T(8,128)}, s32[64,512]{1,0:T(8,128)}, bf16[512,64,256]{2,1,0:T(8,128)(2,1)}, bf16[512,64,256]{2,1,0:T(8,128)(2,1)}) custom-call(s32[1,512]{1,0:T(1,128)} %bitcast.4, f32[1,128]{1,0:T(1,128)} %constant.2.clone.freq_ref, s32[64,512]{1,0:T(8,128)} %bitcast.3, bf16[1,1152]{1,0:T(2,128)(2,1)} %reshape.18.ns_ref, ...), custom_call_target="tpu_custom_call" | custom-call | flops 4000000000 | bytes 72000000 | tf_op jit(solution)/shard_map/pallas_call | solution.py:393
  35.0 0.0 copy-done
  35.1 0.0 copy-done.1
  35.1 0.0 copy-start.2
  35.1 1.7 %copy-done.2 = f32[512,1152]{1,0:T(8,128)S(1)} copy-done((f32[512,1152]{1,0:T(8,128)S(1)}, f32[512,1152]{1,0:T(8,128)}, u32[]{:S(2)}) %copy-start.2) | copy-done | bytes 2359320
  36.7 28.9 %shard_map.148 = bf16[512,1152]{1,0:T(8,128)(2,1)S(1)} custom-call(f32[512,1152]{1,0:T(8,128)S(1)} %copy-done.2, bf16[512,1152]{1,0:T(8,128)(2,1)S(1)} %copy-done, bf16[1024,1152]{1,0:T(8,128)(2,1)S(1)} %copy-done.1, bf16[1,1152]{1,0:T(2,128)(2,1)S(1)} %reshape.19.b_ref), custom_call_target="tpu_custom_call" | custom-call | flops 1200000000 | bytes 6000000 | tf_op jit(solution)/shard_map/pallas_call | solution.py:426
  65.7 1.0 %copy.17 = bf16[512,1152]{1,0:T(8,128)(2,1)} copy(bf16[512,1152]{1,0:T(8,128)(2,1)S(1)} %shard_map.148) | data formatting | bytes 2359296
Async XLA Ops:
  2.6 32.4 %copy-start = (bf16[512,1152]{1,0:T(8,128)(2,1)S(1)}, bf16[512,1152]{1,0:T(8,128)(2,1)}, u32[]{:S(2)}) copy-start(bf16[512,1152]{1,0:T(8,128)(2,1)} %x_ref.1) | copy-start | bytes 3538948
  2.6 32.4 %copy-start.1 = (bf16[1024,1152]{1,0:T(8,128)(2,1)S(1)}, bf16[1024,1152]{1,0:T(8,128)(2,1)}, u32[]{:S(2)}) copy-start(bf16[1024,1152]{1,0:T(8,128)(2,1)} %wo_ref.1) | copy-start | bytes 7077892
  35.1 1.7 %copy-start.2 = (f32[512,1152]{1,0:T(8,128)S(1)}, f32[512,1152]{1,0:T(8,128)}, u32[]{:S(2)}) copy-start(f32[512,1152]{1,0:T(8,128)} %get-tuple-element.8.part_in) | copy-start | bytes 7077892

commit v2 on v1

v2 whole, which is shorter than its diff:
```python
import functools

import jax
import jax.numpy as jnp
import numpy as np
from jax import lax
from jax.experimental import pallas as pl
from jax.experimental.pallas import tpu as pltpu
from jax.sharding import PartitionSpec as P

HEADS = 4
HEAD_DIM = 256
ROPE_DIM = 128
ROPE_HALF = ROPE_DIM // 2
ROPE_BASE = 10000.0
EPS = 1e-6
SCORE_SCALE = HEAD_DIM ** -0.5
NEG_LARGE = float(np.finfo(np.float32).min)
FAR = 1e9
F32 = jnp.float32
BF16 = jnp.bfloat16

BATCH = 512
D_MODEL = 1152
SLOTS = 64
QW = HEADS * HEAD_DIM
PW = QW + 128
GROUP = 8
STEP = 32
CHUNK = 64
AHEAD = 4
NCHUNK = BATCH // CHUNK
ROWS = 256


def sin_cos(theta):
    k = jnp.floor(theta * np.float32(2.0 / np.pi) + 0.5)
    r = theta - k * np.float32(1.5703125)
    r = r - k * np.float32(4.83751296997070312e-4)
    r = r - k * np.float32(7.54978995489188e-8)
    r2 = r * r
    s = r + r * r2 * (-1.6666654611e-1 + r2 * (8.3321608736e-3 + r2 * -1.9515295891e-4))
    c = 1.0 - 0.5 * r2 + r2 * r2 * (4.166664568298827e-2 + r2 * (-1.388731625493765e-3 + r2 * 2.443315711809948e-5))
    q = k - 4.0 * jnp.floor(k * 0.25)
    swap = (q == 1.0) | (q == 3.0)
    sin_v = jnp.where(swap, c, s)
    cos_v = jnp.where(swap, s, c)
    sin_v = jnp.where(q >= 2.0, -sin_v, sin_v)
    cos_v = jnp.where((q == 1.0) | (q == 2.0), -cos_v, cos_v)
    return sin_v, cos_v


def inv_freq_row():
    i = np.arange(ROPE_DIM) % ROPE_HALF
    return (ROPE_BASE ** (-i / ROPE_HALF)).astype(np.float32).reshape(1, ROPE_DIM)


def merge_rows(a_rows, b_rows):
    sa, sb = a_rows[1], b_rows[1]
    lane = lax.broadcasted_iota(jnp.int32, sa.shape, 1)
    ma, mb = sa, sb
    mm = jnp.maximum(ma, mb)
    fa, fb = jnp.exp(ma - mm), jnp.exp(mb - mm)
    fa_l = pltpu.roll(fa, HEADS, 1)
    fb_l = pltpu.roll(fb, HEADS, 1)
    stats = jnp.where(lane < HEADS, mm, sa * fa_l + sb * fb_l)
    vals = []
    for h in range(HEADS):
        va = a_rows[0][:, h * HEAD_DIM:(h + 1) * HEAD_DIM]
        vb = b_rows[0][:, h * HEAD_DIM:(h + 1) * HEAD_DIM]
        vals.append(va * fa[:, h:h + 1] + vb * fb[:, h:h + 1])
    return jnp.concatenate(vals, axis=1), stats


class Places:
    def __init__(self):
        me = lax.axis_index('kv')
        self.core = me % 2
        self.x = (me // 2) % 2
        self.y = me // 4
        self.mate = me + 1 - 2 * self.core
        self.x_peer = me + 2 - 4 * self.x
        self.y_peer = me + 4 - 8 * self.y

    def first(self, c):
        odd = c % 2
        return self.x_peer + odd * (self.y_peer - self.x_peer), self.x + odd * (self.y - self.x)

    def second(self, c):
        odd = c % 2
        return self.y_peer + odd * (self.x_peer - self.y_peer), self.y + odd * (self.x - self.y)


def send(src, dst, ss, rs, peer):
    return pltpu.make_async_remote_copy(src_ref=src, dst_ref=dst, send_sem=ss, recv_sem=rs,
                                        device_id={'kv': peer}, device_id_type=pl.DeviceIdType.MESH)


def al(v, m=8):
    return pl.multiple_of(v, m)


class Reduce:
    def __init__(self, places, part, r0, r1, r2, own, sems):
        self.p = places
        self.part, self.r0, self.r1, self.r2, self.own = part, r0, r1, r2, own
        self.s0s, self.s0r, self.s1s, self.s1r, self.s2s, self.s2r = sems

    def copy0(self, c):
        src = al(c * CHUNK + 32 * (1 - self.p.core))
        return send(self.part.at[pl.ds(src, 32)], self.r0.at[pl.ds(al(c * 32), 32)], self.s0s.at[c], self.s0r.at[c], self.p.mate)

    def copy1(self, c):
        peer, k = self.p.first(c)
        src = al(c * CHUNK + 32 * self.p.core + 16 * (1 - k))
        return send(self.part.at[pl.ds(src, 16)], self.r1.at[pl.ds(al(c * 16), 16)], self.s1s.at[c], self.s1r.at[c], peer)

    def copy2(self, c):
        peer, k2 = self.p.second(c)
        k1 = self.p.first(c)[1]
        src = al(c * CHUNK + 32 * self.p.core + 16 * k1 + 8 * (1 - k2))
        return send(self.part.at[pl.ds(src, 8)], self.r2.at[pl.ds(al(c * 8), 8)], self.s2s.at[c], self.s2r.at[c], peer)

    def merge(self, mine, other_ref, theirs):
        a = self.part[pl.ds(mine, 8), :]
        b = other_ref[pl.ds(theirs, 8), :]
        return merge_rows((a[:, :QW], a[:, QW:]), (b[:, :QW], b[:, QW:]))

    def step0(self, c):
        self.copy0(c).wait_recv()
        base = c * CHUNK + 32 * self.p.core
        for t in range(4):
            v, s = self.merge(al(base + 8 * t), self.r0, al(c * 32 + 8 * t))
            self.part[pl.ds(al(base + 8 * t), 8), :] = jnp.concatenate([v, s], axis=1)

    def step1(self, c):
        self.copy1(c).wait_recv()
        base = c * CHUNK + 32 * self.p.core + 16 * self.p.first(c)[1]
        for t in range(2):
            v, s = self.merge(al(base + 8 * t), self.r1, al(c * 16 + 8 * t))
            self.part[pl.ds(al(base + 8 * t), 8), :] = jnp.concatenate([v, s], axis=1)

    def step2(self, c):
        self.copy2(c).wait_recv()
        base = c * CHUNK + 32 * self.p.core + 16 * self.p.first(c)[1] + 8 * self.p.second(c)[1]
        v, s = self.merge(al(base), self.r2, al(c * 8))
        outs = [v[:, h * HEAD_DIM:(h + 1) * HEAD_DIM] / s[:, HEADS + h:HEADS + h + 1] for h in range(HEADS)]
        self.own[pl.ds(al(base), 8), :] = jnp.concatenate(outs, axis=1)

    def drain(self, c):
        self.copy0(c).wait_send()
        self.copy1(c).wait_send()
        self.copy2(c).wait_send()


class Gather:
    def __init__(self, places, g, sems):
        self.p, self.g = places, g
        self.s0s, self.s0r, self.s1s, self.s1r, self.s2s, self.s2r = sems

    def copy0(self, c):
        peer, k2 = self.p.second(c)
        k1 = self.p.first(c)[1]
        rows = pl.ds(al(c * CHUNK + 32 * self.p.core + 16 * k1 + 8 * k2), 8)
        return send(self.g.at[rows], self.g.at[rows], self.s0s.at[c], self.s0r.at[c], peer)

    def copy1(self, c):
        peer, k1 = self.p.first(c)
        rows = pl.ds(al(c * CHUNK + 32 * self.p.core + 16 * k1), 16)
        return send(self.g.at[rows], self.g.at[rows], self.s1s.at[c], self.s1r.at[c], peer)

    def copy2(self, c):
        rows = pl.ds(al(c * CHUNK + 32 * self.p.core), 32)
        return send(self.g.at[rows], self.g.at[rows], self.s2s.at[c], self.s2r.at[c], self.p.mate)

    def drain(self, c):
        self.copy0(c).wait_send()
        self.copy1(c).wait_send()
        self.copy2(c).wait_send()


def step_kernel(pos_row, freq_ref, ns_ref, b_ref, x_hbm, wq_hbm, wk_hbm, wv_hbm, wo_hbm, k_hbm, v_hbm,
                kbuf, vbuf, out_ref,
                x_v, wq_v, wk_v, wv_v, wo_v, n_v, q_v, kn_v, vn_v, p_col, js_col, cos_v, sin_v,
                part, r0, r1, r2, g, w_sem, k_sem, v_sem, rsems, gsems):
    p = Places()
    barrier = pltpu.get_barrier_semaphore()
    for peer in (p.mate, p.x_peer, p.y_peer):
        pl.semaphore_signal(barrier, inc=1, device_id={'kv': peer}, device_id_type=pl.DeviceIdType.MESH)
    off = lax.axis_index('kv') * SLOTS
    weights = ((x_hbm, x_v), (wk_hbm, wk_v), (wv_hbm, wv_v), (wq_hbm, wq_v), (wo_hbm, wo_v))

    def w_in(n):
        return pltpu.make_async_copy(weights[n][0], weights[n][1], w_sem.at[n])

    def rows_of(c):
        return pl.ds(pl.multiple_of(c * CHUNK, CHUNK), CHUNK)

    def k_in(c):
        return pltpu.make_async_copy(k_hbm.at[rows_of(c)], kbuf.at[rows_of(c)], k_sem.at[c])

    def v_in(c):
        return pltpu.make_async_copy(v_hbm.at[rows_of(c)], vbuf.at[rows_of(c)], v_sem.at[c])

    for n in range(4):
        w_in(n).start()
    for c in range(AHEAD):
        k_in(c).start()
        v_in(c).start()

    offf = off.astype(F32)

    @pl.loop(0, BATCH // 128)
    def _(t):
        rows = pl.ds(pl.multiple_of(t * 128, 128), 128)
        col = jnp.broadcast_to(pos_row[:, rows].astype(F32), (128, 128)).T
        p_col[rows, :] = col
        js = col - 512.0 * jnp.floor(col * (1.0 / 512.0)) - offf
        js_col[rows, :] = jnp.where((js >= 0.0) & (js < float(SLOTS)), js, -1.0)

    @pl.loop(0, BATCH // 64)
    def _(t):
        rows = pl.ds(pl.multiple_of(t * 64, 64), 64)
        s, c = sin_cos(p_col[rows, :] * freq_ref[...])
        lane = lax.broadcasted_iota(jnp.int32, (64, 128), 1)
        sin_v[rows, :] = jnp.where(lane < ROPE_HALF, -s, s)
        cos_v[rows, :] = c

    def rotate(t, rows):
        r = t[:, :ROPE_DIM]
        r = r * cos_v[rows, :] + pltpu.roll(r, ROPE_HALF, 1) * sin_v[rows, :]
        return jnp.concatenate([r, t[:, ROPE_DIM:]], axis=1)

    w_in(0).wait()
    gain = 1.0 + ns_ref[...].astype(F32).reshape(1, D_MODEL)

    @pl.loop(0, BATCH // 64)
    def _(i):
        rows = pl.ds(pl.multiple_of(i * 64, 64), 64)
        xf = x_v[rows, :].astype(F32)
        mean_sq = jnp.sum(xf * xf, axis=1, keepdims=True) * (1.0 / D_MODEL)
        n_v[rows, :] = (xf * lax.rsqrt(mean_sq + EPS) * gain).astype(BF16)

    w_in(1).wait()
    w_in(2).wait()
    w_in(3).wait()

    def project(i):
        rows = pl.ds(pl.multiple_of(i * ROWS, ROWS), ROWS)
        kn_v[rows, :] = rotate(jnp.dot(n_v[rows, :], wk_v[...], preferred_element_type=F32), rows)
        vn_v[rows, :] = jnp.dot(n_v[rows, :], wv_v[...], preferred_element_type=F32)

        @pl.loop(0, HEADS)
        def _(h):
            cols = pl.ds(pl.multiple_of(h * HEAD_DIM, HEAD_DIM), HEAD_DIM)
            qh = jnp.dot(n_v[rows, :], wq_v[:, cols], preferred_element_type=F32)
            q_v[rows, cols] = rotate(qh, rows) * SCORE_SCALE

    sub = lax.broadcasted_iota(jnp.int32, (GROUP, 128), 0)
    lane = lax.broadcasted_iota(jnp.int32, (GROUP, 128), 1)
    slot_c = jnp.where((lane // SLOTS) == (sub % 2), (lane % SLOTS).astype(F32) + offf, FAR)
    pick = [(sub // 2) == cc for cc in range(4)]
    iotas = [(lax.broadcasted_iota(jnp.int32, (16, HEAD_DIM), 0) + 16 * t).astype(F32).astype(BF16) for t in range(SLOTS // 16)]
    def refresh(buf, new_ref, b, hits):
        fresh = jnp.broadcast_to(new_ref[pl.ds(b, 1), :], (16, HEAD_DIM)).astype(BF16)
        out = []
        for t in range(SLOTS // 16):
            piece = jnp.where(hits[t], fresh, buf[b, pl.ds(16 * t, 16), :])
            buf[b, pl.ds(16 * t, 16), :] = piece
            out.append(piece)
        return out

    def group(r0):
        ks, vs = [], []
        for i in range(GROUP):
            b = r0 + i
            js = jnp.broadcast_to(js_col[pl.ds(b, 1), :], (16, 128)).astype(BF16)
            js = jnp.concatenate([js, js], axis=1)
            hits = [io == js for io in iotas]
            ks += refresh(kbuf, kn_v, b, hits)
            vs += refresh(vbuf, vn_v, b, hits)
        rows = pl.ds(r0, GROUP)
        q = jnp.concatenate([q_v[rows, h * HEAD_DIM:(h + 1) * HEAD_DIM] for h in range(HEADS)], axis=0).astype(BF16)
        kmat = jnp.concatenate(ks, axis=0)
        vmat = jnp.concatenate(vs, axis=0)
        s = lax.dot_general(q, kmat, (((1,), (1,)), ((), ())), preferred_element_type=F32)
        valid = slot_c <= p_col[rows, :]
        stats = jnp.zeros((GROUP, 128), F32)
        ps = []
        for h in range(HEADS):
            sh = s[h * GROUP:(h + 1) * GROUP, :]
            c = sh[:, 384:512]
            for cc in range(3):
                c = jnp.where(pick[cc], sh[:, cc * 128:(cc + 1) * 128], c)
            c = jnp.where(valid, c, NEG_LARGE)
            m = jnp.max(c, axis=1, keepdims=True)
            e = jnp.where(valid, jnp.exp(c - m), 0.0)
            l = jnp.sum(e, axis=1, keepdims=True)
            stats = jnp.where(lane == h, m, stats)
            stats = jnp.where(lane == HEADS + h, l, stats)
            ps.append(jnp.concatenate([jnp.where(pick[cc], e, 0.0) for cc in range(4)], axis=1))
        pm = jnp.concatenate(ps, axis=0).astype(BF16)
        o = jnp.dot(pm, vmat, preferred_element_type=F32)
        for h in range(HEADS):
            part[rows, h * HEAD_DIM:(h + 1) * HEAD_DIM] = o[h * GROUP:(h + 1) * GROUP, :]
        part[rows, QW:PW] = stats

    red = Reduce(p, part, r0, r1, r2, g, [rsems.at[i] for i in range(6)])
    gat = Gather(p, g, [gsems.at[i] for i in range(6)])

    def when_chunk(c, body):
        @pl.when((c >= 0) & (c < NCHUNK))
        def _():
            body(c)

    def attend(i):
        @pl.when(i + AHEAD < NCHUNK)
        def _():
            k_in(i + AHEAD).start()
            v_in(i + AHEAD).start()

        @pl.when(i == AHEAD)
        def _():
            w_in(4).start()

        @pl.when(i % (ROWS // CHUNK) == 0)
        def _():
            project(i // (ROWS // CHUNK))

        k_in(i).wait()
        v_in(i).wait()

        @pl.loop(0, CHUNK // STEP)
        def _(t):
            for gg in range(STEP // GROUP):
                group(pl.multiple_of(i * CHUNK + t * STEP + gg * GROUP, GROUP))

        @pl.when(i == 0)
        def _():
            pl.semaphore_wait(barrier, 3)

        red.copy0(i).start()

    def pair_step(c):
        red.step0(c)
        red.copy1(c).start()

    def first_step(c):
        red.step1(c)
        red.copy2(c).start()

    def second_step(c):
        red.step2(c)
        gat.copy0(c).start()

    def back_first(c):
        gat.copy0(c).wait_recv()
        gat.copy1(c).start()

    def back_second(c):
        gat.copy1(c).wait_recv()
        gat.copy2(c).start()

    bias = b_ref[...].astype(F32).reshape(1, D_MODEL)

    def project_out(c):
        gat.copy2(c).wait_recv()

        @pl.when(c == 1)
        def _():
            w_in(4).wait()

        @pl.when(c % 2 == 1)
        def _():
            rows = pl.ds(al((c - 1) * CHUNK, CHUNK), 2 * CHUNK)
            o = g[rows, :].astype(BF16)
            y = x_v[rows, :].astype(F32) + jnp.dot(o, wo_v[...], preferred_element_type=F32) + bias
            out_ref[rows, :] = y.astype(BF16)

    lags = ((0, attend), (1, pair_step), (4, first_step), (6, second_step), (8, back_first), (10, back_second), (11, project_out))

    @pl.loop(0, NCHUNK + lags[-1][0])
    def _(i):
        for lag, body in lags:
            when_chunk(i - lag, body)

    @pl.loop(0, NCHUNK)
    def _(c):
        red.drain(c)
        gat.drain(c)


def slot_kernel(pos_row, sp_ref, sp_out):
    off = lax.axis_index('kv') * SLOTS
    p_all = pos_row[...]
    slot_ids = off + lax.broadcasted_iota(jnp.int32, (SLOTS, BATCH), 0)
    sp_out[...] = jnp.where(slot_ids == (p_all & 511), p_all, sp_ref[...])


def solution(mesh):
    row_spec = P('dp', None)
    cache_spec = P('dp', 'kv', None)
    slot_spec = P('dp', 'kv')
    vec_spec = P(None)
    mat_spec = P(None, None)
    hbm = pl.BlockSpec(memory_space=pltpu.HBM)
    vmem = pl.BlockSpec(memory_space=pltpu.VMEM)

    def local_step(x_in, positions, k_cache, v_cache, slot_pos, norm_scale, w_q, w_k, w_v, w_o, b_o):
        pos_row = positions.reshape(1, BATCH)
        kbuf, vbuf, x_new = pl.pallas_call(
            step_kernel,
            out_shape=(pltpu.VMEM((BATCH, SLOTS, HEAD_DIM), BF16),
                       pltpu.VMEM((BATCH, SLOTS, HEAD_DIM), BF16),
                       pltpu.VMEM((BATCH, D_MODEL), BF16)),
            in_specs=[vmem, vmem, vmem, vmem, hbm, hbm, hbm, hbm, hbm, hbm, hbm],
            out_specs=(vmem, vmem, vmem),
            scratch_shapes=[
                pltpu.VMEM((BATCH, D_MODEL), BF16),
                pltpu.VMEM((D_MODEL, QW), BF16),
                pltpu.VMEM((D_MODEL, HEAD_DIM), BF16),
                pltpu.VMEM((D_MODEL, HEAD_DIM), BF16),
                pltpu.VMEM((QW, D_MODEL), BF16),
                pltpu.VMEM((BATCH, D_MODEL), BF16),
                pltpu.VMEM((BATCH, QW), F32),
                pltpu.VMEM((BATCH, HEAD_DIM), F32),
                pltpu.VMEM((BATCH, HEAD_DIM), F32),
                pltpu.VMEM((BATCH, 128), F32),
                pltpu.VMEM((BATCH, 128), F32),
                pltpu.VMEM((BATCH, 128), F32),
                pltpu.VMEM((BATCH, 128), F32),
                pltpu.VMEM((BATCH, PW), F32),
                pltpu.VMEM((NCHUNK * 32, PW), F32),
                pltpu.VMEM((NCHUNK * 16, PW), F32),
                pltpu.VMEM((NCHUNK * 8, PW), F32),
                pltpu.VMEM((BATCH, QW), F32),
                pltpu.SemaphoreType.DMA((5,)),
                pltpu.SemaphoreType.DMA((NCHUNK,)),
                pltpu.SemaphoreType.DMA((NCHUNK,)),
                pltpu.SemaphoreType.DMA((6, NCHUNK)),
                pltpu.SemaphoreType.DMA((6, NCHUNK)),
            ],
            cost_estimate=pl.CostEstimate(flops=5_000_000_000, bytes_accessed=40_000_000, transcendentals=200_000),
            compiler_params=pltpu.CompilerParams(collective_id=0, has_side_effects=True, vmem_limit_bytes=22 * 1024 * 1024),
        )(pos_row, jnp.asarray(inv_freq_row()), norm_scale, b_o, x_in, w_q, w_k, w_v, w_o, k_cache, v_cache)
        sp_t = pl.pallas_call(
            slot_kernel,
            out_shape=jax.ShapeDtypeStruct((SLOTS, BATCH), jnp.int32),
            in_specs=[vmem, vmem],
            out_specs=vmem,
        )(pos_row, slot_pos.T)
        return x_new, kbuf, vbuf, sp_t.T


    return jax.shard_map(
        local_step,
        mesh=mesh,
        in_specs=(row_spec, P('dp'), cache_spec, cache_spec, slot_spec, vec_spec, mat_spec, mat_spec, mat_spec, mat_spec, vec_spec),
        out_specs=(row_spec, cache_spec, cache_spec, slot_spec),
        check_vma=False)
```

time: 66.9 us -> 74.4 us (1.11)
  local copies, waits for them, and re-layouts: 4.66 us -> 13.3 us
  Pallas kernels: 61.4 us -> 60.3 us
    unnamed x7 -> x3, local copies, waits for them, and re-layouts: 2.68 us -> 13.3 us
    reshape x2 -> x0, local copies, waits for them, and re-layouts: 1.97 us -> none  [the longest x1 1.28 us: local_step(): norm_scale.reshape(1, D_MODEL)]
    pallas_call x2, Pallas kernels: 61.4 us -> 60.3 us  [the longest x1 58.7 us: local_step(): pl.pallas_call(step_kernel, out_shape=(pltpu.VMEM((BATCH, SLOTS, HEAD_DIM...]
where the time goes in v2:
time: 74.4 us; the launch traced here: 74.2 us
  Pallas kernels  60.3 us (81%)
  local copies, waits for them, and re-layouts  13.3 us (18%)
    pallas_call x1, Pallas kernels, local_step(): pl.pallas_call(step_kernel, out_shape=(pltpu.VMEM((BATCH, SLOTS, HEAD_DIM...  58.7 us
    unnamed x3, local copies, waits for them, and re-layouts  13.3 us
    pallas_call x1, Pallas kernels, local_step(): pl.pallas_call(slot_kernel, out_shape=jax.ShapeDtypeStruct((SLOTS, BATCH)...  1.59 us

profile of v2, /device:TPU:0, one launch (start us, length us, event | category | flops | bytes accessed | tf_op | source)
XLA Modules:
  0.0 74.2 jit_solution(2571076028292494831)
XLA Ops:
  0.6 58.7 %shard_map.147 = (bf16[512,64,256]{2,1,0:T(8,128)(2,1)S(1)}, bf16[512,64,256]{2,1,0:T(8,128)(2,1)S(1)}, bf16[512,1152]{1,0:T(8,128)(2,1)S(1)}) custom-call(s32[1,512]{1,0:T(1,128)} %bitcast.5, f32[1,128]{1,0:T(1,128)} %constant.2.clone.freq_ref, bf16[1152]{0:T(1024)(128)(2,1)} %ns_ref.1, bf16[1152]{0:T(1024)(128)(2,1)} %b_ref.1, bf16[512,1152]{1,0:T(8,128)(2,1)} %x_hbm.1, ...), custom_call_target="tpu_custom_call" | custom-call | flops 5000000000 | bytes 40000000 | tf_op jit(solution)/shard_map/pallas_call | solution.py:411
  59.3 6.2 %copy.20 = bf16[512,64,256]{2,1,0:T(8,128)(2,1)} copy(bf16[512,64,256]{2,1,0:T(8,128)(2,1)S(1)} %get-tuple-element.11) | data formatting | bytes 33554432
  65.5 6.2 %copy.21 = bf16[512,64,256]{2,1,0:T(8,128)(2,1)} copy(bf16[512,64,256]{2,1,0:T(8,128)(2,1)S(1)} %get-tuple-element.12) | data formatting | bytes 33554432
  71.6 1.0 %copy.19 = bf16[512,1152]{1,0:T(8,128)(2,1)} copy(bf16[512,1152]{1,0:T(8,128)(2,1)S(1)} %get-tuple-element.10) | data formatting | bytes 2359296
  72.7 1.6 %shard_map.148 = s32[64,512]{1,0:T(8,128)} custom-call(s32[1,512]{1,0:T(1,128)} %bitcast.6, s32[64,512]{1,0:T(8,128)} %bitcast.3), custom_call_target="tpu_custom_call" | custom-call | tf_op jit(solution)/shard_map/pallas_call | solution.py:446

commit v3 on v2

--- a/solution.py
+++ b/solution.py
@@ -26,7 +26,7 @@
 QW = HEADS * HEAD_DIM
 PW = QW + 128
 GROUP = 8
-STEP = 32
+STEP = 64
 CHUNK = 64
 AHEAD = 4
 NCHUNK = BATCH // CHUNK
@@ -121,31 +121,29 @@
         src = al(c * CHUNK + 32 * self.p.core + 16 * k1 + 8 * (1 - k2))
         return send(self.part.at[pl.ds(src, 8)], self.r2.at[pl.ds(al(c * 8), 8)], self.s2s.at[c], self.s2r.at[c], peer)
 
-    def merge(self, mine, other_ref, theirs):
-        a = self.part[pl.ds(mine, 8), :]
-        b = other_ref[pl.ds(theirs, 8), :]
+    def merge(self, mine, other_ref, theirs, n):
+        a = self.part[pl.ds(mine, n), :]
+        b = other_ref[pl.ds(theirs, n), :]
         return merge_rows((a[:, :QW], a[:, QW:]), (b[:, :QW], b[:, QW:]))
 
     def step0(self, c):
         self.copy0(c).wait_recv()
-        base = c * CHUNK + 32 * self.p.core
-        for t in range(4):
-            v, s = self.merge(al(base + 8 * t), self.r0, al(c * 32 + 8 * t))
-            self.part[pl.ds(al(base + 8 * t), 8), :] = jnp.concatenate([v, s], axis=1)
+        base = al(c * CHUNK + 32 * self.p.core)
+        v, s = self.merge(base, self.r0, al(c * 32), 32)
+        self.part[pl.ds(base, 32), :] = jnp.concatenate([v, s], axis=1)
 
     def step1(self, c):
         self.copy1(c).wait_recv()
-        base = c * CHUNK + 32 * self.p.core + 16 * self.p.first(c)[1]
-        for t in range(2):
-            v, s = self.merge(al(base + 8 * t), self.r1, al(c * 16 + 8 * t))
-            self.part[pl.ds(al(base + 8 * t), 8), :] = jnp.concatenate([v, s], axis=1)
+        base = al(c * CHUNK + 32 * self.p.core + 16 * self.p.first(c)[1])
+        v, s = self.merge(base, self.r1, al(c * 16), 16)
+        self.part[pl.ds(base, 16), :] = jnp.concatenate([v, s], axis=1)
 
     def step2(self, c):
         self.copy2(c).wait_recv()
-        base = c * CHUNK + 32 * self.p.core + 16 * self.p.first(c)[1] + 8 * self.p.second(c)[1]
-        v, s = self.merge(al(base), self.r2, al(c * 8))
+        base = al(c * CHUNK + 32 * self.p.core + 16 * self.p.first(c)[1] + 8 * self.p.second(c)[1])
+        v, s = self.merge(base, self.r2, al(c * 8), 8)
         outs = [v[:, h * HEAD_DIM:(h + 1) * HEAD_DIM] / s[:, HEADS + h:HEADS + h + 1] for h in range(HEADS)]
-        self.own[pl.ds(al(base), 8), :] = jnp.concatenate(outs, axis=1)
+        self.own[pl.ds(base, 8), :] = jnp.concatenate(outs, axis=1)
 
     def drain(self, c):
         self.copy0(c).wait_send()
@@ -250,9 +248,8 @@
         kn_v[rows, :] = rotate(jnp.dot(n_v[rows, :], wk_v[...], preferred_element_type=F32), rows)
         vn_v[rows, :] = jnp.dot(n_v[rows, :], wv_v[...], preferred_element_type=F32)
 
-        @pl.loop(0, HEADS)
-        def _(h):
-            cols = pl.ds(pl.multiple_of(h * HEAD_DIM, HEAD_DIM), HEAD_DIM)
+        for h in range(HEADS):
+            cols = pl.ds(h * HEAD_DIM, HEAD_DIM)
             qh = jnp.dot(n_v[rows, :], wq_v[:, cols], preferred_element_type=F32)
             q_v[rows, cols] = rotate(qh, rows) * SCORE_SCALE
 
@@ -261,49 +258,65 @@
     slot_c = jnp.where((lane // SLOTS) == (sub % 2), (lane % SLOTS).astype(F32) + offf, FAR)
     pick = [(sub // 2) == cc for cc in range(4)]
     iotas = [(lax.broadcasted_iota(jnp.int32, (16, HEAD_DIM), 0) + 16 * t).astype(F32).astype(BF16) for t in range(SLOTS // 16)]
-    def refresh(buf, new_ref, b, hits):
-        fresh = jnp.broadcast_to(new_ref[pl.ds(b, 1), :], (16, HEAD_DIM)).astype(BF16)
+    def hits_of(b):
+        js = jnp.broadcast_to(js_col[pl.ds(b, 1), :], (16, 128)).astype(BF16)
+        js = jnp.concatenate([js, js], axis=1)
+        return [io == js for io in iotas]
+
+    def refresh(buf, new_ref, r0):
         out = []
-        for t in range(SLOTS // 16):
-            piece = jnp.where(hits[t], fresh, buf[b, pl.ds(16 * t, 16), :])
-            buf[b, pl.ds(16 * t, 16), :] = piece
-            out.append(piece)
-        return out
-
-    def group(r0):
-        ks, vs = [], []
         for i in range(GROUP):
             b = r0 + i
-            js = jnp.broadcast_to(js_col[pl.ds(b, 1), :], (16, 128)).astype(BF16)
-            js = jnp.concatenate([js, js], axis=1)
-            hits = [io == js for io in iotas]
-            ks += refresh(kbuf, kn_v, b, hits)
-            vs += refresh(vbuf, vn_v, b, hits)
+            hits = hits_of(b)
+            fresh = jnp.broadcast_to(new_ref[pl.ds(b, 1), :], (16, HEAD_DIM)).astype(BF16)
+            for t in range(SLOTS // 16):
+                piece = jnp.where(hits[t], fresh, buf[b, pl.ds(16 * t, 16), :])
+                buf[b, pl.ds(16 * t, 16), :] = piece
+                out.append(piece)
+        return jnp.concatenate(out, axis=0)
+
+    def scores(r0):
         rows = pl.ds(r0, GROUP)
         q = jnp.concatenate([q_v[rows, h * HEAD_DIM:(h + 1) * HEAD_DIM] for h in range(HEADS)], axis=0).astype(BF16)
-        kmat = jnp.concatenate(ks, axis=0)
-        vmat = jnp.concatenate(vs, axis=0)
-        s = lax.dot_general(q, kmat, (((1,), (1,)), ((), ())), preferred_element_type=F32)
-        valid = slot_c <= p_col[rows, :]
-        stats = jnp.zeros((GROUP, 128), F32)
-        ps = []
+        s = lax.dot_general(q, refresh(kbuf, kn_v, r0), (((1,), (1,)), ((), ())), preferred_element_type=F32)
+        out = []
         for h in range(HEADS):
             sh = s[h * GROUP:(h + 1) * GROUP, :]
             c = sh[:, 384:512]
             for cc in range(3):
                 c = jnp.where(pick[cc], sh[:, cc * 128:(cc + 1) * 128], c)
-            c = jnp.where(valid, c, NEG_LARGE)
+            out.append(c)
+        return out
+
+    def soften(r0, cs):
+        rows = pl.ds(r0, GROUP)
+        valid = slot_c <= p_col[rows, :]
+        stats = jnp.zeros((GROUP, 128), F32)
+        ps = []
+        for h in range(HEADS):
+            c = jnp.where(valid, cs[h], NEG_LARGE)
             m = jnp.max(c, axis=1, keepdims=True)
             e = jnp.where(valid, jnp.exp(c - m), 0.0)
             l = jnp.sum(e, axis=1, keepdims=True)
             stats = jnp.where(lane == h, m, stats)
             stats = jnp.where(lane == HEADS + h, l, stats)
-            ps.append(jnp.concatenate([jnp.where(pick[cc], e, 0.0) for cc in range(4)], axis=1))
-        pm = jnp.concatenate(ps, axis=0).astype(BF16)
-        o = jnp.dot(pm, vmat, preferred_element_type=F32)
+            ps.append(e)
+        part[rows, QW:PW] = stats
+        return ps
+
+    def values(r0, ps):
+        rows = pl.ds(r0, GROUP)
+        pm = jnp.concatenate([jnp.concatenate([jnp.where(pick[cc], e, 0.0) for cc in range(4)], axis=1) for e in ps], axis=0).astype(BF16)
+        o = jnp.dot(pm, refresh(vbuf, vn_v, r0), preferred_element_type=F32)
         for h in range(HEADS):
             part[rows, h * HEAD_DIM:(h + 1) * HEAD_DIM] = o[h * GROUP:(h + 1) * GROUP, :]
-        part[rows, QW:PW] = stats
+
+    def attend_rows(base):
+        starts = [al(base + g * GROUP, GROUP) for g in range(STEP // GROUP)]
+        cs = [scores(r0) for r0 in starts]
+        ps = [soften(r0, c) for r0, c in zip(starts, cs)]
+        for r0, e in zip(starts, ps):
+            values(r0, e)
 
     red = Reduce(p, part, r0, r1, r2, g, [rsems.at[i] for i in range(6)])
     gat = Gather(p, g, [gsems.at[i] for i in range(6)])
@@ -330,10 +343,8 @@
         k_in(i).wait()
         v_in(i).wait()
 
-        @pl.loop(0, CHUNK // STEP)
-        def _(t):
-            for gg in range(STEP // GROUP):
-                group(pl.multiple_of(i * CHUNK + t * STEP + gg * GROUP, GROUP))
+        for t in range(CHUNK // STEP):
+            attend_rows(i * CHUNK + t * STEP)
 
         @pl.when(i == 0)
         def _():

time: 74.4 us -> 59.8 us (0.80)
  Pallas kernels: 60.3 us -> 45.6 us
    pallas_call x1, Pallas kernels: 58.7 us -> 44 us  [local_step(): pl.pallas_call(step_kernel, out_shape=(pltpu.VMEM((BATCH, SLOTS, HEAD_DIM...]
where the time goes in v3:
time: 59.8 us; the launch traced here: 59.6 us
  Pallas kernels  45.6 us (76%)
  local copies, waits for them, and re-layouts  13.3 us (22%)
  between operations  0.64 us (1%)
    pallas_call x1, Pallas kernels, local_step(): pl.pallas_call(step_kernel, out_shape=(pltpu.VMEM((BATCH, SLOTS, HEAD_DIM...  44 us
    unnamed x3, local copies, waits for them, and re-layouts  13.3 us
    pallas_call x1, Pallas kernels, local_step(): pl.pallas_call(slot_kernel, out_shape=jax.ShapeDtypeStruct((SLOTS, BATCH)...  1.59 us

profile of v3, /device:TPU:0, one launch (start us, length us, event | category | flops | bytes accessed | tf_op | source)
XLA Modules:
  0.0 59.6 jit_solution(16701498924410451246)
XLA Ops:
  0.6 44.0 %shard_map.147 = (bf16[512,64,256]{2,1,0:T(8,128)(2,1)S(1)}, bf16[512,64,256]{2,1,0:T(8,128)(2,1)S(1)}, bf16[512,1152]{1,0:T(8,128)(2,1)S(1)}) custom-call(s32[1,512]{1,0:T(1,128)} %bitcast.5, f32[1,128]{1,0:T(1,128)} %constant.2.clone.freq_ref, bf16[1152]{0:T(1024)(128)(2,1)} %ns_ref.1, bf16[1152]{0:T(1024)(128)(2,1)} %b_ref.1, bf16[512,1152]{1,0:T(8,128)(2,1)} %x_hbm.1, ...), custom_call_target="tpu_custom_call" | custom-call | flops 5000000000 | bytes 40000000 | tf_op jit(solution)/shard_map/pallas_call | solution.py:422
  44.6 6.2 %copy.20 = bf16[512,64,256]{2,1,0:T(8,128)(2,1)} copy(bf16[512,64,256]{2,1,0:T(8,128)(2,1)S(1)} %get-tuple-element.11) | data formatting | bytes 33554432
  50.8 6.2 %copy.21 = bf16[512,64,256]{2,1,0:T(8,128)(2,1)} copy(bf16[512,64,256]{2,1,0:T(8,128)(2,1)S(1)} %get-tuple-element.12) | data formatting | bytes 33554432
  57.0 1.0 %copy.19 = bf16[512,1152]{1,0:T(8,128)(2,1)} copy(bf16[512,1152]{1,0:T(8,128)(2,1)S(1)} %get-tuple-element.10) | data formatting | bytes 2359296
  58.0 1.6 %shard_map.148 = s32[64,512]{1,0:T(8,128)} custom-call(s32[1,512]{1,0:T(1,128)} %bitcast.6, s32[64,512]{1,0:T(8,128)} %bitcast.3), custom_call_target="tpu_custom_call" | custom-call | tf_op jit(solution)/shard_map/pallas_call | solution.py:457

commit v4 on v3

--- a/solution.py
+++ b/solution.py
@@ -30,6 +30,8 @@
 CHUNK = 64
 AHEAD = 4
 NCHUNK = BATCH // CHUNK
+N_RS = 6
+N_RD = NCHUNK - N_RS
 ROWS = 256
 
 
@@ -72,6 +74,11 @@
     return jnp.concatenate(vals, axis=1), stats
 
 
+def normalise(v, s):
+    inv = 1.0 / s
+    return jnp.concatenate([v[:, h * HEAD_DIM:(h + 1) * HEAD_DIM] * inv[:, HEADS + h:HEADS + h + 1] for h in range(HEADS)], axis=1)
+
+
 class Places:
     def __init__(self):
         me = lax.axis_index('kv')
@@ -142,13 +149,47 @@
         self.copy2(c).wait_recv()
         base = al(c * CHUNK + 32 * self.p.core + 16 * self.p.first(c)[1] + 8 * self.p.second(c)[1])
         v, s = self.merge(base, self.r2, al(c * 8), 8)
-        outs = [v[:, h * HEAD_DIM:(h + 1) * HEAD_DIM] / s[:, HEADS + h:HEADS + h + 1] for h in range(HEADS)]
-        self.own[pl.ds(base, 8), :] = jnp.concatenate(outs, axis=1)
+        self.own[pl.ds(base, 8), :] = normalise(v, s)
 
     def drain(self, c):
-        self.copy0(c).wait_send()
         self.copy1(c).wait_send()
         self.copy2(c).wait_send()
+
+
+class Double:
+    def __init__(self, places, red, mid, d1, d2, sems):
+        self.p, self.red, self.mid, self.d1, self.d2 = places, red, mid, d1, d2
+        self.s1s, self.s1r, self.s2s, self.s2r = sems
+
+    def copies1(self, c):
+        d = c - N_RS
+        base = c * CHUNK + 32 * self.p.core
+        return [send(self.red.part.at[pl.ds(al(base + 16 * t), 16)], self.d1.at[pl.ds(al(d * 32 + 16 * t), 16)],
+                     self.s1s.at[2 * d + t], self.s1r.at[2 * d + t], (self.p.x_peer, self.p.y_peer)[t]) for t in range(2)]
+
+    def copies2(self, c):
+        d = c - N_RS
+        return [send(self.mid.at[pl.ds(al(d * 32 + 16 * t), 16)], self.d2.at[pl.ds(al(d * 32 + 16 * t), 16)],
+                     self.s2s.at[2 * d + t], self.s2r.at[2 * d + t], (self.p.y_peer, self.p.x_peer)[t]) for t in range(2)]
+
+    def step1(self, c):
+        for cp in self.copies1(c):
+            cp.wait_recv()
+        d = c - N_RS
+        v, s = self.red.merge(al(c * CHUNK + 32 * self.p.core), self.d1, al(d * 32), 32)
+        self.mid[pl.ds(al(d * 32), 32), :] = jnp.concatenate([v, s], axis=1)
+
+    def step2(self, c):
+        for cp in self.copies2(c):
+            cp.wait_recv()
+        rows = pl.ds(al((c - N_RS) * 32), 32)
+        a, b = self.mid[rows, :], self.d2[rows, :]
+        v, s = merge_rows((a[:, :QW], a[:, QW:]), (b[:, :QW], b[:, QW:]))
+        self.red.own[pl.ds(al(c * CHUNK + 32 * self.p.core), 32), :] = normalise(v, s)
+
+    def drain(self, c):
+        for cp in self.copies1(c) + self.copies2(c):
+            cp.wait_send()
 
 
 class Gather:
@@ -174,13 +215,12 @@
     def drain(self, c):
         self.copy0(c).wait_send()
         self.copy1(c).wait_send()
-        self.copy2(c).wait_send()
-
-
-def step_kernel(pos_row, freq_ref, ns_ref, b_ref, x_hbm, wq_hbm, wk_hbm, wv_hbm, wo_hbm, k_hbm, v_hbm,
-                kbuf, vbuf, out_ref,
+
+
+def step_kernel(pos_row, freq_ref, sp_ref, ns_ref, b_ref, x_hbm, wq_hbm, wk_hbm, wv_hbm, wo_hbm, k_hbm, v_hbm,
+                kbuf, vbuf, out_ref, sp_out,
                 x_v, wq_v, wk_v, wv_v, wo_v, n_v, q_v, kn_v, vn_v, p_col, js_col, cos_v, sin_v,
-                part, r0, r1, r2, g, w_sem, k_sem, v_sem, rsems, gsems):
+                part, r0, r1, r2, g, mid, d1, d2, w_sem, k_sem, v_sem, rsems, gsems, dsems):
     p = Places()
     barrier = pltpu.get_barrier_semaphore()
     for peer in (p.mate, p.x_peer, p.y_peer):
@@ -320,9 +360,10 @@
 
     red = Reduce(p, part, r0, r1, r2, g, [rsems.at[i] for i in range(6)])
     gat = Gather(p, g, [gsems.at[i] for i in range(6)])
-
-    def when_chunk(c, body):
-        @pl.when((c >= 0) & (c < NCHUNK))
+    dbl = Double(p, red, mid, d1, d2, [dsems.at[i] for i in range(4)])
+
+    def when_chunk(c, body, lo=0, hi=NCHUNK):
+        @pl.when((c >= lo) & (c < hi))
         def _():
             body(c)
 
@@ -376,10 +417,6 @@
 
     def project_out(c):
         gat.copy2(c).wait_recv()
-
-        @pl.when(c == 1)
-        def _():
-            w_in(4).wait()
 
         @pl.when(c % 2 == 1)
         def _():
@@ -388,24 +425,53 @@
             y = x_v[rows, :].astype(F32) + jnp.dot(o, wo_v[...], preferred_element_type=F32) + bias
             out_ref[rows, :] = y.astype(BF16)
 
-    lags = ((0, attend), (1, pair_step), (4, first_step), (6, second_step), (8, back_first), (10, back_second), (11, project_out))
-
-    @pl.loop(0, NCHUNK + lags[-1][0])
+    def pair_double(c):
+        red.step0(c)
+        for cp in dbl.copies1(c):
+            cp.start()
+
+    def double_first(c):
+        dbl.step1(c)
+        for cp in dbl.copies2(c):
+            cp.start()
+
+    def double_second(c):
+        dbl.step2(c)
+        gat.copy2(c).start()
+
+    p_all = pos_row[...]
+    slot_ids = off + lax.broadcasted_iota(jnp.int32, (SLOTS, BATCH), 0)
+    sp_out[...] = jnp.where(slot_ids == (p_all & 511), p_all, sp_ref[...])
+
+    lags = ((0, attend, 0, NCHUNK),
+            (1, pair_step, 0, N_RS), (1, pair_double, N_RS, NCHUNK),
+            (4, first_step, 0, N_RS), (4, double_first, N_RS, NCHUNK),
+            (7, second_step, 0, N_RS), (7, double_second, N_RS, NCHUNK),
+            (10, back_first, 0, N_RS), (13, back_second, 0, N_RS),
+            (15, project_out, 0, N_RS), (9, project_out, N_RS, NCHUNK))
+
+    @pl.loop(0, max(lag + hi for lag, _, _, hi in lags))
     def _(i):
-        for lag, body in lags:
-            when_chunk(i - lag, body)
+        @pl.when(i == NCHUNK + 2)
+        def _():
+            w_in(4).wait()
+
+        for lag, body, lo, hi in lags:
+            when_chunk(i - lag, body, lo, hi)
 
     @pl.loop(0, NCHUNK)
+    def _(c):
+        red.copy0(c).wait_send()
+        gat.copy2(c).wait_send()
+
+    @pl.loop(0, N_RS)
     def _(c):
         red.drain(c)
         gat.drain(c)
 
-
-def slot_kernel(pos_row, sp_ref, sp_out):
-    off = lax.axis_index('kv') * SLOTS
-    p_all = pos_row[...]
-    slot_ids = off + lax.broadcasted_iota(jnp.int32, (SLOTS, BATCH), 0)
-    sp_out[...] = jnp.where(slot_ids == (p_all & 511), p_all, sp_ref[...])
+    @pl.loop(N_RS, NCHUNK)
+    def _(c):
+        dbl.drain(c)
 
 
 def solution(mesh):
@@ -419,13 +485,14 @@
 
     def local_step(x_in, positions, k_cache, v_cache, slot_pos, norm_scale, w_q, w_k, w_v, w_o, b_o):
         pos_row = positions.reshape(1, BATCH)
-        kbuf, vbuf, x_new = pl.pallas_call(
+        kbuf, vbuf, x_new, sp_t = pl.pallas_call(
             step_kernel,
             out_shape=(pltpu.VMEM((BATCH, SLOTS, HEAD_DIM), BF16),
                        pltpu.VMEM((BATCH, SLOTS, HEAD_DIM), BF16),
-                       pltpu.VMEM((BATCH, D_MODEL), BF16)),
-            in_specs=[vmem, vmem, vmem, vmem, hbm, hbm, hbm, hbm, hbm, hbm, hbm],
-            out_specs=(vmem, vmem, vmem),
+                       pltpu.VMEM((BATCH, D_MODEL), BF16),
+                       pltpu.VMEM((SLOTS, BATCH), jnp.int32)),
+            in_specs=[vmem, vmem, vmem, vmem, vmem, hbm, hbm, hbm, hbm, hbm, hbm, hbm],
+            out_specs=(vmem, vmem, vmem, vmem),
             scratch_shapes=[
                 pltpu.VMEM((BATCH, D_MODEL), BF16),
                 pltpu.VMEM((D_MODEL, QW), BF16),
@@ -442,24 +509,22 @@
                 pltpu.VMEM((BATCH, 128), F32),
                 pltpu.VMEM((BATCH, PW), F32),
                 pltpu.VMEM((NCHUNK * 32, PW), F32),
-                pltpu.VMEM((NCHUNK * 16, PW), F32),
-                pltpu.VMEM((NCHUNK * 8, PW), F32),
+                pltpu.VMEM((N_RS * 16, PW), F32),
+                pltpu.VMEM((N_RS * 8, PW), F32),
                 pltpu.VMEM((BATCH, QW), F32),
+                pltpu.VMEM((N_RD * 32, PW), F32),
+                pltpu.VMEM((N_RD * 32, PW), F32),
+                pltpu.VMEM((N_RD * 32, PW), F32),
                 pltpu.SemaphoreType.DMA((5,)),
                 pltpu.SemaphoreType.DMA((NCHUNK,)),
                 pltpu.SemaphoreType.DMA((NCHUNK,)),
                 pltpu.SemaphoreType.DMA((6, NCHUNK)),
                 pltpu.SemaphoreType.DMA((6, NCHUNK)),
+                pltpu.SemaphoreType.DMA((4, 2 * N_RD)),
             ],
             cost_estimate=pl.CostEstimate(flops=5_000_000_000, bytes_accessed=40_000_000, transcendentals=200_000),
             compiler_params=pltpu.CompilerParams(collective_id=0, has_side_effects=True, vmem_limit_bytes=22 * 1024 * 1024),
-        )(pos_row, jnp.asarray(inv_freq_row()), norm_scale, b_o, x_in, w_q, w_k, w_v, w_o, k_cache, v_cache)
-        sp_t = pl.pallas_call(
-            slot_kernel,
-            out_shape=jax.ShapeDtypeStruct((SLOTS, BATCH), jnp.int32),
-            in_specs=[vmem, vmem],
-            out_specs=vmem,
-        )(pos_row, slot_pos.T)
+        )(pos_row, jnp.asarray(inv_freq_row()), slot_pos.T, norm_scale, b_o, x_in, w_q, w_k, w_v, w_o, k_cache, v_cache)
         return x_new, kbuf, vbuf, sp_t.T
 
 

time: 59.8 us -> 58.1 us (0.972)
  Pallas kernels: 45.6 us -> 43.4 us
  local copies, waits for them, and re-layouts: 13.3 us -> 14 us
    pallas_call x1 -> x0, Pallas kernels: 1.59 us -> none  [local_step(): pl.pallas_call(slot_kernel, out_shape=jax.ShapeDtypeStruct((SLOTS, BATCH)...]
    unnamed x3 -> x4, local copies, waits for them, and re-layouts: 13.3 us -> 14 us
    pallas_call x1, Pallas kernels: 44 us -> 43.4 us  [local_step(): pl.pallas_call(step_kernel, out_shape=(pltpu.VMEM((BATCH, SLOTS, HEAD_DIM...]
where the time goes in v4:
time: 58.1 us; the launch traced here: 58 us
  Pallas kernels  43.4 us (75%)
  local copies, waits for them, and re-layouts  14 us (24%)
  between operations  0.64 us (1%)
    pallas_call x1, Pallas kernels, local_step(): pl.pallas_call(step_kernel, out_shape=(pltpu.VMEM((BATCH, SLOTS, HEAD_DIM...  43.4 us
    unnamed x4, local copies, waits for them, and re-layouts  14 us

profile of v4, /device:TPU:0, one launch (start us, length us, event | category | flops | bytes accessed | tf_op | source)
XLA Modules:
  0.0 58.0 jit_solution(318224592856535333)
XLA Ops:
  0.6 43.4 %shard_map.147 = (bf16[512,64,256]{2,1,0:T(8,128)(2,1)S(1)}, bf16[512,64,256]{2,1,0:T(8,128)(2,1)S(1)}, bf16[512,1152]{1,0:T(8,128)(2,1)S(1)}, s32[64,512]{1,0:T(8,128)S(1)}) custom-call(s32[1,512]{1,0:T(1,128)} %bitcast.5, f32[1,128]{1,0:T(1,128)} %constant.2.clone.freq_ref, s32[64,512]{1,0:T(8,128)} %bitcast.4, bf16[1152]{0:T(1024)(128)(2,1)} %ns_ref.1, ...), custom_call_target="tpu_custom_call" | custom-call | flops 5000000000 | bytes 40000000 | tf_op jit(solution)/shard_map/pallas_call | solution.py:488
  44.0 1.0 %copy.20 = bf16[512,1152]{1,0:T(8,128)(2,1)} copy(bf16[512,1152]{1,0:T(8,128)(2,1)S(1)} %get-tuple-element.12) | data formatting | bytes 2359296
  45.0 0.7 %copy.23 = s32[512,64]{0,1:T(8,128)} copy(s32[512,64]{0,1:T(8,128)S(1)} %bitcast.3) | data formatting | bytes 262144
  45.7 6.2 %copy.21 = bf16[512,64,256]{2,1,0:T(8,128)(2,1)} copy(bf16[512,64,256]{2,1,0:T(8,128)(2,1)S(1)} %get-tuple-element.13) | data formatting | bytes 33554432
  51.8 6.2 %copy.22 = bf16[512,64,256]{2,1,0:T(8,128)(2,1)} copy(bf16[512,64,256]{2,1,0:T(8,128)(2,1)S(1)} %get-tuple-element.14) | data formatting | bytes 33554432

commit v5 on v4

--- a/solution.py
+++ b/solution.py
@@ -226,7 +226,7 @@
     for peer in (p.mate, p.x_peer, p.y_peer):
         pl.semaphore_signal(barrier, inc=1, device_id={'kv': peer}, device_id_type=pl.DeviceIdType.MESH)
     off = lax.axis_index('kv') * SLOTS
-    weights = ((x_hbm, x_v), (wk_hbm, wk_v), (wv_hbm, wv_v), (wq_hbm, wq_v), (wo_hbm, wo_v))
+    weights = ((x_hbm, x_v), (wk_hbm, wk_v), (wv_hbm, wv_v), (wq_hbm, wq_v), (wo_hbm, wo_v), (sp_ref, sp_out))
 
     def w_in(n):
         return pltpu.make_async_copy(weights[n][0], weights[n][1], w_sem.at[n])
@@ -242,10 +242,6 @@
 
     for n in range(4):
         w_in(n).start()
-    for c in range(AHEAD):
-        k_in(c).start()
-        v_in(c).start()
-
     offf = off.astype(F32)
 
     @pl.loop(0, BATCH // 128)
@@ -270,6 +266,8 @@
         return jnp.concatenate([r, t[:, ROPE_DIM:]], axis=1)
 
     w_in(0).wait()
+    k_in(0).start()
+    v_in(0).start()
     gain = 1.0 + ns_ref[...].astype(F32).reshape(1, D_MODEL)
 
     @pl.loop(0, BATCH // 64)
@@ -282,6 +280,9 @@
     w_in(1).wait()
     w_in(2).wait()
     w_in(3).wait()
+    for c in range(1, AHEAD):
+        k_in(c).start()
+        v_in(c).start()
 
     def project(i):
         rows = pl.ds(pl.multiple_of(i * ROWS, ROWS), ROWS)
@@ -376,6 +377,7 @@
         @pl.when(i == AHEAD)
         def _():
             w_in(4).start()
+            w_in(5).start()
 
         @pl.when(i % (ROWS // CHUNK) == 0)
         def _():
@@ -438,10 +440,6 @@
     def double_second(c):
         dbl.step2(c)
         gat.copy2(c).start()
-
-    p_all = pos_row[...]
-    slot_ids = off + lax.broadcasted_iota(jnp.int32, (SLOTS, BATCH), 0)
-    sp_out[...] = jnp.where(slot_ids == (p_all & 511), p_all, sp_ref[...])
 
     lags = ((0, attend, 0, NCHUNK),
             (1, pair_step, 0, N_RS), (1, pair_double, N_RS, NCHUNK),
@@ -455,6 +453,10 @@
         @pl.when(i == NCHUNK + 2)
         def _():
             w_in(4).wait()
+            w_in(5).wait()
+            p_all = pos_row[...]
+            slot_ids = off + lax.broadcasted_iota(jnp.int32, (SLOTS, BATCH), 0)
+            sp_out[...] = jnp.where(slot_ids == (p_all & 511), p_all, sp_out[...])
 
         for lag, body, lo, hi in lags:
             when_chunk(i - lag, body, lo, hi)
@@ -491,7 +493,7 @@
                        pltpu.VMEM((BATCH, SLOTS, HEAD_DIM), BF16),
                        pltpu.VMEM((BATCH, D_MODEL), BF16),
                        pltpu.VMEM((SLOTS, BATCH), jnp.int32)),
-            in_specs=[vmem, vmem, vmem, vmem, vmem, hbm, hbm, hbm, hbm, hbm, hbm, hbm],
+            in_specs=[vmem, vmem, hbm, vmem, vmem, hbm, hbm, hbm, hbm, hbm, hbm, hbm],
             out_specs=(vmem, vmem, vmem, vmem),
             scratch_shapes=[
                 pltpu.VMEM((BATCH, D_MODEL), BF16),
@@ -515,7 +517,7 @@
                 pltpu.VMEM((N_RD * 32, PW), F32),
                 pltpu.VMEM((N_RD * 32, PW), F32),
                 pltpu.VMEM((N_RD * 32, PW), F32),
-                pltpu.SemaphoreType.DMA((5,)),
+                pltpu.SemaphoreType.DMA((6,)),
                 pltpu.SemaphoreType.DMA((NCHUNK,)),
                 pltpu.SemaphoreType.DMA((NCHUNK,)),
                 pltpu.SemaphoreType.DMA((6, NCHUNK)),

time: 58.1 us -> 54.5 us (0.938)
  Pallas kernels: 43.4 us -> 39.8 us
    pallas_call x1, Pallas kernels: 43.4 us -> 39.8 us  [local_step(): pl.pallas_call(step_kernel, out_shape=(pltpu.VMEM((BATCH, SLOTS, HEAD_DIM...]
where the time goes in v5:
time: 54.5 us; the launch traced here: 54.4 us
  Pallas kernels  39.8 us (73%)
  local copies, waits for them, and re-layouts  14 us (26%)
  between operations  0.64 us (1%)
    pallas_call x1, Pallas kernels, local_step(): pl.pallas_call(step_kernel, out_shape=(pltpu.VMEM((BATCH, SLOTS, HEAD_DIM...  39.8 us
    unnamed x4, local copies, waits for them, and re-layouts  14 us

profile of v5, /device:TPU:0, one launch (start us, length us, event | category | flops | bytes accessed | tf_op | source)
XLA Modules:
  0.0 54.4 jit_solution(10265843754659482449)
XLA Ops:
  0.6 39.8 %shard_map.147 = (bf16[512,64,256]{2,1,0:T(8,128)(2,1)S(1)}, bf16[512,64,256]{2,1,0:T(8,128)(2,1)S(1)}, bf16[512,1152]{1,0:T(8,128)(2,1)S(1)}, s32[64,512]{1,0:T(8,128)S(1)}) custom-call(s32[1,512]{1,0:T(1,128)} %bitcast.5, f32[1,128]{1,0:T(1,128)} %constant.2.clone.freq_ref, s32[64,512]{1,0:T(8,128)} %bitcast.4, bf16[1152]{0:T(1024)(128)(2,1)} %ns_ref.1, ...), custom_call_target="tpu_custom_call" | custom-call | flops 5000000000 | bytes 40000000 | tf_op jit(solution)/shard_map/pallas_call | solution.py:490
  40.4 1.0 %copy.20 = bf16[512,1152]{1,0:T(8,128)(2,1)} copy(bf16[512,1152]{1,0:T(8,128)(2,1)S(1)} %get-tuple-element.12) | data formatting | bytes 2359296
  41.4 0.7 %copy.23 = s32[512,64]{0,1:T(8,128)} copy(s32[512,64]{0,1:T(8,128)S(1)} %bitcast.3) | data formatting | bytes 262144
  42.1 6.2 %copy.21 = bf16[512,64,256]{2,1,0:T(8,128)(2,1)} copy(bf16[512,64,256]{2,1,0:T(8,128)(2,1)S(1)} %get-tuple-element.13) | data formatting | bytes 33554432
  48.2 6.2 %copy.22 = bf16[512,64,256]{2,1,0:T(8,128)(2,1)} copy(bf16[512,64,256]{2,1,0:T(8,128)(2,1)S(1)} %get-tuple-element.14) | data formatting | bytes 33554432

commit v6 on v3

v6 whole, which is shorter than its diff:
```python
import functools

import jax
import jax.numpy as jnp
import numpy as np
from jax import lax
from jax.experimental import pallas as pl
from jax.experimental.pallas import tpu as pltpu
from jax.sharding import PartitionSpec as P

HEADS = 4
HEAD_DIM = 256
ROPE_DIM = 128
ROPE_HALF = ROPE_DIM // 2
ROPE_BASE = 10000.0
EPS = 1e-6
SCORE_SCALE = HEAD_DIM ** -0.5
NEG_LARGE = float(np.finfo(np.float32).min)
FAR = 1e9
F32 = jnp.float32
BF16 = jnp.bfloat16

BATCH = 512
D_MODEL = 1152
SLOTS = 64
QW = HEADS * HEAD_DIM
PW = QW + 128
GROUP = 8
STEP = 64
CHUNK = 64
AHEAD = 4
NCHUNK = BATCH // CHUNK
EARLY = 4
SPLIT = EARLY * CHUNK
LATE = BATCH - SPLIT
ROWS = 256


def sin_cos(theta):
    k = jnp.floor(theta * np.float32(2.0 / np.pi) + 0.5)
    r = theta - k * np.float32(1.5703125)
    r = r - k * np.float32(4.83751296997070312e-4)
    r = r - k * np.float32(7.54978995489188e-8)
    r2 = r * r
    s = r + r * r2 * (-1.6666654611e-1 + r2 * (8.3321608736e-3 + r2 * -1.9515295891e-4))
    c = 1.0 - 0.5 * r2 + r2 * r2 * (4.166664568298827e-2 + r2 * (-1.388731625493765e-3 + r2 * 2.443315711809948e-5))
    q = k - 4.0 * jnp.floor(k * 0.25)
    swap = (q == 1.0) | (q == 3.0)
    sin_v = jnp.where(swap, c, s)
    cos_v = jnp.where(swap, s, c)
    sin_v = jnp.where(q >= 2.0, -sin_v, sin_v)
    cos_v = jnp.where((q == 1.0) | (q == 2.0), -cos_v, cos_v)
    return sin_v, cos_v


def inv_freq_row():
    i = np.arange(ROPE_DIM) % ROPE_HALF
    return (ROPE_BASE ** (-i / ROPE_HALF)).astype(np.float32).reshape(1, ROPE_DIM)


def merge_rows(a_rows, b_rows):
    sa, sb = a_rows[1], b_rows[1]
    lane = lax.broadcasted_iota(jnp.int32, sa.shape, 1)
    ma, mb = sa, sb
    mm = jnp.maximum(ma, mb)
    fa, fb = jnp.exp(ma - mm), jnp.exp(mb - mm)
    fa_l = pltpu.roll(fa, HEADS, 1)
    fb_l = pltpu.roll(fb, HEADS, 1)
    stats = jnp.where(lane < HEADS, mm, sa * fa_l + sb * fb_l)
    vals = []
    for h in range(HEADS):
        va = a_rows[0][:, h * HEAD_DIM:(h + 1) * HEAD_DIM]
        vb = b_rows[0][:, h * HEAD_DIM:(h + 1) * HEAD_DIM]
        vals.append(va * fa[:, h:h + 1] + vb * fb[:, h:h + 1])
    return jnp.concatenate(vals, axis=1), stats


def normalise(v, s):
    inv = 1.0 / s
    return jnp.concatenate([v[:, h * HEAD_DIM:(h + 1) * HEAD_DIM] * inv[:, HEADS + h:HEADS + h + 1] for h in range(HEADS)], axis=1)


class Places:
    def __init__(self):
        me = lax.axis_index('kv')
        self.core = me % 2
        self.x = (me // 2) % 2
        self.y = me // 4
        self.mate = me + 1 - 2 * self.core
        self.x_peer = me + 2 - 4 * self.x
        self.y_peer = me + 4 - 8 * self.y

    def first(self, c):
        odd = c % 2
        return self.x_peer + odd * (self.y_peer - self.x_peer), self.x + odd * (self.y - self.x)

    def second(self, c):
        odd = c % 2
        return self.y_peer + odd * (self.x_peer - self.y_peer), self.y + odd * (self.x - self.y)


def send(src, dst, ss, rs, peer):
    return pltpu.make_async_remote_copy(src_ref=src, dst_ref=dst, send_sem=ss, recv_sem=rs,
                                        device_id={'kv': peer}, device_id_type=pl.DeviceIdType.MESH)


def al(v, m=8):
    return pl.multiple_of(v, m)


class Reduce:
    def __init__(self, places, part, r0, r1, r2, own, sems):
        self.p = places
        self.part, self.r0, self.r1, self.r2, self.own = part, r0, r1, r2, own
        self.s0s, self.s0r, self.s1s, self.s1r, self.s2s, self.s2r = sems

    def copy0(self, c):
        src = al(c * CHUNK + 32 * (1 - self.p.core))
        return send(self.part.at[pl.ds(src, 32)], self.r0.at[pl.ds(al(c * 32), 32)], self.s0s.at[c], self.s0r.at[c], self.p.mate)

    def copy1(self, c):
        peer, k = self.p.first(c)
        src = al(c * CHUNK + 32 * self.p.core + 16 * (1 - k))
        return send(self.part.at[pl.ds(src, 16)], self.r1.at[pl.ds(al(c * 16), 16)], self.s1s.at[c], self.s1r.at[c], peer)

    def copy2(self, c):
        peer, k2 = self.p.second(c)
        k1 = self.p.first(c)[1]
        src = al(c * CHUNK + 32 * self.p.core + 16 * k1 + 8 * (1 - k2))
        return send(self.part.at[pl.ds(src, 8)], self.r2.at[pl.ds(al(c * 8), 8)], self.s2s.at[c], self.s2r.at[c], peer)

    def merge(self, mine, other_ref, theirs, n):
        a = self.part[pl.ds(mine, n), :]
        b = other_ref[pl.ds(theirs, n), :]
        return merge_rows((a[:, :QW], a[:, QW:]), (b[:, :QW], b[:, QW:]))

    def step0(self, c):
        self.copy0(c).wait_recv()
        base = al(c * CHUNK + 32 * self.p.core)
        v, s = self.merge(base, self.r0, al(c * 32), 32)
        self.part[pl.ds(base, 32), :] = jnp.concatenate([v, s], axis=1)

    def step1(self, c):
        self.copy1(c).wait_recv()
        base = al(c * CHUNK + 32 * self.p.core + 16 * self.p.first(c)[1])
        v, s = self.merge(base, self.r1, al(c * 16), 16)
        self.part[pl.ds(base, 16), :] = jnp.concatenate([v, s], axis=1)

    def step2(self, c):
        self.copy2(c).wait_recv()
        base = al(c * CHUNK + 32 * self.p.core + 16 * self.p.first(c)[1] + 8 * self.p.second(c)[1])
        v, s = self.merge(base, self.r2, al(c * 8), 8)
        self.own[pl.ds(base, 8), :] = normalise(v, s)

    def drain(self, c):
        self.copy1(c).wait_send()
        self.copy2(c).wait_send()


class Gather:
    def __init__(self, places, g, sems):
        self.p, self.g = places, g
        self.s0s, self.s0r, self.s1s, self.s1r, self.s2s, self.s2r = sems

    def copy0(self, c):
        peer, k2 = self.p.second(c)
        k1 = self.p.first(c)[1]
        rows = pl.ds(al(c * CHUNK + 32 * self.p.core + 16 * k1 + 8 * k2), 8)
        return send(self.g.at[rows], self.g.at[rows], self.s0s.at[c], self.s0r.at[c], peer)

    def copy1(self, c):
        peer, k1 = self.p.first(c)
        rows = pl.ds(al(c * CHUNK + 32 * self.p.core + 16 * k1), 16)
        return send(self.g.at[rows], self.g.at[rows], self.s1s.at[c], self.s1r.at[c], peer)

    def copy2(self, c):
        rows = pl.ds(al(c * CHUNK + 32 * self.p.core), 32)
        return send(self.g.at[rows], self.g.at[rows], self.s2s.at[c], self.s2r.at[c], self.p.mate)

    def drain(self, c):
        self.copy0(c).wait_send()
        self.copy1(c).wait_send()


SLOTS_TOTAL = 37
PLAN = (
    (0, ((4, 0), (5, 4), (6, 5), (7, 6))),
    (1, ((0, 0), (1, 1), (2, 2), (3, 3), (4, 4), (5, 6), (6, 7), (7, 9))),
    (2, ()),
    (3, ((0, 7), (1, 8), (2, 9), (3, 10), (4, 11), (5, 12), (6, 13), (7, 16))),
    (4, ()),
    (5, ((0, 13), (1, 14), (2, 15), (3, 16), (4, 17), (5, 18), (6, 19), (7, 22))),
    (6, ()),
    (7, ((0, 19), (1, 20), (2, 21), (3, 22), (4, 23), (5, 24), (6, 25), (7, 27))),
    (8, ((0, 25), (1, 26), (2, 28), (3, 29), (4, 30), (5, 31), (6, 33), (7, 34))),
    (9, ((0, 27), (1, 28), (2, 30), (3, 31), (4, 32), (5, 34), (6, 35), (7, 36))),
)


class Attention:
    def __init__(self, off, kbuf, vbuf, q_v, kn_v, vn_v, p_col, js_col, part, shift):
        self.refs = kbuf, vbuf, q_v, kn_v, vn_v, p_col, js_col, part
        self.shift = shift
        self.sub = lax.broadcasted_iota(jnp.int32, (GROUP, 128), 0)
        self.lane = lax.broadcasted_iota(jnp.int32, (GROUP, 128), 1)
        self.slot_c = jnp.where((self.lane // SLOTS) == (self.sub % 2), (self.lane % SLOTS).astype(F32) + off.astype(F32), FAR)
        self.pick = [(self.sub // 2) == cc for cc in range(4)]
        self.iotas = [(lax.broadcasted_iota(jnp.int32, (16, HEAD_DIM), 0) + 16 * t).astype(F32).astype(BF16) for t in range(SLOTS // 16)]

    def rows(self, base):
        kbuf, vbuf, q_v, kn_v, vn_v, p_col, js_col, part = self.refs
        pick, iotas, lane, slot_c = self.pick, self.iotas, self.lane, self.slot_c

        def hits_of(b):
            js = jnp.broadcast_to(js_col[pl.ds(b, 1), :], (16, 128)).astype(BF16)
            js = jnp.concatenate([js, js], axis=1)
            return [io == js for io in iotas]

        def refresh(buf, new_ref, r0):
            out = []
            for i in range(GROUP):
                b = r0 + i
                hits = hits_of(b)
                fresh = jnp.broadcast_to(new_ref[pl.ds(b, 1), :], (16, HEAD_DIM)).astype(BF16)
                for t in range(SLOTS // 16):
                    piece = jnp.where(hits[t], fresh, buf[b, pl.ds(16 * t, 16), :])
                    buf[b, pl.ds(16 * t, 16), :] = piece
                    out.append(piece)
            return jnp.concatenate(out, axis=0)

        def scores(r0):
            rows = pl.ds(r0, GROUP)
            q = jnp.concatenate([q_v[rows, h * HEAD_DIM:(h + 1) * HEAD_DIM] for h in range(HEADS)], axis=0).astype(BF16)
            s = lax.dot_general(q, refresh(kbuf, kn_v, r0), (((1,), (1,)), ((), ())), preferred_element_type=F32)
            out = []
            for h in range(HEADS):
                sh = s[h * GROUP:(h + 1) * GROUP, :]
                c = sh[:, 384:512]
                for cc in range(3):
                    c = jnp.where(pick[cc], sh[:, cc * 128:(cc + 1) * 128], c)
                out.append(c)
            return out

        def soften(r0, cs):
            valid = slot_c <= p_col[pl.ds(r0, GROUP), :]
            stats = jnp.zeros((GROUP, 128), F32)
            ps = []
            for h in range(HEADS):
                c = jnp.where(valid, cs[h], NEG_LARGE)
                m = jnp.max(c, axis=1, keepdims=True)
                e = jnp.where(valid, jnp.exp(c - m), 0.0)
                l = jnp.sum(e, axis=1, keepdims=True)
                stats = jnp.where(lane == h, m, stats)
                stats = jnp.where(lane == HEADS + h, l, stats)
                ps.append(e)
            part[pl.ds(r0 + self.shift, GROUP), QW:PW] = stats
            return ps

        def values(r0, ps):
            pm = jnp.concatenate([jnp.concatenate([jnp.where(pick[cc], e, 0.0) for cc in range(4)], axis=1) for e in ps], axis=0).astype(BF16)
            o = jnp.dot(pm, refresh(vbuf, vn_v, r0), preferred_element_type=F32)
            rows = pl.ds(r0 + self.shift, GROUP)
            for h in range(HEADS):
                part[rows, h * HEAD_DIM:(h + 1) * HEAD_DIM] = o[h * GROUP:(h + 1) * GROUP, :]

        starts = [al(base + g * GROUP, GROUP) for g in range(CHUNK // GROUP)]
        cs = [scores(r0) for r0 in starts]
        ps = [soften(r0, c) for r0, c in zip(starts, cs)]
        for r0, e in zip(starts, ps):
            values(r0, e)


def chunk_rows(c):
    return pl.ds(pl.multiple_of(c * CHUNK, CHUNK), CHUNK)


def early_kernel(pos_row, freq_ref, ns_ref, sp_hbm, x_hbm, wq_hbm, wk_hbm, wv_hbm, k_hbm, v_hbm,
                 part, q_late, kn_late, vn_late, p_late, js_late, sp_out, k_out, v_out,
                 kbuf, vbuf, x_v, wq_v, wk_v, wv_v, n_v, q_v, kn_v, vn_v, p_col, js_col, cos_v, sin_v,
                 w_sem, k_sem, v_sem, ko_sem, vo_sem):
    off = lax.axis_index('kv') * SLOTS
    weights = ((x_hbm, x_v), (wk_hbm, wk_v), (wv_hbm, wv_v), (wq_hbm, wq_v), (sp_hbm, sp_out))

    def w_in(n):
        return pltpu.make_async_copy(weights[n][0], weights[n][1], w_sem.at[n])

    def kv_in(c):
        return (pltpu.make_async_copy(k_hbm.at[chunk_rows(c)], kbuf.at[chunk_rows(c)], k_sem.at[c]),
                pltpu.make_async_copy(v_hbm.at[chunk_rows(c)], vbuf.at[chunk_rows(c)], v_sem.at[c]))

    def kv_back(c):
        return (pltpu.make_async_copy(kbuf.at[chunk_rows(c)], k_out.at[chunk_rows(c)], ko_sem.at[c]),
                pltpu.make_async_copy(vbuf.at[chunk_rows(c)], v_out.at[chunk_rows(c)], vo_sem.at[c]))

    for n in range(4):
        w_in(n).start()

    offf = off.astype(F32)

    @pl.loop(0, BATCH // 128)
    def _(t):
        rows = pl.ds(pl.multiple_of(t * 128, 128), 128)
        col = jnp.broadcast_to(pos_row[:, rows].astype(F32), (128, 128)).T
        p_col[rows, :] = col
        js = col - 512.0 * jnp.floor(col * (1.0 / 512.0)) - offf
        js_col[rows, :] = jnp.where((js >= 0.0) & (js < float(SLOTS)), js, -1.0)

    @pl.loop(0, BATCH // 64)
    def _(t):
        rows = pl.ds(pl.multiple_of(t * 64, 64), 64)
        s, c = sin_cos(p_col[rows, :] * freq_ref[...])
        lane = lax.broadcasted_iota(jnp.int32, (64, 128), 1)
        sin_v[rows, :] = jnp.where(lane < ROPE_HALF, -s, s)
        cos_v[rows, :] = c

    p_late[...] = p_col[SPLIT:, :]
    js_late[...] = js_col[SPLIT:, :]

    def rotate(t, rows):
        r = t[:, :ROPE_DIM]
        r = r * cos_v[rows, :] + pltpu.roll(r, ROPE_HALF, 1) * sin_v[rows, :]
        return jnp.concatenate([r, t[:, ROPE_DIM:]], axis=1)

    w_in(0).wait()
    for cp in kv_in(0):
        cp.start()
    gain = 1.0 + ns_ref[...].astype(F32).reshape(1, D_MODEL)

    @pl.loop(0, BATCH // 64)
    def _(i):
        rows = pl.ds(pl.multiple_of(i * 64, 64), 64)
        xf = x_v[rows, :].astype(F32)
        mean_sq = jnp.sum(xf * xf, axis=1, keepdims=True) * (1.0 / D_MODEL)
        n_v[rows, :] = (xf * lax.rsqrt(mean_sq + EPS) * gain).astype(BF16)

    for n in range(1, 4):
        w_in(n).wait()
    for c in range(1, EARLY):
        for cp in kv_in(c):
            cp.start()
    w_in(4).start()

    def project(lo, n, q_to, k_to, v_to):
        rows = pl.ds(lo, n)
        k_to[...] = rotate(jnp.dot(n_v[rows, :], wk_v[...], preferred_element_type=F32), rows)
        v_to[...] = jnp.dot(n_v[rows, :], wv_v[...], preferred_element_type=F32)
        for h in range(HEADS):
            cols = pl.ds(h * HEAD_DIM, HEAD_DIM)
            qh = jnp.dot(n_v[rows, :], wq_v[:, cols], preferred_element_type=F32)
            q_to[:, cols] = rotate(qh, rows) * SCORE_SCALE

    project(0, SPLIT, q_v, kn_v, vn_v)
    att = Attention(off, kbuf, vbuf, q_v, kn_v, vn_v, p_col, js_col, part, 0)

    @pl.loop(0, EARLY)
    def _(c):
        for cp in kv_in(c):
            cp.wait()
        att.rows(c * CHUNK)
        for cp in kv_back(c):
            cp.start()

    project(SPLIT, LATE, q_late, kn_late, vn_late)
    w_in(4).wait()
    p_all = pos_row[...]
    slot_ids = off + lax.broadcasted_iota(jnp.int32, (SLOTS, BATCH), 0)
    sp_out[...] = jnp.where(slot_ids == (p_all & 511), p_all, sp_out[...])

    @pl.loop(0, EARLY)
    def _(c):
        for cp in kv_back(c):
            cp.wait()


def late_kernel(part_in, q_v, kn_v, vn_v, p_col, js_col, x_v, wo_v, b_ref, k_hbm, v_hbm,
                kbuf, vbuf, out_ref,
                part, r0, r1, r2, g, l_sem, k_sem, v_sem, rsems, gsems):
    p = Places()
    barrier = pltpu.get_barrier_semaphore()
    for peer in (p.mate, p.x_peer, p.y_peer):
        pl.semaphore_signal(barrier, inc=1, device_id={'kv': peer}, device_id_type=pl.DeviceIdType.MESH)
    off = lax.axis_index('kv') * SLOTS
    load = pltpu.make_async_copy(part_in, part.at[pl.ds(0, SPLIT)], l_sem)
    load.start()

    def kv_in(j):
        return (pltpu.make_async_copy(k_hbm.at[chunk_rows(j + EARLY)], kbuf.at[chunk_rows(j)], k_sem.at[j]),
                pltpu.make_async_copy(v_hbm.at[chunk_rows(j + EARLY)], vbuf.at[chunk_rows(j)], v_sem.at[j]))

    for cp in kv_in(0):
        cp.start()
    load.wait()
    red = Reduce(p, part, r0, r1, r2, g, [rsems.at[i] for i in range(6)])
    gat = Gather(p, g, [gsems.at[i] for i in range(6)])
    att = Attention(off, kbuf, vbuf, q_v, kn_v, vn_v, p_col, js_col, part, SPLIT)
    pl.semaphore_wait(barrier, 3)

    @pl.loop(0, EARLY)
    def _(c):
        red.copy0(c).start()

    for j in range(1, NCHUNK - EARLY):
        for cp in kv_in(j):
            cp.start()

    def when_chunk(c, body, lo=0, hi=NCHUNK):
        @pl.when((c >= lo) & (c < hi))
        def _():
            body(c)

    def attend(c):
        for cp in kv_in(c - EARLY):
            cp.wait()
        att.rows((c - EARLY) * CHUNK)
        red.copy0(c).start()

    def pair_step(c):
        red.step0(c)
        red.copy1(c).start()

    def first_step(c):
        red.step1(c)
        red.copy2(c).start()

    def second_step(c):
        red.step2(c)
        gat.copy0(c).start()

    def back_first(c):
        gat.copy0(c).wait_recv()
        gat.copy1(c).start()

    def back_second(c):
        gat.copy1(c).wait_recv()
        gat.copy2(c).start()

    bias = b_ref[...].astype(F32).reshape(1, D_MODEL)

    def project_out(c):
        gat.copy2(c).wait_recv()

        @pl.when(c % 2 == 1)
        def _():
            rows = pl.ds(al((c - 1) * CHUNK, CHUNK), 2 * CHUNK)
            o = g[rows, :].astype(BF16)
            y = x_v[rows, :].astype(F32) + jnp.dot(o, wo_v[...], preferred_element_type=F32) + bias
            out_ref[rows, :] = y.astype(BF16)

    stages = (attend, pair_step, None, first_step, None, second_step, None, back_first, back_second, project_out)
    plan = [(stages[n], at) for n, at in PLAN if at]

    @pl.loop(0, SLOTS_TOTAL)
    def _(i):
        for body, at in plan:
            lo, hi = at[0][0], at[-1][0] + 1
            c = lo
            live = i == at[0][1]
            for k, slot in at[1:]:
                c = c + jnp.where(i >= slot, 1, 0)
                live = live | (i == slot)

            @pl.when(live)
            def _(body=body, c=c):
                body(c)

    @pl.loop(0, NCHUNK)
    def _(c):
        red.copy0(c).wait_send()
        gat.copy2(c).wait_send()

    @pl.loop(0, NCHUNK)
    def _(c):
        red.drain(c)
        gat.drain(c)


def solution(mesh):
    row_spec = P('dp', None)
    cache_spec = P('dp', 'kv', None)
    slot_spec = P('dp', 'kv')
    vec_spec = P(None)
    mat_spec = P(None, None)
    hbm = pl.BlockSpec(memory_space=pltpu.HBM)
    vmem = pl.BlockSpec(memory_space=pltpu.VMEM)

    def local_step(x_in, positions, k_cache, v_cache, slot_pos, norm_scale, w_q, w_k, w_v, w_o, b_o):
        part, q_late, kn_late, vn_late, p_late, js_late, sp_t, k_mid, v_mid = pl.pallas_call(
            early_kernel,
            out_shape=(jax.ShapeDtypeStruct((SPLIT, PW), F32),
                       jax.ShapeDtypeStruct((LATE, QW), F32),
                       jax.ShapeDtypeStruct((LATE, HEAD_DIM), F32),
                       jax.ShapeDtypeStruct((LATE, HEAD_DIM), F32),
                       jax.ShapeDtypeStruct((LATE, 128), F32),
                       jax.ShapeDtypeStruct((LATE, 128), F32),
                       jax.ShapeDtypeStruct((SLOTS, BATCH), jnp.int32),
                       jax.ShapeDtypeStruct(k_cache.shape, BF16),
                       jax.ShapeDtypeStruct(v_cache.shape, BF16)),
            in_specs=[vmem, vmem, vmem, hbm, hbm, hbm, hbm, hbm, hbm, hbm],
            out_specs=(vmem, vmem, vmem, vmem, vmem, vmem, vmem, hbm, hbm),
            scratch_shapes=[
                pltpu.VMEM((SPLIT, SLOTS, HEAD_DIM), BF16),
                pltpu.VMEM((SPLIT, SLOTS, HEAD_DIM), BF16),
                pltpu.VMEM((BATCH, D_MODEL), BF16),
                pltpu.VMEM((D_MODEL, QW), BF16),
                pltpu.VMEM((D_MODEL, HEAD_DIM), BF16),
                pltpu.VMEM((D_MODEL, HEAD_DIM), BF16),
                pltpu.VMEM((BATCH, D_MODEL), BF16),
                pltpu.VMEM((SPLIT, QW), F32),
                pltpu.VMEM((SPLIT, HEAD_DIM), F32),
                pltpu.VMEM((SPLIT, HEAD_DIM), F32),
                pltpu.VMEM((BATCH, 128), F32),
                pltpu.VMEM((BATCH, 128), F32),
                pltpu.VMEM((BATCH, 128), F32),
                pltpu.VMEM((BATCH, 128), F32),
                pltpu.SemaphoreType.DMA((5,)),
                pltpu.SemaphoreType.DMA((EARLY,)),
                pltpu.SemaphoreType.DMA((EARLY,)),
                pltpu.SemaphoreType.DMA((EARLY,)),
                pltpu.SemaphoreType.DMA((EARLY,)),
            ],
            cost_estimate=pl.CostEstimate(flops=3_000_000_000, bytes_accessed=40_000_000, transcendentals=100_000),
            compiler_params=pltpu.CompilerParams(vmem_limit_bytes=40 * 1024 * 1024),
        )(positions.reshape(1, BATCH), jnp.asarray(inv_freq_row()), norm_scale, *[pltpu.with_memory_space_constraint(a, pltpu.HBM) for a in (slot_pos.T, x_in, w_q, w_k, w_v, k_cache, v_cache)])
        k_new, v_new, x_out = pl.pallas_call(
            late_kernel,
            out_shape=(pltpu.VMEM((LATE, SLOTS, HEAD_DIM), BF16),
                       pltpu.VMEM((LATE, SLOTS, HEAD_DIM), BF16),
                       pltpu.VMEM((BATCH, D_MODEL), BF16)),
            in_specs=[pl.BlockSpec(memory_space=pl.ANY)] + [vmem] * 8 + [hbm, hbm],
            out_specs=(vmem, vmem, vmem),
            scratch_shapes=[
                pltpu.VMEM((BATCH, PW), F32),
                pltpu.VMEM((NCHUNK * 32, PW), F32),
                pltpu.VMEM((NCHUNK * 16, PW), F32),
                pltpu.VMEM((NCHUNK * 8, PW), F32),
                pltpu.VMEM((BATCH, QW), F32),
                pltpu.SemaphoreType.DMA,
                pltpu.SemaphoreType.DMA((NCHUNK - EARLY,)),
                pltpu.SemaphoreType.DMA((NCHUNK - EARLY,)),
                pltpu.SemaphoreType.DMA((6, NCHUNK)),
                pltpu.SemaphoreType.DMA((6, NCHUNK)),
            ],
            cost_estimate=pl.CostEstimate(flops=3_000_000_000, bytes_accessed=20_000_000, transcendentals=100_000),
            compiler_params=pltpu.CompilerParams(collective_id=0, has_side_effects=True, vmem_limit_bytes=24 * 1024 * 1024),
        )(part, q_late, kn_late, vn_late, p_late, js_late, x_in, w_o, b_o, k_cache, v_cache)
        k_out = lax.dynamic_update_slice(k_mid, k_new, (SPLIT, 0, 0))
        v_out = lax.dynamic_update_slice(v_mid, v_new, (SPLIT, 0, 0))
        return x_out, k_out, v_out, sp_t.T

    return jax.shard_map(
        local_step,
        mesh=mesh,
        in_specs=(row_spec, P('dp'), cache_spec, cache_spec, slot_spec, vec_spec, mat_spec, mat_spec, mat_spec, mat_spec, vec_spec),
        out_specs=(row_spec, cache_spec, cache_spec, slot_spec),
        check_vma=False)
```

time: 59.8 us -> 58 us (0.970)
  local copies, waits for them, and re-layouts: 13.3 us -> 9.51 us
  Pallas kernels: 45.6 us -> 47.7 us
    unnamed x3 -> x13, local copies, waits for them, and re-layouts: 13.3 us -> 3.04 us
    dynamic_update_slice x0 -> x1, local copies, waits for them, and re-layouts: none -> 6.46 us  [local_step(): v_out = lax.dynamic_update_slice(v_mid, v_new, (SPLIT, 0, 0))]
    pallas_call x2, Pallas kernels: 45.6 us -> 47.7 us  [the longest x1 32.7 us: local_step(): pl.pallas_call(late_kernel, out_shape=(pltpu.VMEM((LATE, SLOTS, HEAD_DIM)...]
where the time goes in v6:
time: 58 us; the launch traced here: 57.9 us
  Pallas kernels  47.7 us (82%)
  local copies, waits for them, and re-layouts  9.51 us (16%)
  between operations  0.69 us (1%)
    pallas_call x1, Pallas kernels, local_step(): pl.pallas_call(late_kernel, out_shape=(pltpu.VMEM((LATE, SLOTS, HEAD_DIM)...  32.7 us
    pallas_call x1, Pallas kernels, local_step(): pl.pallas_call(early_kernel, out_shape=(jax.ShapeDtypeStruct((SPLIT, PW),...  14.9 us
    dynamic_update_slice x1, local copies, waits for them, and re-layouts, local_step(): v_out = lax.dynamic_update_slice(v_mid, v_new, (SPLIT, 0, 0))  6.46 us
    unnamed x13, local copies, waits for them, and re-layouts  3.04 us

profile of v6, /device:TPU:0, one launch (start us, length us, event | category | flops | bytes accessed | tf_op | source)
XLA Modules:
  0.0 57.9 jit_solution(1322044167058068316)
XLA Ops:
  0.6 0.0 copy-start.2
  0.6 0.7 %copy-done.2 = bf16[1152]{0:T(1024)(128)(2,1)S(1)} copy-done((bf16[1152]{0:T(1024)(128)(2,1)S(1)}, bf16[1152]{0:T(1024)(128)(2,1)}, u32[]{:S(2)}) %copy-start.2) | copy-done | bytes 2328
  1.3 0.0 copy-start.4
  1.3 0.7 %copy-done.4 = s32[512]{0:T(512)S(1)} copy-done((s32[512]{0:T(512)S(1)}, s32[512]{0:T(512)}, u32[]{:S(2)}) %copy-start.4) | copy-done | bytes 2072
  2.0 0.0 copy-start.5
  2.0 0.7 %copy-done.5 = f32[1,128]{1,0:T(1,128)S(1)} copy-done((f32[1,128]{1,0:T(1,128)S(1)}, f32[1,128]{1,0:T(1,128)}, u32[]{:S(2)}) %copy-start.5) | copy-done | bytes 536
  2.7 0.0 copy-start
  2.7 0.0 copy-start.1
  2.7 0.0 copy-start.3
  2.7 14.9 %shard_map.147 = (f32[256,1152]{1,0:T(8,128)S(1)}, f32[256,1024]{1,0:T(8,128)S(1)}, f32[256,256]{1,0:T(8,128)S(1)}, f32[256,256]{1,0:T(8,128)S(1)}, f32[256,128]...) custom-call(s32[1,512]{1,0:T(1,128)S(1)} %bitcast.3, ...), custom_call_target="tpu_custom_call" | custom-call | flops 3000000000 | bytes 40000000 | tf_op jit(solution)/shard_map/pallas_call | solution.py:487
  17.6 0.0 copy-done
  17.6 0.0 copy-done.1
  17.6 0.0 copy-done.3
  17.6 32.7 %shard_map.148 = (bf16[256,64,256]{2,1,0:T(8,128)(2,1)S(1)}, bf16[256,64,256]{2,1,0:T(8,128)(2,1)S(1)}, bf16[512,1152]{1,0:T(8,128)(2,1)S(1)}) custom-call(f32[256,1152]{1,0:T(8,128)S(1)} %get-tuple-element.16.part_in, f32[256,1024]{1,0:T(8,128)S(1)} %get-tuple-element.17.q_v, f32[256,256]{1,0:T(8,128)S(1)} %get-tuple-element.18.kn_v, ...), custom_call_target="tpu_custom_call" | custom-call | flops 3000000000 | bytes 20000000 | tf_op jit(solution)/shard_map/pallas_call | solution.py:524
  50.4 1.0 %copy.19 = bf16[512,1152]{1,0:T(8,128)(2,1)} copy(bf16[512,1152]{1,0:T(8,128)(2,1)S(1)} %get-tuple-element.30) | data formatting | bytes 2359296
  51.4 6.5 %constant_dynamic-update-slice_fusion = (bf16[512,64,256]{2,1,0:T(8,128)(2,1)}, bf16[512,64,256]{2,1,0:T(8,128)(2,1)}) fusion(bf16[512,64,256]{2,1,0:T(8,128)(2,1)} %get-tuple-element.25, bf16[256,64,256]{2,1,0:T(8,128)(2,1)S(1)} %get-tuple-element.26, bf16[512,64,256]{2,1,0:T(8,128)(2,1)} %get-tuple-element.23, bf16[256,64,256]{2,1,0:T(8,128)(2,1)S(1)} %get-tuple-element.24), kind=kLoop, calls=%fused_computation | loop fusion | bytes 33554432 | tf_op jit(solution)/shard_map/dynamic_update_slice | solution.py:547
Async XLA Ops:
  0.6 0.7 %copy-start.2 = (bf16[1152]{0:T(1024)(128)(2,1)S(1)}, bf16[1152]{0:T(1024)(128)(2,1)}, u32[]{:S(2)}) copy-start(bf16[1152]{0:T(1024)(128)(2,1)} %ns_ref.1) | copy-start | bytes 6916
  1.3 0.7 %copy-start.4 = (s32[512]{0:T(512)S(1)}, s32[512]{0:T(512)}, u32[]{:S(2)}) copy-start(s32[512]{0:T(512)} %param.13) | copy-start | bytes 6148
  2.0 0.7 %copy-start.5 = (f32[1,128]{1,0:T(1,128)S(1)}, f32[1,128]{1,0:T(1,128)}, u32[]{:S(2)}) copy-start(f32[1,128]{1,0:T(1,128)} %constant.6.clone.freq_ref) | copy-start | bytes 1540
  2.7 14.9 %copy-start = (bf16[512,1152]{1,0:T(8,128)(2,1)S(1)}, bf16[512,1152]{1,0:T(8,128)(2,1)}, u32[]{:S(2)}) copy-start(bf16[512,1152]{1,0:T(8,128)(2,1)} %x_v.1) | copy-start | bytes 3538948
  2.7 15.0 %copy-start.1 = (bf16[1024,1152]{1,0:T(8,128)(2,1)S(1)}, bf16[1024,1152]{1,0:T(8,128)(2,1)}, u32[]{:S(2)}) copy-start(bf16[1024,1152]{1,0:T(8,128)(2,1)} %wo_v.1) | copy-start | bytes 7077892
  2.7 15.0 %copy-start.3 = (bf16[1152]{0:T(1024)(128)(2,1)S(1)}, bf16[1152]{0:T(1024)(128)(2,1)}, u32[]{:S(2)}) copy-start(bf16[1152]{0:T(1024)(128)(2,1)} %b_ref.1) | copy-start | bytes 6916

commit v7 on v6

v7 whole, which is shorter than its diff:
```python
import functools

import jax
import jax.numpy as jnp
import numpy as np
from jax import lax
from jax.experimental import pallas as pl
from jax.experimental.pallas import tpu as pltpu
from jax.sharding import PartitionSpec as P

HEADS = 4
HEAD_DIM = 256
ROPE_DIM = 128
ROPE_HALF = ROPE_DIM // 2
ROPE_BASE = 10000.0
EPS = 1e-6
SCORE_SCALE = HEAD_DIM ** -0.5
NEG_LARGE = float(np.finfo(np.float32).min)
FAR = 1e9
F32 = jnp.float32
BF16 = jnp.bfloat16

BATCH = 512
D_MODEL = 1152
SLOTS = 64
QW = HEADS * HEAD_DIM
PW = QW + 128
GROUP = 8
STEP = 64
CHUNK = 64
AHEAD = 4
NCHUNK = BATCH // CHUNK
ROWS = 256


def sin_cos(theta):
    k = jnp.floor(theta * np.float32(2.0 / np.pi) + 0.5)
    r = theta - k * np.float32(1.5703125)
    r = r - k * np.float32(4.83751296997070312e-4)
    r = r - k * np.float32(7.54978995489188e-8)
    r2 = r * r
    s = r + r * r2 * (-1.6666654611e-1 + r2 * (8.3321608736e-3 + r2 * -1.9515295891e-4))
    c = 1.0 - 0.5 * r2 + r2 * r2 * (4.166664568298827e-2 + r2 * (-1.388731625493765e-3 + r2 * 2.443315711809948e-5))
    q = k - 4.0 * jnp.floor(k * 0.25)
    swap = (q == 1.0) | (q == 3.0)
    sin_v = jnp.where(swap, c, s)
    cos_v = jnp.where(swap, s, c)
    sin_v = jnp.where(q >= 2.0, -sin_v, sin_v)
    cos_v = jnp.where((q == 1.0) | (q == 2.0), -cos_v, cos_v)
    return sin_v, cos_v


def inv_freq_row():
    i = np.arange(ROPE_DIM) % ROPE_HALF
    return (ROPE_BASE ** (-i / ROPE_HALF)).astype(np.float32).reshape(1, ROPE_DIM)


def merge_rows(a_rows, b_rows):
    sa, sb = a_rows[1], b_rows[1]
    lane = lax.broadcasted_iota(jnp.int32, sa.shape, 1)
    ma, mb = sa, sb
    mm = jnp.maximum(ma, mb)
    fa, fb = jnp.exp(ma - mm), jnp.exp(mb - mm)
    fa_l = pltpu.roll(fa, HEADS, 1)
    fb_l = pltpu.roll(fb, HEADS, 1)
    stats = jnp.where(lane < HEADS, mm, sa * fa_l + sb * fb_l)
    vals = []
    for h in range(HEADS):
        va = a_rows[0][:, h * HEAD_DIM:(h + 1) * HEAD_DIM]
        vb = b_rows[0][:, h * HEAD_DIM:(h + 1) * HEAD_DIM]
        vals.append(va * fa[:, h:h + 1] + vb * fb[:, h:h + 1])
    return jnp.concatenate(vals, axis=1), stats


def normalise(v, s):
    inv = 1.0 / s
    return jnp.concatenate([v[:, h * HEAD_DIM:(h + 1) * HEAD_DIM] * inv[:, HEADS + h:HEADS + h + 1] for h in range(HEADS)], axis=1)


class Places:
    def __init__(self):
        me = lax.axis_index('kv')
        self.core = me % 2
        self.x = (me // 2) % 2
        self.y = me // 4
        self.mate = me + 1 - 2 * self.core
        self.x_peer = me + 2 - 4 * self.x
        self.y_peer = me + 4 - 8 * self.y

    def first(self, c):
        odd = c % 2
        return self.x_peer + odd * (self.y_peer - self.x_peer), self.x + odd * (self.y - self.x)

    def second(self, c):
        odd = c % 2
        return self.y_peer + odd * (self.x_peer - self.y_peer), self.y + odd * (self.x - self.y)


def send(src, dst, ss, rs, peer):
    return pltpu.make_async_remote_copy(src_ref=src, dst_ref=dst, send_sem=ss, recv_sem=rs,
                                        device_id={'kv': peer}, device_id_type=pl.DeviceIdType.MESH)


def al(v, m=8):
    return pl.multiple_of(v, m)


class Reduce:
    def __init__(self, places, part, r0, r1, r2, own, sems):
        self.p = places
        self.part, self.r0, self.r1, self.r2, self.own = part, r0, r1, r2, own
        self.s0s, self.s0r, self.s1s, self.s1r, self.s2s, self.s2r = sems

    def copy0(self, c):
        src = al(c * CHUNK + 32 * (1 - self.p.core))
        return send(self.part.at[pl.ds(src, 32)], self.r0.at[pl.ds(al(c * 32), 32)], self.s0s.at[c], self.s0r.at[c], self.p.mate)

    def copy1(self, c):
        peer, k = self.p.first(c)
        src = al(c * CHUNK + 32 * self.p.core + 16 * (1 - k))
        return send(self.part.at[pl.ds(src, 16)], self.r1.at[pl.ds(al(c * 16), 16)], self.s1s.at[c], self.s1r.at[c], peer)

    def copy2(self, c):
        peer, k2 = self.p.second(c)
        k1 = self.p.first(c)[1]
        src = al(c * CHUNK + 32 * self.p.core + 16 * k1 + 8 * (1 - k2))
        return send(self.part.at[pl.ds(src, 8)], self.r2.at[pl.ds(al(c * 8), 8)], self.s2s.at[c], self.s2r.at[c], peer)

    def merge(self, mine, other_ref, theirs, n):
        a = self.part[pl.ds(mine, n), :]
        b = other_ref[pl.ds(theirs, n), :]
        return merge_rows((a[:, :QW], a[:, QW:]), (b[:, :QW], b[:, QW:]))

    def step0(self, c):
        self.copy0(c).wait_recv()
        base = al(c * CHUNK + 32 * self.p.core)
        v, s = self.merge(base, self.r0, al(c * 32), 32)
        self.part[pl.ds(base, 32), :] = jnp.concatenate([v, s], axis=1)

    def step1(self, c):
        self.copy1(c).wait_recv()
        base = al(c * CHUNK + 32 * self.p.core + 16 * self.p.first(c)[1])
        v, s = self.merge(base, self.r1, al(c * 16), 16)
        self.part[pl.ds(base, 16), :] = jnp.concatenate([v, s], axis=1)

    def step2(self, c):
        self.copy2(c).wait_recv()
        base = al(c * CHUNK + 32 * self.p.core + 16 * self.p.first(c)[1] + 8 * self.p.second(c)[1])
        v, s = self.merge(base, self.r2, al(c * 8), 8)
        self.own[pl.ds(al(c * 8), 8), :] = normalise(v, s)

    def drain(self, c):
        self.copy1(c).wait_send()
        self.copy2(c).wait_send()


class Attention:
    def __init__(self, off, kbuf, vbuf, q_v, kn_v, vn_v, p_col, js_col, part):
        self.refs = kbuf, vbuf, q_v, kn_v, vn_v, p_col, js_col, part
        self.sub = lax.broadcasted_iota(jnp.int32, (GROUP, 128), 0)
        self.lane = lax.broadcasted_iota(jnp.int32, (GROUP, 128), 1)
        self.slot_c = jnp.where((self.lane // SLOTS) == (self.sub % 2), (self.lane % SLOTS).astype(F32) + off.astype(F32), FAR)
        self.pick = [(self.sub // 2) == cc for cc in range(4)]
        self.iotas = [(lax.broadcasted_iota(jnp.int32, (16, HEAD_DIM), 0) + 16 * t).astype(F32).astype(BF16) for t in range(SLOTS // 16)]

    def rows(self, base):
        kbuf, vbuf, q_v, kn_v, vn_v, p_col, js_col, part = self.refs
        pick, iotas, lane, slot_c = self.pick, self.iotas, self.lane, self.slot_c

        def hits_of(b):
            js = jnp.broadcast_to(js_col[pl.ds(b, 1), :], (16, 128)).astype(BF16)
            js = jnp.concatenate([js, js], axis=1)
            return [io == js for io in iotas]

        def refresh(buf, new_ref, r0):
            out = []
            for i in range(GROUP):
                b = r0 + i
                hits = hits_of(b)
                fresh = jnp.broadcast_to(new_ref[pl.ds(b, 1), :], (16, HEAD_DIM)).astype(BF16)
                for t in range(SLOTS // 16):
                    piece = jnp.where(hits[t], fresh, buf[b, pl.ds(16 * t, 16), :])
                    buf[b, pl.ds(16 * t, 16), :] = piece
                    out.append(piece)
            return jnp.concatenate(out, axis=0)

        def scores(r0):
            rows = pl.ds(r0, GROUP)
            q = jnp.concatenate([q_v[rows, h * HEAD_DIM:(h + 1) * HEAD_DIM] for h in range(HEADS)], axis=0).astype(BF16)
            s = lax.dot_general(q, refresh(kbuf, kn_v, r0), (((1,), (1,)), ((), ())), preferred_element_type=F32)
            out = []
            for h in range(HEADS):
                sh = s[h * GROUP:(h + 1) * GROUP, :]
                c = sh[:, 384:512]
                for cc in range(3):
                    c = jnp.where(pick[cc], sh[:, cc * 128:(cc + 1) * 128], c)
                out.append(c)
            return out

        def soften(r0, cs):
            valid = slot_c <= p_col[pl.ds(r0, GROUP), :]
            stats = jnp.zeros((GROUP, 128), F32)
            ps = []
            for h in range(HEADS):
                c = jnp.where(valid, cs[h], NEG_LARGE)
                m = jnp.max(c, axis=1, keepdims=True)
                e = jnp.where(valid, jnp.exp(c - m), 0.0)
                l = jnp.sum(e, axis=1, keepdims=True)
                stats = jnp.where(lane == h, m, stats)
                stats = jnp.where(lane == HEADS + h, l, stats)
                ps.append(e)
            part[pl.ds(r0, GROUP), QW:PW] = stats
            return ps

        def values(r0, ps):
            pm = jnp.concatenate([jnp.concatenate([jnp.where(pick[cc], e, 0.0) for cc in range(4)], axis=1) for e in ps], axis=0).astype(BF16)
            o = jnp.dot(pm, refresh(vbuf, vn_v, r0), preferred_element_type=F32)
            rows = pl.ds(r0, GROUP)
            for h in range(HEADS):
                part[rows, h * HEAD_DIM:(h + 1) * HEAD_DIM] = o[h * GROUP:(h + 1) * GROUP, :]

        starts = [al(base + g * GROUP, GROUP) for g in range(CHUNK // GROUP)]
        cs = [scores(r0) for r0 in starts]
        ps = [soften(r0, c) for r0, c in zip(starts, cs)]
        for r0, e in zip(starts, ps):
            values(r0, e)


def chunk_rows(c):
    return pl.ds(pl.multiple_of(c * CHUNK, CHUNK), CHUNK)


def step_kernel(pos_row, freq_ref, ns_ref, sp_hbm, x_hbm, wq_hbm, wk_hbm, wv_hbm, k_hbm, v_hbm,
                own, kbuf, vbuf, sp_out,
                x_v, wq_v, wk_v, wv_v, n_v, q_v, kn_v, vn_v, p_col, js_col, cos_v, sin_v,
                part, r0, r1, r2, w_sem, k_sem, v_sem, rsems):
    p = Places()
    barrier = pltpu.get_barrier_semaphore()
    for peer in (p.mate, p.x_peer, p.y_peer):
        pl.semaphore_signal(barrier, inc=1, device_id={'kv': peer}, device_id_type=pl.DeviceIdType.MESH)
    off = lax.axis_index('kv') * SLOTS
    weights = ((x_hbm, x_v), (wk_hbm, wk_v), (wv_hbm, wv_v), (wq_hbm, wq_v), (sp_hbm, sp_out))

    def w_in(n):
        return pltpu.make_async_copy(weights[n][0], weights[n][1], w_sem.at[n])

    def kv_in(c):
        return (pltpu.make_async_copy(k_hbm.at[chunk_rows(c)], kbuf.at[chunk_rows(c)], k_sem.at[c]),
                pltpu.make_async_copy(v_hbm.at[chunk_rows(c)], vbuf.at[chunk_rows(c)], v_sem.at[c]))

    for n in range(4):
        w_in(n).start()

    offf = off.astype(F32)

    @pl.loop(0, BATCH // 128)
    def _(t):
        rows = pl.ds(pl.multiple_of(t * 128, 128), 128)
        col = jnp.broadcast_to(pos_row[:, rows].astype(F32), (128, 128)).T
        p_col[rows, :] = col
        js = col - 512.0 * jnp.floor(col * (1.0 / 512.0)) - offf
        js_col[rows, :] = jnp.where((js >= 0.0) & (js < float(SLOTS)), js, -1.0)

    @pl.loop(0, BATCH // 64)
    def _(t):
        rows = pl.ds(pl.multiple_of(t * 64, 64), 64)
        s, c = sin_cos(p_col[rows, :] * freq_ref[...])
        lane = lax.broadcasted_iota(jnp.int32, (64, 128), 1)
        sin_v[rows, :] = jnp.where(lane < ROPE_HALF, -s, s)
        cos_v[rows, :] = c

    def rotate(t, rows):
        r = t[:, :ROPE_DIM]
        r = r * cos_v[rows, :] + pltpu.roll(r, ROPE_HALF, 1) * sin_v[rows, :]
        return jnp.concatenate([r, t[:, ROPE_DIM:]], axis=1)

    w_in(0).wait()
    for cp in kv_in(0):
        cp.start()
    gain = 1.0 + ns_ref[...].astype(F32).reshape(1, D_MODEL)

    @pl.loop(0, BATCH // 64)
    def _(i):
        rows = pl.ds(pl.multiple_of(i * 64, 64), 64)
        xf = x_v[rows, :].astype(F32)
        mean_sq = jnp.sum(xf * xf, axis=1, keepdims=True) * (1.0 / D_MODEL)
        n_v[rows, :] = (xf * lax.rsqrt(mean_sq + EPS) * gain).astype(BF16)

    for n in range(1, 4):
        w_in(n).wait()
    for c in range(1, AHEAD):
        for cp in kv_in(c):
            cp.start()
    red = Reduce(p, part, r0, r1, r2, own, [rsems.at[i] for i in range(6)])
    att = Attention(off, kbuf, vbuf, q_v, kn_v, vn_v, p_col, js_col, part)

    def attend(c):
        @pl.when(c + AHEAD < NCHUNK)
        def _():
            for cp in kv_in(c + AHEAD):
                cp.start()

        @pl.when(c == AHEAD)
        def _():
            w_in(4).start()

        @pl.when(c % (ROWS // CHUNK) == 0)
        def _():
            rows = pl.ds(al(c * CHUNK, ROWS), ROWS)
            kn_v[rows, :] = rotate(jnp.dot(n_v[rows, :], wk_v[...], preferred_element_type=F32), rows)
            vn_v[rows, :] = jnp.dot(n_v[rows, :], wv_v[...], preferred_element_type=F32)
            for h in range(HEADS):
                cols = pl.ds(h * HEAD_DIM, HEAD_DIM)
                qh = jnp.dot(n_v[rows, :], wq_v[:, cols], preferred_element_type=F32)
                q_v[rows, cols] = rotate(qh, rows) * SCORE_SCALE

        for cp in kv_in(c):
            cp.wait()
        att.rows(c * CHUNK)

        @pl.when(c == 0)
        def _():
            pl.semaphore_wait(barrier, 3)

        red.copy0(c).start()

    def pair_step(c):
        red.step0(c)
        red.copy1(c).start()

    def first_step(c):
        red.step1(c)
        red.copy2(c).start()

    lags = ((0, attend), (1, pair_step), (3, first_step), (5, red.step2))

    @pl.loop(0, NCHUNK + lags[-1][0])
    def _(i):
        for lag, body in lags:
            @pl.when((i >= lag) & (i < NCHUNK + lag))
            def _(lag=lag, body=body):
                body(i - lag)

    w_in(4).wait()
    p_all = pos_row[...]
    slot_ids = off + lax.broadcasted_iota(jnp.int32, (SLOTS, BATCH), 0)
    sp_out[...] = jnp.where(slot_ids == (p_all & 511), p_all, sp_out[...])

    @pl.loop(0, NCHUNK)
    def _(c):
        red.copy0(c).wait_send()
        red.drain(c)


def out_kernel(own, from_x, from_y, from_d, x_v, wo_v, b_ref, out_ref, g, lsem, ssem, rsem):
    p = Places()
    barrier = pltpu.get_barrier_semaphore()
    pl.semaphore_signal(barrier, inc=1, device_id={'kv': p.mate}, device_id_type=pl.DeviceIdType.MESH)
    refs = (own, from_x, from_y, from_d)

    def copy(n):
        return send(refs[n], g.at[n], ssem.at[n], rsem.at[n], p.mate)

    pl.semaphore_wait(barrier, 1)
    for n in range(4):
        copy(n).start()
    bias = b_ref[...].astype(F32).reshape(1, D_MODEL)

    def rows_of(n, t, core):
        x = p.x + (n % 2) * (1 - 2 * p.x)
        y = p.y + (n // 2) * (1 - 2 * p.y)
        a, b = (x, y) if t % 2 == 0 else (y, x)
        return al(t * CHUNK + 32 * core + 16 * a + 8 * b)

    def emit(n, ref, core):
        rows = [rows_of(n, t, core) for t in range(NCHUNK)]
        xin = jnp.concatenate([x_v[pl.ds(r, 8), :].astype(F32) for r in rows], axis=0)
        y = xin + jnp.dot(ref[...].astype(BF16), wo_v[...], preferred_element_type=F32) + bias
        for t, r in enumerate(rows):
            out_ref[pl.ds(r, 8), :] = y[8 * t:8 * t + 8, :]

    for n in range(4):
        emit(n, refs[n], p.core)
    for n in range(4):
        copy(n).wait_recv()
        emit(n, g.at[n], 1 - p.core)
    for n in range(4):
        copy(n).wait_send()


def solution(mesh):
    row_spec = P('dp', None)
    cache_spec = P('dp', 'kv', None)
    slot_spec = P('dp', 'kv')
    vec_spec = P(None)
    mat_spec = P(None, None)
    hbm = pl.BlockSpec(memory_space=pltpu.HBM)
    vmem = pl.BlockSpec(memory_space=pltpu.VMEM)

    def in_hbm(a):
        return pltpu.with_memory_space_constraint(a, pltpu.HBM)

    def local_step(x_in, positions, k_cache, v_cache, slot_pos, norm_scale, w_q, w_k, w_v, w_o, b_o):
        own, k_out, v_out, sp_t = pl.pallas_call(
            step_kernel,
            out_shape=(jax.ShapeDtypeStruct((BATCH // 8, QW), F32),
                       pltpu.VMEM((BATCH, SLOTS, HEAD_DIM), BF16),
                       pltpu.VMEM((BATCH, SLOTS, HEAD_DIM), BF16),
                       pltpu.VMEM((SLOTS, BATCH), jnp.int32)),
            in_specs=[vmem, vmem, vmem] + [hbm] * 7,
            out_specs=(vmem,) * 4,
            scratch_shapes=[
                pltpu.VMEM((BATCH, D_MODEL), BF16),
                pltpu.VMEM((D_MODEL, QW), BF16),
                pltpu.VMEM((D_MODEL, HEAD_DIM), BF16),
                pltpu.VMEM((D_MODEL, HEAD_DIM), BF16),
                pltpu.VMEM((BATCH, D_MODEL), BF16),
                pltpu.VMEM((BATCH, QW), F32),
                pltpu.VMEM((BATCH, HEAD_DIM), F32),
                pltpu.VMEM((BATCH, HEAD_DIM), F32),
                pltpu.VMEM((BATCH, 128), F32),
                pltpu.VMEM((BATCH, 128), F32),
                pltpu.VMEM((BATCH, 128), F32),
                pltpu.VMEM((BATCH, 128), F32),
                pltpu.VMEM((BATCH, PW), F32),
                pltpu.VMEM((NCHUNK * 32, PW), F32),
                pltpu.VMEM((NCHUNK * 16, PW), F32),
                pltpu.VMEM((NCHUNK * 8, PW), F32),
                pltpu.SemaphoreType.DMA((5,)),
                pltpu.SemaphoreType.DMA((NCHUNK,)),
                pltpu.SemaphoreType.DMA((NCHUNK,)),
                pltpu.SemaphoreType.DMA((6, NCHUNK)),
            ],
            cost_estimate=pl.CostEstimate(flops=30_000_000_000, bytes_accessed=40_000_000, transcendentals=200_000),
            compiler_params=pltpu.CompilerParams(collective_id=0, has_side_effects=True, vmem_limit_bytes=20 * 1024 * 1024),
        )(positions.reshape(1, BATCH), jnp.asarray(inv_freq_row()), norm_scale,
          *[in_hbm(a) for a in (slot_pos.T, x_in, w_q, w_k, w_v, k_cache, v_cache)])
        far = [lax.ppermute(own, 'kv', [(i, i ^ m) for i in range(8)]) for m in (2, 4, 6)]
        x_out = pl.pallas_call(
            out_kernel,
            out_shape=jax.ShapeDtypeStruct((BATCH, D_MODEL), F32),
            in_specs=[vmem] * 7,
            out_specs=vmem,
            scratch_shapes=[
                pltpu.VMEM((4, BATCH // 8, QW), F32),
                pltpu.SemaphoreType.DMA,
                pltpu.SemaphoreType.DMA((4,)),
                pltpu.SemaphoreType.DMA((4,)),
            ],
            cost_estimate=pl.CostEstimate(flops=1_200_000_000, bytes_accessed=6_000_000, transcendentals=0),
            compiler_params=pltpu.CompilerParams(collective_id=1, has_side_effects=True, vmem_limit_bytes=20 * 1024 * 1024),
        )(own, *far, x_in, w_o, b_o)
        return x_out.astype(BF16), k_out, v_out, sp_t.T

    return jax.shard_map(
        local_step,
        mesh=mesh,
        in_specs=(row_spec, P('dp'), cache_spec, cache_spec, slot_spec, vec_spec, mat_spec, mat_spec, mat_spec, mat_spec, vec_spec),
        out_specs=(row_spec, cache_spec, cache_spec, slot_spec),
        check_vma=False)
```

time: 58 us -> 54.5 us (0.940)
  Pallas kernels: 47.7 us -> 33.4 us
  local copies, waits for them, and re-layouts: 9.51 us -> 15.7 us
  starting transfers between devices: 0 us -> 3.51 us
  other arithmetic: 0 us -> 1.14 us
    pallas_call x2, Pallas kernels: 47.7 us -> 33.4 us  [the longest x1 29.3 us: local_step(): pl.pallas_call(step_kernel, out_shape=(jax.ShapeDtypeStruct((BATCH // 8,...]
    unnamed x13 -> x15, local copies, waits for them, and re-layouts: 3.04 us -> 15.7 us
    dynamic_update_slice x1 -> x0, local copies, waits for them, and re-layouts: 6.46 us -> none  [local_step(): v_out = lax.dynamic_update_slice(v_mid, v_new, (SPLIT, 0, 0))]
    ppermute x0 -> x3, starting transfers between devices: none -> 3.51 us  [local_step(): lax.ppermute(own, 'kv', [(i, i ^ m) for i in range(8)])]
    convert_element_type x0 -> x1, other arithmetic: none -> 1.14 us  [local_step(): return (x_out.astype(BF16), k_out, v_out, sp_t.T)]
  transfers between devices with their start and end apart: 0 -> 3, of which waited for: 0 -> 0; matrix products, arithmetic and copies ran while one was open for 0% -> 25% of each run, Pallas kernels for 0% -> 0%
where the time goes in v7:
time: 54.5 us; the launch traced here: 54.4 us
  Pallas kernels  33.4 us (61%)
  local copies, waits for them, and re-layouts  15.7 us (29%)
  starting transfers between devices  3.51 us (6%)
  other arithmetic  1.14 us (2%)
  between operations  0.69 us (1%)
    pallas_call x1, Pallas kernels, local_step(): pl.pallas_call(step_kernel, out_shape=(jax.ShapeDtypeStruct((BATCH // 8,...  29.3 us
    unnamed x15, local copies, waits for them, and re-layouts  15.7 us
    pallas_call x1, Pallas kernels, local_step(): pl.pallas_call(out_kernel, out_shape=jax.ShapeDtypeStruct((BATCH, D_MODEL...  4.08 us
    ppermute x3, starting transfers between devices, local_step(): lax.ppermute(own, 'kv', [(i, i ^ m) for i in range(8)])  3.51 us
    convert_element_type x1, other arithmetic, local_step(): return (x_out.astype(BF16), k_out, v_out, sp_t.T)  1.14 us
  transfers between devices with their start and end apart: 3, of which 0 were waited for; matrix products, arithmetic and copies ran while one was open for 25% of the time, Pallas kernels for 0%

profile of v7, /device:TPU:0, one launch (start us, length us, event | category | flops | bytes accessed | tf_op | source)
XLA Modules:
  0.0 54.4 jit_solution(15305760111082953927)
XLA Ops:
  0.6 0.0 copy-start.3
  0.6 0.7 %copy-done.3 = bf16[1152]{0:T(1024)(128)(2,1)S(1)} copy-done((bf16[1152]{0:T(1024)(128)(2,1)S(1)}, bf16[1152]{0:T(1024)(128)(2,1)}, u32[]{:S(2)}) %copy-start.3) | copy-done | bytes 2328
  1.3 0.0 copy-start.4
  1.3 0.7 %copy-done.4 = s32[512]{0:T(512)S(1)} copy-done((s32[512]{0:T(512)S(1)}, s32[512]{0:T(512)}, u32[]{:S(2)}) %copy-start.4) | copy-done | bytes 2072
  2.0 0.0 copy-start.5
  2.0 0.7 %copy-done.5 = f32[1,128]{1,0:T(1,128)S(1)} copy-done((f32[1,128]{1,0:T(1,128)S(1)}, f32[1,128]{1,0:T(1,128)}, u32[]{:S(2)}) %copy-start.5) | copy-done | bytes 536
  2.7 29.3 %shard_map.147 = (f32[64,1024]{1,0:T(8,128)S(1)}, bf16[512,64,256]{2,1,0:T(8,128)(2,1)S(1)}, bf16[512,64,256]{2,1,0:T(8,128)(2,1)S(1)}, s32[64,512]{1,0:T(8,128)S(1)}) custom-call(s32[1,512]{1,0:T(1,128)S(1)} %bitcast.4, f32[1,128]{1,0:T(1,128)S(1)} %copy-done.5, bf16[1152]{0:T(1024)(128)(2,1)S(1)} %copy-done.3, s32[64,512]{1,0:T(8,128)} %bitcast.5, ...), custom_call_target="tpu_custom_call" | custom-call | flops 30000001024 | bytes 40000000 | tf_op jit(solution)/shard_map/pallas_call | solution.py:404
  31.9 1.4 %collective-permute-start.2 = (f32[64,1024]{1,0:T(8,128)S(1)}, f32[64,1024]{1,0:T(8,128)S(1)}, u32[]{:S(2)}, u32[]{:S(2)}) collective-permute-start(f32[64,1024]{1,0:T(8,128)S(1)} %get-tuple-element.8.own), channel_id=1, source_target_pairs={{0,6},{1,7},{2,4},{3,5},{4,2},{5,3},{6,0},{7,1}} | collective-permute-start | bytes 786440 | tf_op jit(solution)/shard_map/ppermute | solution.py:438
  33.3 1.2 %collective-permute-start.1 = (f32[64,1024]{1,0:T(8,128)S(1)}, f32[64,1024]{1,0:T(8,128)S(1)}, u32[]{:S(2)}, u32[]{:S(2)}) collective-permute-start(f32[64,1024]{1,0:T(8,128)S(1)} %get-tuple-element.8.own), channel_id=1, source_target_pairs={{0,4},{1,5},{2,6},{3,7},{4,0},{5,1},{6,2},{7,3}} | collective-permute-start | bytes 786440 | tf_op jit(solution)/shard_map/ppermute | solution.py:438
  34.5 1.0 %collective-permute-start = (f32[64,1024]{1,0:T(8,128)S(1)}, f32[64,1024]{1,0:T(8,128)S(1)}, u32[]{:S(2)}, u32[]{:S(2)}) collective-permute-start(f32[64,1024]{1,0:T(8,128)S(1)} %get-tuple-element.8.own), channel_id=1, source_target_pairs={{0,2},{1,3},{2,0},{3,1},{4,6},{5,7},{6,4},{7,5}} | collective-permute-start | bytes 786440 | tf_op jit(solution)/shard_map/ppermute | solution.py:438
  35.5 6.2 %copy.19 = bf16[512,64,256]{2,1,0:T(8,128)(2,1)} copy(bf16[512,64,256]{2,1,0:T(8,128)(2,1)S(1)} %get-tuple-element.13) | data formatting | bytes 33554432
  41.6 0.7 %copy.21 = s32[512,64]{0,1:T(8,128)} copy(s32[512,64]{0,1:T(8,128)S(1)} %bitcast.3) | data formatting | bytes 262144
  42.3 0.0 copy-start
  42.3 0.0 copy-start.1
  42.3 0.0 copy-start.2
  42.3 6.8 %copy.20 = bf16[512,64,256]{2,1,0:T(8,128)(2,1)} copy(bf16[512,64,256]{2,1,0:T(8,128)(2,1)S(1)} %get-tuple-element.14) | data formatting | bytes 33554432
  49.1 0.0 collective-permute-done.2.from_d
  49.1 0.0 collective-permute-done.1.from_y
  49.1 0.0 collective-permute-done.from_x
  49.1 0.0 copy-done
  49.1 0.0 copy-done.1
  49.1 0.0 copy-done.2
  49.1 4.1 %shard_map.148 = f32[512,1152]{1,0:T(8,128)S(1)} custom-call(f32[64,1024]{1,0:T(8,128)S(1)} %get-tuple-element.8.own, f32[64,1024]{1,0:T(8,128)S(1)} %collective-permute-done.from_x, f32[64,1024]{1,0:T(8,128)S(1)} %collective-permute-done.1.from_y, f32[64,1024]{1,0:T(8,128)S(1)} %collective-permute-done.2.from_d, bf16[512,1152]{1,0:T(8,128)(2,1)S(1)} %copy-done.1, ...), custom_call_target="tpu_custom_call" | custom-call | flops 1200000000 | bytes 6000000 | tf_op jit(solution)/shard_map/pallas_call | solution.py:439
  53.2 1.1 %convert_element_type.3 = bf16[512,1152]{1,0:T(8,128)(2,1)} convert(f32[512,1152]{1,0:T(8,128)S(1)} %shard_map.148) | non-fusion elementwise | flops 589824 | bytes 3538944 | tf_op jit(solution)/shard_map/convert_element_type | solution.py:453
Async XLA Ops:
  0.6 0.7 %copy-start.3 = (bf16[1152]{0:T(1024)(128)(2,1)S(1)}, bf16[1152]{0:T(1024)(128)(2,1)}, u32[]{:S(2)}) copy-start(bf16[1152]{0:T(1024)(128)(2,1)} %ns_ref.1) | copy-start | bytes 6916
  1.3 0.7 %copy-start.4 = (s32[512]{0:T(512)S(1)}, s32[512]{0:T(512)}, u32[]{:S(2)}) copy-start(s32[512]{0:T(512)} %param.13) | copy-start | bytes 6148
  2.0 0.7 %copy-start.5 = (f32[1,128]{1,0:T(1,128)S(1)}, f32[1,128]{1,0:T(1,128)}, u32[]{:S(2)}) copy-start(f32[1,128]{1,0:T(1,128)} %constant.2.clone.freq_ref) | copy-start | bytes 1540
  31.9 17.2 %collective-permute-start.2 = (f32[64,1024]{1,0:T(8,128)S(1)}, f32[64,1024]{1,0:T(8,128)S(1)}, u32[]{:S(2)}, u32[]{:S(2)}) collective-permute-start(f32[64,1024]{1,0:T(8,128)S(1)} %get-tuple-element.8.own), channel_id=1, source_target_pairs={{0,6},{1,7},{2,4},{3,5},{4,2},{5,3},{6,0},{7,1}} | collective-permute-start | bytes 786440 | tf_op jit(solution)/shard_map/ppermute | solution.py:438
  33.3 15.8 %collective-permute-start.1 = (f32[64,1024]{1,0:T(8,128)S(1)}, f32[64,1024]{1,0:T(8,128)S(1)}, u32[]{:S(2)}, u32[]{:S(2)}) collective-permute-start(f32[64,1024]{1,0:T(8,128)S(1)} %get-tuple-element.8.own), channel_id=1, source_target_pairs={{0,4},{1,5},{2,6},{3,7},{4,0},{5,1},{6,2},{7,3}} | collective-permute-start | bytes 786440 | tf_op jit(solution)/shard_map/ppermute | solution.py:438
  34.5 14.6 %collective-permute-start = (f32[64,1024]{1,0:T(8,128)S(1)}, f32[64,1024]{1,0:T(8,128)S(1)}, u32[]{:S(2)}, u32[]{:S(2)}) collective-permute-start(f32[64,1024]{1,0:T(8,128)S(1)} %get-tuple-element.8.own), channel_id=1, source_target_pairs={{0,2},{1,3},{2,0},{3,1},{4,6},{5,7},{6,4},{7,5}} | collective-permute-start | bytes 786440 | tf_op jit(solution)/shard_map/ppermute | solution.py:438
  42.3 6.9 %copy-start = (bf16[1024,1152]{1,0:T(8,128)(2,1)S(1)}, bf16[1024,1152]{1,0:T(8,128)(2,1)}, u32[]{:S(2)}) copy-start(bf16[1024,1152]{1,0:T(8,128)(2,1)} %wo_v.1) | copy-start | bytes 7077892
  42.3 6.9 %copy-start.1 = (bf16[512,1152]{1,0:T(8,128)(2,1)S(1)}, bf16[512,1152]{1,0:T(8,128)(2,1)}, u32[]{:S(2)}) copy-start(bf16[512,1152]{1,0:T(8,128)(2,1)} %x_v.1) | copy-start | bytes 3538948
  42.3 6.9 %copy-start.2 = (bf16[1152]{0:T(1024)(128)(2,1)S(1)}, bf16[1152]{0:T(1024)(128)(2,1)}, u32[]{:S(2)}) copy-start(bf16[1152]{0:T(1024)(128)(2,1)} %b_ref.1) | copy-start | bytes 6916

commit v8 on v7

--- a/solution.py
+++ b/solution.py
@@ -55,21 +55,18 @@
     return (ROPE_BASE ** (-i / ROPE_HALF)).astype(np.float32).reshape(1, ROPE_DIM)
 
 
-def merge_rows(a_rows, b_rows):
-    sa, sb = a_rows[1], b_rows[1]
-    lane = lax.broadcasted_iota(jnp.int32, sa.shape, 1)
-    ma, mb = sa, sb
-    mm = jnp.maximum(ma, mb)
-    fa, fb = jnp.exp(ma - mm), jnp.exp(mb - mm)
-    fa_l = pltpu.roll(fa, HEADS, 1)
-    fb_l = pltpu.roll(fb, HEADS, 1)
-    stats = jnp.where(lane < HEADS, mm, sa * fa_l + sb * fb_l)
+def merge_rows(blocks):
+    stats = [t[:, QW:] for t in blocks]
+    lane = lax.broadcasted_iota(jnp.int32, stats[0].shape, 1)
+    top = functools.reduce(jnp.maximum, stats)
+    factors = [jnp.exp(t - top) for t in stats]
+    sums = [t * pltpu.roll(f, HEADS, 1) for t, f in zip(stats, factors)]
+    out = jnp.where(lane < HEADS, top, functools.reduce(jnp.add, sums))
     vals = []
     for h in range(HEADS):
-        va = a_rows[0][:, h * HEAD_DIM:(h + 1) * HEAD_DIM]
-        vb = b_rows[0][:, h * HEAD_DIM:(h + 1) * HEAD_DIM]
-        vals.append(va * fa[:, h:h + 1] + vb * fb[:, h:h + 1])
-    return jnp.concatenate(vals, axis=1), stats
+        terms = [t[:, h * HEAD_DIM:(h + 1) * HEAD_DIM] * f[:, h:h + 1] for t, f in zip(blocks, factors)]
+        vals.append(functools.reduce(jnp.add, terms))
+    return jnp.concatenate(vals, axis=1), out
 
 
 def normalise(v, s):
@@ -84,16 +81,19 @@
         self.x = (me // 2) % 2
         self.y = me // 4
         self.mate = me + 1 - 2 * self.core
-        self.x_peer = me + 2 - 4 * self.x
-        self.y_peer = me + 4 - 8 * self.y
-
-    def first(self, c):
-        odd = c % 2
-        return self.x_peer + odd * (self.y_peer - self.x_peer), self.x + odd * (self.y - self.x)
-
-    def second(self, c):
-        odd = c % 2
-        return self.y_peer + odd * (self.x_peer - self.y_peer), self.y + odd * (self.x - self.y)
+
+    def flip(self, m):
+        x = self.x + (m % 2) * (1 - 2 * self.x)
+        y = self.y + (m // 2) * (1 - 2 * self.y)
+        return x, y
+
+    def peer(self, m):
+        x, y = self.flip(m)
+        return y * 4 + x * 2 + self.core
+
+    def eighth(self, m, core):
+        x, y = self.flip(m)
+        return 32 * core + 16 * x + 8 * y
 
 
 def send(src, dst, ss, rs, peer):
@@ -106,52 +106,38 @@
 
 
 class Reduce:
-    def __init__(self, places, part, r0, r1, r2, own, sems):
+    def __init__(self, places, part, r0, r1, own, s0, s1):
         self.p = places
-        self.part, self.r0, self.r1, self.r2, self.own = part, r0, r1, r2, own
-        self.s0s, self.s0r, self.s1s, self.s1r, self.s2s, self.s2r = sems
-
-    def copy0(self, c):
+        self.part, self.r0, self.r1, self.own, self.s0, self.s1 = part, r0, r1, own, s0, s1
+
+    def pair_copy(self, c):
         src = al(c * CHUNK + 32 * (1 - self.p.core))
-        return send(self.part.at[pl.ds(src, 32)], self.r0.at[pl.ds(al(c * 32), 32)], self.s0s.at[c], self.s0r.at[c], self.p.mate)
-
-    def copy1(self, c):
-        peer, k = self.p.first(c)
-        src = al(c * CHUNK + 32 * self.p.core + 16 * (1 - k))
-        return send(self.part.at[pl.ds(src, 16)], self.r1.at[pl.ds(al(c * 16), 16)], self.s1s.at[c], self.s1r.at[c], peer)
-
-    def copy2(self, c):
-        peer, k2 = self.p.second(c)
-        k1 = self.p.first(c)[1]
-        src = al(c * CHUNK + 32 * self.p.core + 16 * k1 + 8 * (1 - k2))
-        return send(self.part.at[pl.ds(src, 8)], self.r2.at[pl.ds(al(c * 8), 8)], self.s2s.at[c], self.s2r.at[c], peer)
-
-    def merge(self, mine, other_ref, theirs, n):
-        a = self.part[pl.ds(mine, n), :]
-        b = other_ref[pl.ds(theirs, n), :]
-        return merge_rows((a[:, :QW], a[:, QW:]), (b[:, :QW], b[:, QW:]))
-
-    def step0(self, c):
-        self.copy0(c).wait_recv()
-        base = al(c * CHUNK + 32 * self.p.core)
-        v, s = self.merge(base, self.r0, al(c * 32), 32)
-        self.part[pl.ds(base, 32), :] = jnp.concatenate([v, s], axis=1)
-
-    def step1(self, c):
-        self.copy1(c).wait_recv()
-        base = al(c * CHUNK + 32 * self.p.core + 16 * self.p.first(c)[1])
-        v, s = self.merge(base, self.r1, al(c * 16), 16)
-        self.part[pl.ds(base, 16), :] = jnp.concatenate([v, s], axis=1)
-
-    def step2(self, c):
-        self.copy2(c).wait_recv()
-        base = al(c * CHUNK + 32 * self.p.core + 16 * self.p.first(c)[1] + 8 * self.p.second(c)[1])
-        v, s = self.merge(base, self.r2, al(c * 8), 8)
+        return send(self.part.at[pl.ds(src, 32)], self.r0.at[pl.ds(al(c * 32), 32)], self.s0.at[0, c], self.s0.at[1, c], self.p.mate)
+
+    def chip_copies(self, c):
+        return [send(self.part.at[pl.ds(al(c * CHUNK + self.p.eighth(m, self.p.core)), 8)],
+                     self.r1.at[pl.ds(al(c * 24 + 8 * (m - 1)), 8)],
+                     self.s1.at[0, 3 * c + m - 1], self.s1.at[1, 3 * c + m - 1], self.p.peer(m)) for m in (3, 1, 2)]
+
+    def pair_step(self, c):
+        self.pair_copy(c).wait_recv()
+        rows = pl.ds(al(c * CHUNK + 32 * self.p.core), 32)
+        v, s = merge_rows([self.part[rows, :], self.r0[pl.ds(al(c * 32), 32), :]])
+        self.part[rows, :] = jnp.concatenate([v, s], axis=1)
+        for cp in self.chip_copies(c):
+            cp.start()
+
+    def chip_step(self, c):
+        for cp in self.chip_copies(c):
+            cp.wait_recv()
+        mine = self.part[pl.ds(al(c * CHUNK + self.p.eighth(0, self.p.core)), 8), :]
+        v, s = merge_rows([mine] + [self.r1[pl.ds(al(c * 24 + 8 * n), 8), :] for n in range(3)])
         self.own[pl.ds(al(c * 8), 8), :] = normalise(v, s)
 
     def drain(self, c):
-        self.copy1(c).wait_send()
-        self.copy2(c).wait_send()
+        self.pair_copy(c).wait_send()
+        for cp in self.chip_copies(c):
+            cp.wait_send()
 
 
 class Attention:
@@ -230,16 +216,17 @@
     return pl.ds(pl.multiple_of(c * CHUNK, CHUNK), CHUNK)
 
 
-def step_kernel(pos_row, freq_ref, ns_ref, sp_hbm, x_hbm, wq_hbm, wk_hbm, wv_hbm, k_hbm, v_hbm,
+def step_kernel(pos_hbm, freq_hbm, ns_hbm, sp_hbm, x_hbm, wq_hbm, wk_hbm, wv_hbm, k_hbm, v_hbm,
                 own, kbuf, vbuf, sp_out,
                 x_v, wq_v, wk_v, wv_v, n_v, q_v, kn_v, vn_v, p_col, js_col, cos_v, sin_v,
-                part, r0, r1, r2, w_sem, k_sem, v_sem, rsems):
+                part, r0, r1, pos_row, freq_ref, ns_ref, w_sem, k_sem, v_sem, s0, s1):
     p = Places()
     barrier = pltpu.get_barrier_semaphore()
-    for peer in (p.mate, p.x_peer, p.y_peer):
+    for peer in (p.mate, p.peer(1), p.peer(2), p.peer(3)):
         pl.semaphore_signal(barrier, inc=1, device_id={'kv': peer}, device_id_type=pl.DeviceIdType.MESH)
     off = lax.axis_index('kv') * SLOTS
-    weights = ((x_hbm, x_v), (wk_hbm, wk_v), (wv_hbm, wv_v), (wq_hbm, wq_v), (sp_hbm, sp_out))
+    weights = ((x_hbm, x_v), (wk_hbm, wk_v), (wv_hbm, wv_v), (wq_hbm, wq_v), (sp_hbm, sp_out),
+               (pos_hbm, pos_row), (freq_hbm, freq_ref), (ns_hbm, ns_ref))
 
     def w_in(n):
         return pltpu.make_async_copy(weights[n][0], weights[n][1], w_sem.at[n])
@@ -248,8 +235,10 @@
         return (pltpu.make_async_copy(k_hbm.at[chunk_rows(c)], kbuf.at[chunk_rows(c)], k_sem.at[c]),
                 pltpu.make_async_copy(v_hbm.at[chunk_rows(c)], vbuf.at[chunk_rows(c)], v_sem.at[c]))
 
-    for n in range(4):
+    for n in (5, 6, 7, 0, 1, 2, 3):
         w_in(n).start()
+    for n in (5, 6, 7):
+        w_in(n).wait()
 
     offf = off.astype(F32)
 
@@ -291,7 +280,7 @@
     for c in range(1, AHEAD):
         for cp in kv_in(c):
             cp.start()
-    red = Reduce(p, part, r0, r1, r2, own, [rsems.at[i] for i in range(6)])
+    red = Reduce(p, part, r0, r1, own, s0, s1)
     att = Attention(off, kbuf, vbuf, q_v, kn_v, vn_v, p_col, js_col, part)
 
     def attend(c):
@@ -320,19 +309,11 @@
 
         @pl.when(c == 0)
         def _():
-            pl.semaphore_wait(barrier, 3)
-
-        red.copy0(c).start()
-
-    def pair_step(c):
-        red.step0(c)
-        red.copy1(c).start()
-
-    def first_step(c):
-        red.step1(c)
-        red.copy2(c).start()
-
-    lags = ((0, attend), (1, pair_step), (3, first_step), (5, red.step2))
+            pl.semaphore_wait(barrier, 4)
+
+        red.pair_copy(c).start()
+
+    lags = ((0, attend), (1, red.pair_step), (4, red.chip_step))
 
     @pl.loop(0, NCHUNK + lags[-1][0])
     def _(i):
@@ -348,7 +329,6 @@
 
     @pl.loop(0, NCHUNK)
     def _(c):
-        red.copy0(c).wait_send()
         red.drain(c)
 
 
@@ -366,24 +346,18 @@
         copy(n).start()
     bias = b_ref[...].astype(F32).reshape(1, D_MODEL)
 
-    def rows_of(n, t, core):
-        x = p.x + (n % 2) * (1 - 2 * p.x)
-        y = p.y + (n // 2) * (1 - 2 * p.y)
-        a, b = (x, y) if t % 2 == 0 else (y, x)
-        return al(t * CHUNK + 32 * core + 16 * a + 8 * b)
-
-    def emit(n, ref, core):
-        rows = [rows_of(n, t, core) for t in range(NCHUNK)]
+    def emit(blocks, core):
+        rows = [al(t * CHUNK + p.eighth(n, core)) for n in range(4) for t in range(NCHUNK)]
+        o = jnp.concatenate([t[...].astype(BF16) for t in blocks], axis=0)
         xin = jnp.concatenate([x_v[pl.ds(r, 8), :].astype(F32) for r in rows], axis=0)
-        y = xin + jnp.dot(ref[...].astype(BF16), wo_v[...], preferred_element_type=F32) + bias
+        y = xin + jnp.dot(o, wo_v[...], preferred_element_type=F32) + bias
         for t, r in enumerate(rows):
             out_ref[pl.ds(r, 8), :] = y[8 * t:8 * t + 8, :]
 
-    for n in range(4):
-        emit(n, refs[n], p.core)
+    emit(refs, p.core)
     for n in range(4):
         copy(n).wait_recv()
-        emit(n, g.at[n], 1 - p.core)
+    emit([g.at[n] for n in range(4)], 1 - p.core)
     for n in range(4):
         copy(n).wait_send()
 
@@ -407,7 +381,7 @@
                        pltpu.VMEM((BATCH, SLOTS, HEAD_DIM), BF16),
                        pltpu.VMEM((BATCH, SLOTS, HEAD_DIM), BF16),
                        pltpu.VMEM((SLOTS, BATCH), jnp.int32)),
-            in_specs=[vmem, vmem, vmem] + [hbm] * 7,
+            in_specs=[hbm] * 10,
             out_specs=(vmem,) * 4,
             scratch_shapes=[
                 pltpu.VMEM((BATCH, D_MODEL), BF16),
@@ -424,17 +398,19 @@
                 pltpu.VMEM((BATCH, 128), F32),
                 pltpu.VMEM((BATCH, PW), F32),
                 pltpu.VMEM((NCHUNK * 32, PW), F32),
-                pltpu.VMEM((NCHUNK * 16, PW), F32),
-                pltpu.VMEM((NCHUNK * 8, PW), F32),
-                pltpu.SemaphoreType.DMA((5,)),
+                pltpu.VMEM((NCHUNK * 24, PW), F32),
+                pltpu.VMEM((1, BATCH), jnp.int32),
+                pltpu.VMEM((1, ROPE_DIM), F32),
+                pltpu.VMEM((D_MODEL,), BF16),
+                pltpu.SemaphoreType.DMA((8,)),
                 pltpu.SemaphoreType.DMA((NCHUNK,)),
                 pltpu.SemaphoreType.DMA((NCHUNK,)),
-                pltpu.SemaphoreType.DMA((6, NCHUNK)),
+                pltpu.SemaphoreType.DMA((2, NCHUNK)),
+                pltpu.SemaphoreType.DMA((2, 3 * NCHUNK)),
             ],
             cost_estimate=pl.CostEstimate(flops=30_000_000_000, bytes_accessed=40_000_000, transcendentals=200_000),
             compiler_params=pltpu.CompilerParams(collective_id=0, has_side_effects=True, vmem_limit_bytes=20 * 1024 * 1024),
-        )(positions.reshape(1, BATCH), jnp.asarray(inv_freq_row()), norm_scale,
-          *[in_hbm(a) for a in (slot_pos.T, x_in, w_q, w_k, w_v, k_cache, v_cache)])
+        )(*[in_hbm(a) for a in (positions.reshape(1, BATCH), jnp.asarray(inv_freq_row()), norm_scale, slot_pos.T, x_in, w_q, w_k, w_v, k_cache, v_cache)])
         far = [lax.ppermute(own, 'kv', [(i, i ^ m) for i in range(8)]) for m in (2, 4, 6)]
         x_out = pl.pallas_call(
             out_kernel,

time: 54.5 us -> 48.3 us (0.89)
  Pallas kernels: 33.4 us -> 29.2 us
  local copies, waits for them, and re-layouts: 15.7 us -> 13.7 us
    pallas_call x1, Pallas kernels: 29.3 us -> 25.5 us  [local_step(): pl.pallas_call(step_kernel, out_shape=(jax.ShapeDtypeStruct((BATCH // 8,...]
    unnamed x15 -> x9, local copies, waits for them, and re-layouts: 15.7 us -> 13.7 us
  transfers between devices with their start and end apart: 3 -> 3, of which waited for: 0 -> 0; matrix products, arithmetic and copies ran while one was open for 25% -> 28% of each run, Pallas kernels for 0% -> 0%
where the time goes in v8:
time: 48.3 us; the launch traced here: 48.2 us
  Pallas kernels  29.2 us (60%)
  local copies, waits for them, and re-layouts  13.7 us (28%)
  starting transfers between devices  3.51 us (7%)
  other arithmetic  1.14 us (2%)
  between operations  0.68 us (1%)
    pallas_call x1, Pallas kernels, local_step(): pl.pallas_call(step_kernel, out_shape=(jax.ShapeDtypeStruct((BATCH // 8,...  25.5 us
    unnamed x9, local copies, waits for them, and re-layouts  13.7 us
    pallas_call x1, Pallas kernels, local_step(): pl.pallas_call(out_kernel, out_shape=jax.ShapeDtypeStruct((BATCH, D_MODEL...  3.65 us
    ppermute x3, starting transfers between devices, local_step(): lax.ppermute(own, 'kv', [(i, i ^ m) for i in range(8)])  3.51 us
    convert_element_type x1, other arithmetic, local_step(): return (x_out.astype(BF16), k_out, v_out, sp_t.T)  1.14 us
  transfers between devices with their start and end apart: 3, of which 0 were waited for; matrix products, arithmetic and copies ran while one was open for 28% of the time, Pallas kernels for 0%

profile of v8, /device:TPU:0, one launch (start us, length us, event | category | flops | bytes accessed | tf_op | source)
XLA Modules:
  0.0 48.2 jit_solution(7643995281676752412)
XLA Ops:
  0.6 25.5 %shard_map.147 = (f32[64,1024]{1,0:T(8,128)S(1)}, bf16[512,64,256]{2,1,0:T(8,128)(2,1)S(1)}, bf16[512,64,256]{2,1,0:T(8,128)(2,1)S(1)}, s32[64,512]{1,0:T(8,128)S(1)}) custom-call(s32[1,512]{1,0:T(1,128)} %bitcast.5, f32[1,128]{1,0:T(1,128)} %constant.2.clone.freq_hbm, bf16[1152]{0:T(1024)(128)(2,1)} %ns_hbm.1, s32[64,512]{1,0:T(8,128)} %bitcast.4, ...), custom_call_target="tpu_custom_call" | custom-call | flops 30000001024 | bytes 40000000 | tf_op jit(solution)/shard_map/pallas_call | solution.py:378
  26.2 1.0 %collective-permute-start.2 = (f32[64,1024]{1,0:T(8,128)S(1)}, f32[64,1024]{1,0:T(8,128)S(1)}, u32[]{:S(2)}, u32[]{:S(2)}) collective-permute-start(f32[64,1024]{1,0:T(8,128)S(1)} %get-tuple-element.8.own), channel_id=1, source_target_pairs={{0,6},{1,7},{2,4},{3,5},{4,2},{5,3},{6,0},{7,1}} | collective-permute-start | bytes 786440 | tf_op jit(solution)/shard_map/ppermute | solution.py:414
  27.2 1.5 %collective-permute-start.1 = (f32[64,1024]{1,0:T(8,128)S(1)}, f32[64,1024]{1,0:T(8,128)S(1)}, u32[]{:S(2)}, u32[]{:S(2)}) collective-permute-start(f32[64,1024]{1,0:T(8,128)S(1)} %get-tuple-element.8.own), channel_id=1, source_target_pairs={{0,4},{1,5},{2,6},{3,7},{4,0},{5,1},{6,2},{7,3}} | collective-permute-start | bytes 786440 | tf_op jit(solution)/shard_map/ppermute | solution.py:414
  28.8 0.9 %collective-permute-start = (f32[64,1024]{1,0:T(8,128)S(1)}, f32[64,1024]{1,0:T(8,128)S(1)}, u32[]{:S(2)}, u32[]{:S(2)}) collective-permute-start(f32[64,1024]{1,0:T(8,128)S(1)} %get-tuple-element.8.own), channel_id=1, source_target_pairs={{0,2},{1,3},{2,0},{3,1},{4,6},{5,7},{6,4},{7,5}} | collective-permute-start | bytes 786440 | tf_op jit(solution)/shard_map/ppermute | solution.py:414
  29.7 6.2 %copy.19 = bf16[512,64,256]{2,1,0:T(8,128)(2,1)} copy(bf16[512,64,256]{2,1,0:T(8,128)(2,1)S(1)} %get-tuple-element.13) | data formatting | bytes 33554432
  35.9 0.7 %copy.21 = s32[512,64]{0,1:T(8,128)} copy(s32[512,64]{0,1:T(8,128)S(1)} %bitcast.3) | data formatting | bytes 262144
  36.5 0.0 copy-start
  36.5 0.0 copy-start.1
  36.5 0.0 copy-start.2
  36.5 6.8 %copy.20 = bf16[512,64,256]{2,1,0:T(8,128)(2,1)} copy(bf16[512,64,256]{2,1,0:T(8,128)(2,1)S(1)} %get-tuple-element.14) | data formatting | bytes 33554432
  43.3 0.0 collective-permute-done.2.from_d
  43.4 0.0 collective-permute-done.1.from_y
  43.4 0.0 collective-permute-done.from_x
  43.4 0.0 copy-done
  43.4 0.0 copy-done.1
  43.4 0.0 copy-done.2
  43.4 3.6 %shard_map.148 = f32[512,1152]{1,0:T(8,128)S(1)} custom-call(f32[64,1024]{1,0:T(8,128)S(1)} %get-tuple-element.8.own, f32[64,1024]{1,0:T(8,128)S(1)} %collective-permute-done.from_x, f32[64,1024]{1,0:T(8,128)S(1)} %collective-permute-done.1.from_y, f32[64,1024]{1,0:T(8,128)S(1)} %collective-permute-done.2.from_d, bf16[512,1152]{1,0:T(8,128)(2,1)S(1)} %copy-done.1, ...), custom_call_target="tpu_custom_call" | custom-call | flops 1200000000 | bytes 6000000 | tf_op jit(solution)/shard_map/pallas_call | solution.py:415
  47.0 1.1 %convert_element_type.3 = bf16[512,1152]{1,0:T(8,128)(2,1)} convert(f32[512,1152]{1,0:T(8,128)S(1)} %shard_map.148) | non-fusion elementwise | flops 589824 | bytes 3538944 | tf_op jit(solution)/shard_map/convert_element_type | solution.py:429
Async XLA Ops:
  26.2 17.2 %collective-permute-start.2 = (f32[64,1024]{1,0:T(8,128)S(1)}, f32[64,1024]{1,0:T(8,128)S(1)}, u32[]{:S(2)}, u32[]{:S(2)}) collective-permute-start(f32[64,1024]{1,0:T(8,128)S(1)} %get-tuple-element.8.own), channel_id=1, source_target_pairs={{0,6},{1,7},{2,4},{3,5},{4,2},{5,3},{6,0},{7,1}} | collective-permute-start | bytes 786440 | tf_op jit(solution)/shard_map/ppermute | solution.py:414
  27.2 16.1 %collective-permute-start.1 = (f32[64,1024]{1,0:T(8,128)S(1)}, f32[64,1024]{1,0:T(8,128)S(1)}, u32[]{:S(2)}, u32[]{:S(2)}) collective-permute-start(f32[64,1024]{1,0:T(8,128)S(1)} %get-tuple-element.8.own), channel_id=1, source_target_pairs={{0,4},{1,5},{2,6},{3,7},{4,0},{5,1},{6,2},{7,3}} | collective-permute-start | bytes 786440 | tf_op jit(solution)/shard_map/ppermute | solution.py:414
  28.8 14.6 %collective-permute-start = (f32[64,1024]{1,0:T(8,128)S(1)}, f32[64,1024]{1,0:T(8,128)S(1)}, u32[]{:S(2)}, u32[]{:S(2)}) collective-permute-start(f32[64,1024]{1,0:T(8,128)S(1)} %get-tuple-element.8.own), channel_id=1, source_target_pairs={{0,2},{1,3},{2,0},{3,1},{4,6},{5,7},{6,4},{7,5}} | collective-permute-start | bytes 786440 | tf_op jit(solution)/shard_map/ppermute | solution.py:414
  36.5 6.9 %copy-start = (bf16[1024,1152]{1,0:T(8,128)(2,1)S(1)}, bf16[1024,1152]{1,0:T(8,128)(2,1)}, u32[]{:S(2)}) copy-start(bf16[1024,1152]{1,0:T(8,128)(2,1)} %wo_v.1) | copy-start | bytes 7077892
  36.5 6.9 %copy-start.1 = (bf16[512,1152]{1,0:T(8,128)(2,1)S(1)}, bf16[512,1152]{1,0:T(8,128)(2,1)}, u32[]{:S(2)}) copy-start(bf16[512,1152]{1,0:T(8,128)(2,1)} %x_v.1) | copy-start | bytes 3538948
  36.5 6.9 %copy-start.2 = (bf16[1152]{0:T(1024)(128)(2,1)S(1)}, bf16[1152]{0:T(1024)(128)(2,1)}, u32[]{:S(2)}) copy-start(bf16[1152]{0:T(1024)(128)(2,1)} %b_ref.1) | copy-start | bytes 6916

commit v9 on v8

--- a/solution.py
+++ b/solution.py
@@ -30,7 +30,7 @@
 CHUNK = 64
 AHEAD = 4
 NCHUNK = BATCH // CHUNK
-ROWS = 256
+ROWS = 512
 
 
 def sin_cos(theta):
@@ -116,7 +116,7 @@
 
     def chip_copies(self, c):
         return [send(self.part.at[pl.ds(al(c * CHUNK + self.p.eighth(m, self.p.core)), 8)],
-                     self.r1.at[pl.ds(al(c * 24 + 8 * (m - 1)), 8)],
+                     self.r1.at[pl.ds(al((c // 2) * 48 + 16 * (m - 1) + 8 * (c % 2)), 8)],
                      self.s1.at[0, 3 * c + m - 1], self.s1.at[1, 3 * c + m - 1], self.p.peer(m)) for m in (3, 1, 2)]
 
     def pair_step(self, c):
@@ -128,11 +128,13 @@
             cp.start()
 
     def chip_step(self, c):
-        for cp in self.chip_copies(c):
-            cp.wait_recv()
-        mine = self.part[pl.ds(al(c * CHUNK + self.p.eighth(0, self.p.core)), 8), :]
-        v, s = merge_rows([mine] + [self.r1[pl.ds(al(c * 24 + 8 * n), 8), :] for n in range(3)])
-        self.own[pl.ds(al(c * 8), 8), :] = normalise(v, s)
+        @pl.when(c % 2 == 1)
+        def _():
+            for cp in self.chip_copies(c - 1) + self.chip_copies(c):
+                cp.wait_recv()
+            mine = jnp.concatenate([self.part[pl.ds(al(k * CHUNK + self.p.eighth(0, self.p.core)), 8), :] for k in (c - 1, c)], axis=0)
+            v, s = merge_rows([mine] + [self.r1[pl.ds(al((c // 2) * 48 + 16 * n), 16), :] for n in range(3)])
+            self.own[pl.ds(al((c - 1) * 8), 16), :] = normalise(v, s)
 
     def drain(self, c):
         self.pair_copy(c).wait_send()
@@ -268,9 +270,9 @@
         cp.start()
     gain = 1.0 + ns_ref[...].astype(F32).reshape(1, D_MODEL)
 
-    @pl.loop(0, BATCH // 64)
+    @pl.loop(0, BATCH // 128)
     def _(i):
-        rows = pl.ds(pl.multiple_of(i * 64, 64), 64)
+        rows = pl.ds(pl.multiple_of(i * 128, 128), 128)
         xf = x_v[rows, :].astype(F32)
         mean_sq = jnp.sum(xf * xf, axis=1, keepdims=True) * (1.0 / D_MODEL)
         n_v[rows, :] = (xf * lax.rsqrt(mean_sq + EPS) * gain).astype(BF16)

time: 48.3 us -> 48.5 us (level)
  no operation moved by 1% of the time
where the time goes in v9:
time: 48.5 us; the launch traced here: 48.4 us
  Pallas kernels  29.4 us (61%)
  local copies, waits for them, and re-layouts  13.7 us (28%)
  starting transfers between devices  3.51 us (7%)
  other arithmetic  1.14 us (2%)
  between operations  0.68 us (1%)
    pallas_call x1, Pallas kernels, local_step(): pl.pallas_call(step_kernel, out_shape=(jax.ShapeDtypeStruct((BATCH // 8,...  25.8 us
    unnamed x9, local copies, waits for them, and re-layouts  13.7 us
    pallas_call x1, Pallas kernels, local_step(): pl.pallas_call(out_kernel, out_shape=jax.ShapeDtypeStruct((BATCH, D_MODEL...  3.65 us
    ppermute x3, starting transfers between devices, local_step(): lax.ppermute(own, 'kv', [(i, i ^ m) for i in range(8)])  3.51 us
    convert_element_type x1, other arithmetic, local_step(): return (x_out.astype(BF16), k_out, v_out, sp_t.T)  1.14 us
  transfers between devices with their start and end apart: 3, of which 0 were waited for; matrix products, arithmetic and copies ran while one was open for 28% of the time, Pallas kernels for 0%

profile of v9, /device:TPU:0, one launch (start us, length us, event | category | flops | bytes accessed | tf_op | source)
XLA Modules:
  0.0 48.4 jit_solution(253791121630626776)
XLA Ops:
  0.6 25.8 %shard_map.147 = (f32[64,1024]{1,0:T(8,128)S(1)}, bf16[512,64,256]{2,1,0:T(8,128)(2,1)S(1)}, bf16[512,64,256]{2,1,0:T(8,128)(2,1)S(1)}, s32[64,512]{1,0:T(8,128)S(1)}) custom-call(s32[1,512]{1,0:T(1,128)} %bitcast.5, f32[1,128]{1,0:T(1,128)} %constant.2.clone.freq_hbm, bf16[1152]{0:T(1024)(128)(2,1)} %ns_hbm.1, s32[64,512]{1,0:T(8,128)} %bitcast.4, ...), custom_call_target="tpu_custom_call" | custom-call | flops 30000001024 | bytes 40000000 | tf_op jit(solution)/shard_map/pallas_call | solution.py:380
  26.4 1.1 %collective-permute-start.2 = (f32[64,1024]{1,0:T(8,128)S(1)}, f32[64,1024]{1,0:T(8,128)S(1)}, u32[]{:S(2)}, u32[]{:S(2)}) collective-permute-start(f32[64,1024]{1,0:T(8,128)S(1)} %get-tuple-element.8.own), channel_id=1, source_target_pairs={{0,6},{1,7},{2,4},{3,5},{4,2},{5,3},{6,0},{7,1}} | collective-permute-start | bytes 786440 | tf_op jit(solution)/shard_map/ppermute | solution.py:416
  27.5 1.5 %collective-permute-start.1 = (f32[64,1024]{1,0:T(8,128)S(1)}, f32[64,1024]{1,0:T(8,128)S(1)}, u32[]{:S(2)}, u32[]{:S(2)}) collective-permute-start(f32[64,1024]{1,0:T(8,128)S(1)} %get-tuple-element.8.own), channel_id=1, source_target_pairs={{0,4},{1,5},{2,6},{3,7},{4,0},{5,1},{6,2},{7,3}} | collective-permute-start | bytes 786440 | tf_op jit(solution)/shard_map/ppermute | solution.py:416
  29.0 0.9 %collective-permute-start = (f32[64,1024]{1,0:T(8,128)S(1)}, f32[64,1024]{1,0:T(8,128)S(1)}, u32[]{:S(2)}, u32[]{:S(2)}) collective-permute-start(f32[64,1024]{1,0:T(8,128)S(1)} %get-tuple-element.8.own), channel_id=1, source_target_pairs={{0,2},{1,3},{2,0},{3,1},{4,6},{5,7},{6,4},{7,5}} | collective-permute-start | bytes 786440 | tf_op jit(solution)/shard_map/ppermute | solution.py:416
  29.9 6.2 %copy.19 = bf16[512,64,256]{2,1,0:T(8,128)(2,1)} copy(bf16[512,64,256]{2,1,0:T(8,128)(2,1)S(1)} %get-tuple-element.13) | data formatting | bytes 33554432
  36.1 0.7 %copy.21 = s32[512,64]{0,1:T(8,128)} copy(s32[512,64]{0,1:T(8,128)S(1)} %bitcast.3) | data formatting | bytes 262144
  36.7 0.0 copy-start
  36.7 0.0 copy-start.1
  36.7 0.0 copy-start.2
  36.7 6.8 %copy.20 = bf16[512,64,256]{2,1,0:T(8,128)(2,1)} copy(bf16[512,64,256]{2,1,0:T(8,128)(2,1)S(1)} %get-tuple-element.14) | data formatting | bytes 33554432
  43.6 0.0 collective-permute-done.2.from_d
  43.6 0.0 collective-permute-done.1.from_y
  43.6 0.0 collective-permute-done.from_x
  43.6 0.0 copy-done
  43.6 0.0 copy-done.1
  43.6 0.0 copy-done.2
  43.6 3.6 %shard_map.148 = f32[512,1152]{1,0:T(8,128)S(1)} custom-call(f32[64,1024]{1,0:T(8,128)S(1)} %get-tuple-element.8.own, f32[64,1024]{1,0:T(8,128)S(1)} %collective-permute-done.from_x, f32[64,1024]{1,0:T(8,128)S(1)} %collective-permute-done.1.from_y, f32[64,1024]{1,0:T(8,128)S(1)} %collective-permute-done.2.from_d, bf16[512,1152]{1,0:T(8,128)(2,1)S(1)} %copy-done.1, ...), custom_call_target="tpu_custom_call" | custom-call | flops 1200000000 | bytes 6000000 | tf_op jit(solution)/shard_map/pallas_call | solution.py:417
  47.3 1.1 %convert_element_type.3 = bf16[512,1152]{1,0:T(8,128)(2,1)} convert(f32[512,1152]{1,0:T(8,128)S(1)} %shard_map.148) | non-fusion elementwise | flops 589824 | bytes 3538944 | tf_op jit(solution)/shard_map/convert_element_type | solution.py:431
Async XLA Ops:
  26.4 17.2 %collective-permute-start.2 = (f32[64,1024]{1,0:T(8,128)S(1)}, f32[64,1024]{1,0:T(8,128)S(1)}, u32[]{:S(2)}, u32[]{:S(2)}) collective-permute-start(f32[64,1024]{1,0:T(8,128)S(1)} %get-tuple-element.8.own), channel_id=1, source_target_pairs={{0,6},{1,7},{2,4},{3,5},{4,2},{5,3},{6,0},{7,1}} | collective-permute-start | bytes 786440 | tf_op jit(solution)/shard_map/ppermute | solution.py:416
  27.5 16.1 %collective-permute-start.1 = (f32[64,1024]{1,0:T(8,128)S(1)}, f32[64,1024]{1,0:T(8,128)S(1)}, u32[]{:S(2)}, u32[]{:S(2)}) collective-permute-start(f32[64,1024]{1,0:T(8,128)S(1)} %get-tuple-element.8.own), channel_id=1, source_target_pairs={{0,4},{1,5},{2,6},{3,7},{4,0},{5,1},{6,2},{7,3}} | collective-permute-start | bytes 786440 | tf_op jit(solution)/shard_map/ppermute | solution.py:416
  29.0 14.6 %collective-permute-start = (f32[64,1024]{1,0:T(8,128)S(1)}, f32[64,1024]{1,0:T(8,128)S(1)}, u32[]{:S(2)}, u32[]{:S(2)}) collective-permute-start(f32[64,1024]{1,0:T(8,128)S(1)} %get-tuple-element.8.own), channel_id=1, source_target_pairs={{0,2},{1,3},{2,0},{3,1},{4,6},{5,7},{6,4},{7,5}} | collective-permute-start | bytes 786440 | tf_op jit(solution)/shard_map/ppermute | solution.py:416
  36.7 6.9 %copy-start = (bf16[1024,1152]{1,0:T(8,128)(2,1)S(1)}, bf16[1024,1152]{1,0:T(8,128)(2,1)}, u32[]{:S(2)}) copy-start(bf16[1024,1152]{1,0:T(8,128)(2,1)} %wo_v.1) | copy-start | bytes 7077892
  36.7 6.9 %copy-start.1 = (bf16[512,1152]{1,0:T(8,128)(2,1)S(1)}, bf16[512,1152]{1,0:T(8,128)(2,1)}, u32[]{:S(2)}) copy-start(bf16[512,1152]{1,0:T(8,128)(2,1)} %x_v.1) | copy-start | bytes 3538948
  36.7 6.9 %copy-start.2 = (bf16[1152]{0:T(1024)(128)(2,1)S(1)}, bf16[1152]{0:T(1024)(128)(2,1)}, u32[]{:S(2)}) copy-start(bf16[1152]{0:T(1024)(128)(2,1)} %b_ref.1) | copy-start | bytes 6916

commit v10 on v9

--- a/solution.py
+++ b/solution.py
@@ -315,7 +315,7 @@
 
         red.pair_copy(c).start()
 
-    lags = ((0, attend), (1, red.pair_step), (4, red.chip_step))
+    lags = ((0, attend), (2, red.pair_step), (9, red.chip_step))
 
     @pl.loop(0, NCHUNK + lags[-1][0])
     def _(i):

time: 48.5 us -> 49.5 us (1.021)
  Pallas kernels: 29.4 us -> 30.4 us
    pallas_call x1, Pallas kernels: 25.8 us -> 26.7 us  [local_step(): pl.pallas_call(step_kernel, out_shape=(jax.ShapeDtypeStruct((BATCH // 8,...]
where the time goes in v10:
time: 49.5 us; the launch traced here: 49.4 us
  Pallas kernels  30.4 us (61%)
  local copies, waits for them, and re-layouts  13.7 us (28%)
  starting transfers between devices  3.51 us (7%)
  other arithmetic  1.14 us (2%)
  between operations  0.68 us (1%)
    pallas_call x1, Pallas kernels, local_step(): pl.pallas_call(step_kernel, out_shape=(jax.ShapeDtypeStruct((BATCH // 8,...  26.7 us
    unnamed x9, local copies, waits for them, and re-layouts  13.7 us
    pallas_call x1, Pallas kernels, local_step(): pl.pallas_call(out_kernel, out_shape=jax.ShapeDtypeStruct((BATCH, D_MODEL...  3.65 us
    ppermute x3, starting transfers between devices, local_step(): lax.ppermute(own, 'kv', [(i, i ^ m) for i in range(8)])  3.51 us
    convert_element_type x1, other arithmetic, local_step(): return (x_out.astype(BF16), k_out, v_out, sp_t.T)  1.14 us
  transfers between devices with their start and end apart: 3, of which 0 were waited for; matrix products, arithmetic and copies ran while one was open for 28% of the time, Pallas kernels for 0%

profile of v10, /device:TPU:0, one launch (start us, length us, event | category | flops | bytes accessed | tf_op | source)
XLA Modules:
  0.0 49.4 jit_solution(9326142193265144579)
XLA Ops:
  0.6 26.7 %shard_map.147 = (f32[64,1024]{1,0:T(8,128)S(1)}, bf16[512,64,256]{2,1,0:T(8,128)(2,1)S(1)}, bf16[512,64,256]{2,1,0:T(8,128)(2,1)S(1)}, s32[64,512]{1,0:T(8,128)S(1)}) custom-call(s32[1,512]{1,0:T(1,128)} %bitcast.5, f32[1,128]{1,0:T(1,128)} %constant.2.clone.freq_hbm, bf16[1152]{0:T(1024)(128)(2,1)} %ns_hbm.1, s32[64,512]{1,0:T(8,128)} %bitcast.4, ...), custom_call_target="tpu_custom_call" | custom-call | flops 30000001024 | bytes 40000000 | tf_op jit(solution)/shard_map/pallas_call | solution.py:380
  27.4 0.9 %collective-permute-start.2 = (f32[64,1024]{1,0:T(8,128)S(1)}, f32[64,1024]{1,0:T(8,128)S(1)}, u32[]{:S(2)}, u32[]{:S(2)}) collective-permute-start(f32[64,1024]{1,0:T(8,128)S(1)} %get-tuple-element.8.own), channel_id=1, source_target_pairs={{0,6},{1,7},{2,4},{3,5},{4,2},{5,3},{6,0},{7,1}} | collective-permute-start | bytes 786440 | tf_op jit(solution)/shard_map/ppermute | solution.py:416
  28.3 1.5 %collective-permute-start.1 = (f32[64,1024]{1,0:T(8,128)S(1)}, f32[64,1024]{1,0:T(8,128)S(1)}, u32[]{:S(2)}, u32[]{:S(2)}) collective-permute-start(f32[64,1024]{1,0:T(8,128)S(1)} %get-tuple-element.8.own), channel_id=1, source_target_pairs={{0,4},{1,5},{2,6},{3,7},{4,0},{5,1},{6,2},{7,3}} | collective-permute-start | bytes 786440 | tf_op jit(solution)/shard_map/ppermute | solution.py:416
  29.9 1.0 %collective-permute-start = (f32[64,1024]{1,0:T(8,128)S(1)}, f32[64,1024]{1,0:T(8,128)S(1)}, u32[]{:S(2)}, u32[]{:S(2)}) collective-permute-start(f32[64,1024]{1,0:T(8,128)S(1)} %get-tuple-element.8.own), channel_id=1, source_target_pairs={{0,2},{1,3},{2,0},{3,1},{4,6},{5,7},{6,4},{7,5}} | collective-permute-start | bytes 786440 | tf_op jit(solution)/shard_map/ppermute | solution.py:416
  30.9 6.2 %copy.19 = bf16[512,64,256]{2,1,0:T(8,128)(2,1)} copy(bf16[512,64,256]{2,1,0:T(8,128)(2,1)S(1)} %get-tuple-element.13) | data formatting | bytes 33554432
  37.1 0.7 %copy.21 = s32[512,64]{0,1:T(8,128)} copy(s32[512,64]{0,1:T(8,128)S(1)} %bitcast.3) | data formatting | bytes 262144
  37.7 0.0 copy-start
  37.7 0.0 copy-start.1
  37.7 0.0 copy-start.2
  37.7 6.8 %copy.20 = bf16[512,64,256]{2,1,0:T(8,128)(2,1)} copy(bf16[512,64,256]{2,1,0:T(8,128)(2,1)S(1)} %get-tuple-element.14) | data formatting | bytes 33554432
  44.6 0.0 collective-permute-done.2.from_d
  44.6 0.0 collective-permute-done.1.from_y
  44.6 0.0 collective-permute-done.from_x
  44.6 0.0 copy-done
  44.6 0.0 copy-done.1
  44.6 0.0 copy-done.2
  44.6 3.6 %shard_map.148 = f32[512,1152]{1,0:T(8,128)S(1)} custom-call(f32[64,1024]{1,0:T(8,128)S(1)} %get-tuple-element.8.own, f32[64,1024]{1,0:T(8,128)S(1)} %collective-permute-done.from_x, f32[64,1024]{1,0:T(8,128)S(1)} %collective-permute-done.1.from_y, f32[64,1024]{1,0:T(8,128)S(1)} %collective-permute-done.2.from_d, bf16[512,1152]{1,0:T(8,128)(2,1)S(1)} %copy-done.1, ...), custom_call_target="tpu_custom_call" | custom-call | flops 1200000000 | bytes 6000000 | tf_op jit(solution)/shard_map/pallas_call | solution.py:417
  48.2 1.1 %convert_element_type.3 = bf16[512,1152]{1,0:T(8,128)(2,1)} convert(f32[512,1152]{1,0:T(8,128)S(1)} %shard_map.148) | non-fusion elementwise | flops 589824 | bytes 3538944 | tf_op jit(solution)/shard_map/convert_element_type | solution.py:431
Async XLA Ops:
  27.4 17.2 %collective-permute-start.2 = (f32[64,1024]{1,0:T(8,128)S(1)}, f32[64,1024]{1,0:T(8,128)S(1)}, u32[]{:S(2)}, u32[]{:S(2)}) collective-permute-start(f32[64,1024]{1,0:T(8,128)S(1)} %get-tuple-element.8.own), channel_id=1, source_target_pairs={{0,6},{1,7},{2,4},{3,5},{4,2},{5,3},{6,0},{7,1}} | collective-permute-start | bytes 786440 | tf_op jit(solution)/shard_map/ppermute | solution.py:416
  28.3 16.2 %collective-permute-start.1 = (f32[64,1024]{1,0:T(8,128)S(1)}, f32[64,1024]{1,0:T(8,128)S(1)}, u32[]{:S(2)}, u32[]{:S(2)}) collective-permute-start(f32[64,1024]{1,0:T(8,128)S(1)} %get-tuple-element.8.own), channel_id=1, source_target_pairs={{0,4},{1,5},{2,6},{3,7},{4,0},{5,1},{6,2},{7,3}} | collective-permute-start | bytes 786440 | tf_op jit(solution)/shard_map/ppermute | solution.py:416
  29.9 14.7 %collective-permute-start = (f32[64,1024]{1,0:T(8,128)S(1)}, f32[64,1024]{1,0:T(8,128)S(1)}, u32[]{:S(2)}, u32[]{:S(2)}) collective-permute-start(f32[64,1024]{1,0:T(8,128)S(1)} %get-tuple-element.8.own), channel_id=1, source_target_pairs={{0,2},{1,3},{2,0},{3,1},{4,6},{5,7},{6,4},{7,5}} | collective-permute-start | bytes 786440 | tf_op jit(solution)/shard_map/ppermute | solution.py:416
  37.7 6.9 %copy-start = (bf16[1024,1152]{1,0:T(8,128)(2,1)S(1)}, bf16[1024,1152]{1,0:T(8,128)(2,1)}, u32[]{:S(2)}) copy-start(bf16[1024,1152]{1,0:T(8,128)(2,1)} %wo_v.1) | copy-start | bytes 7077892
  37.7 6.9 %copy-start.1 = (bf16[512,1152]{1,0:T(8,128)(2,1)S(1)}, bf16[512,1152]{1,0:T(8,128)(2,1)}, u32[]{:S(2)}) copy-start(bf16[512,1152]{1,0:T(8,128)(2,1)} %x_v.1) | copy-start | bytes 3538948
  37.7 6.9 %copy-start.2 = (bf16[1152]{0:T(1024)(128)(2,1)S(1)}, bf16[1152]{0:T(1024)(128)(2,1)}, u32[]{:S(2)}) copy-start(bf16[1152]{0:T(1024)(128)(2,1)} %b_ref.1) | copy-start | bytes 6916

commit v11 on v10

--- a/solution.py
+++ b/solution.py
@@ -28,7 +28,6 @@
 GROUP = 8
 STEP = 64
 CHUNK = 64
-AHEAD = 4
 NCHUNK = BATCH // CHUNK
 ROWS = 512
 
@@ -266,7 +265,7 @@
         return jnp.concatenate([r, t[:, ROPE_DIM:]], axis=1)
 
     w_in(0).wait()
-    for cp in kv_in(0):
+    for cp in kv_in(0) + kv_in(1):
         cp.start()
     gain = 1.0 + ns_ref[...].astype(F32).reshape(1, D_MODEL)
 
@@ -279,19 +278,14 @@
 
     for n in range(1, 4):
         w_in(n).wait()
-    for c in range(1, AHEAD):
+    for c in range(2, NCHUNK):
         for cp in kv_in(c):
             cp.start()
     red = Reduce(p, part, r0, r1, own, s0, s1)
     att = Attention(off, kbuf, vbuf, q_v, kn_v, vn_v, p_col, js_col, part)
 
     def attend(c):
-        @pl.when(c + AHEAD < NCHUNK)
-        def _():
-            for cp in kv_in(c + AHEAD):
-                cp.start()
-
-        @pl.when(c == AHEAD)
+        @pl.when(c == NCHUNK // 2)
         def _():
             w_in(4).start()
 
@@ -315,7 +309,7 @@
 
         red.pair_copy(c).start()
 
-    lags = ((0, attend), (2, red.pair_step), (9, red.chip_step))
+    lags = ((0, attend), (1, red.pair_step), (6, red.chip_step))
 
     @pl.loop(0, NCHUNK + lags[-1][0])
     def _(i):

time: 49.5 us -> 48.5 us (0.980)
  Pallas kernels: 30.4 us -> 29.4 us
    pallas_call x1, Pallas kernels: 26.7 us -> 25.8 us  [local_step(): pl.pallas_call(step_kernel, out_shape=(jax.ShapeDtypeStruct((BATCH // 8,...]
where the time goes in v11:
time: 48.5 us; the launch traced here: 48.4 us
  Pallas kernels  29.4 us (61%)
  local copies, waits for them, and re-layouts  13.7 us (28%)
  starting transfers between devices  3.51 us (7%)
  other arithmetic  1.14 us (2%)
  between operations  0.68 us (1%)
    pallas_call x1, Pallas kernels, local_step(): pl.pallas_call(step_kernel, out_shape=(jax.ShapeDtypeStruct((BATCH // 8,...  25.8 us
    unnamed x9, local copies, waits for them, and re-layouts  13.7 us
    pallas_call x1, Pallas kernels, local_step(): pl.pallas_call(out_kernel, out_shape=jax.ShapeDtypeStruct((BATCH, D_MODEL...  3.65 us
    ppermute x3, starting transfers between devices, local_step(): lax.ppermute(own, 'kv', [(i, i ^ m) for i in range(8)])  3.51 us
    convert_element_type x1, other arithmetic, local_step(): return (x_out.astype(BF16), k_out, v_out, sp_t.T)  1.14 us
  transfers between devices with their start and end apart: 3, of which 0 were waited for; matrix products, arithmetic and copies ran while one was open for 28% of the time, Pallas kernels for 0%

profile of v11, /device:TPU:0, one launch (start us, length us, event | category | flops | bytes accessed | tf_op | source)
XLA Modules:
  0.0 48.4 jit_solution(11044724491410581340)
XLA Ops:
  0.6 25.8 %shard_map.147 = (f32[64,1024]{1,0:T(8,128)S(1)}, bf16[512,64,256]{2,1,0:T(8,128)(2,1)S(1)}, bf16[512,64,256]{2,1,0:T(8,128)(2,1)S(1)}, s32[64,512]{1,0:T(8,128)S(1)}) custom-call(s32[1,512]{1,0:T(1,128)} %bitcast.5, f32[1,128]{1,0:T(1,128)} %constant.2.clone.freq_hbm, bf16[1152]{0:T(1024)(128)(2,1)} %ns_hbm.1, s32[64,512]{1,0:T(8,128)} %bitcast.4, ...), custom_call_target="tpu_custom_call" | custom-call | flops 30000001024 | bytes 40000000 | tf_op jit(solution)/shard_map/pallas_call | solution.py:374
  26.4 1.1 %collective-permute-start.2 = (f32[64,1024]{1,0:T(8,128)S(1)}, f32[64,1024]{1,0:T(8,128)S(1)}, u32[]{:S(2)}, u32[]{:S(2)}) collective-permute-start(f32[64,1024]{1,0:T(8,128)S(1)} %get-tuple-element.8.own), channel_id=1, source_target_pairs={{0,6},{1,7},{2,4},{3,5},{4,2},{5,3},{6,0},{7,1}} | collective-permute-start | bytes 786440 | tf_op jit(solution)/shard_map/ppermute | solution.py:410
  27.5 1.5 %collective-permute-start.1 = (f32[64,1024]{1,0:T(8,128)S(1)}, f32[64,1024]{1,0:T(8,128)S(1)}, u32[]{:S(2)}, u32[]{:S(2)}) collective-permute-start(f32[64,1024]{1,0:T(8,128)S(1)} %get-tuple-element.8.own), channel_id=1, source_target_pairs={{0,4},{1,5},{2,6},{3,7},{4,0},{5,1},{6,2},{7,3}} | collective-permute-start | bytes 786440 | tf_op jit(solution)/shard_map/ppermute | solution.py:410
  29.0 1.0 %collective-permute-start = (f32[64,1024]{1,0:T(8,128)S(1)}, f32[64,1024]{1,0:T(8,128)S(1)}, u32[]{:S(2)}, u32[]{:S(2)}) collective-permute-start(f32[64,1024]{1,0:T(8,128)S(1)} %get-tuple-element.8.own), channel_id=1, source_target_pairs={{0,2},{1,3},{2,0},{3,1},{4,6},{5,7},{6,4},{7,5}} | collective-permute-start | bytes 786440 | tf_op jit(solution)/shard_map/ppermute | solution.py:410
  29.9 6.2 %copy.19 = bf16[512,64,256]{2,1,0:T(8,128)(2,1)} copy(bf16[512,64,256]{2,1,0:T(8,128)(2,1)S(1)} %get-tuple-element.13) | data formatting | bytes 33554432
  36.1 0.7 %copy.21 = s32[512,64]{0,1:T(8,128)} copy(s32[512,64]{0,1:T(8,128)S(1)} %bitcast.3) | data formatting | bytes 262144
  36.7 0.0 copy-start
  36.7 0.0 copy-start.1
  36.7 0.0 copy-start.2
  36.7 6.8 %copy.20 = bf16[512,64,256]{2,1,0:T(8,128)(2,1)} copy(bf16[512,64,256]{2,1,0:T(8,128)(2,1)S(1)} %get-tuple-element.14) | data formatting | bytes 33554432
  43.6 0.0 collective-permute-done.2.from_d
  43.6 0.0 collective-permute-done.1.from_y
  43.6 0.0 collective-permute-done.from_x
  43.6 0.0 copy-done
  43.6 0.0 copy-done.1
  43.6 0.0 copy-done.2
  43.6 3.6 %shard_map.148 = f32[512,1152]{1,0:T(8,128)S(1)} custom-call(f32[64,1024]{1,0:T(8,128)S(1)} %get-tuple-element.8.own, f32[64,1024]{1,0:T(8,128)S(1)} %collective-permute-done.from_x, f32[64,1024]{1,0:T(8,128)S(1)} %collective-permute-done.1.from_y, f32[64,1024]{1,0:T(8,128)S(1)} %collective-permute-done.2.from_d, bf16[512,1152]{1,0:T(8,128)(2,1)S(1)} %copy-done.1, ...), custom_call_target="tpu_custom_call" | custom-call | flops 1200000000 | bytes 6000000 | tf_op jit(solution)/shard_map/pallas_call | solution.py:411
  47.3 1.1 %convert_element_type.3 = bf16[512,1152]{1,0:T(8,128)(2,1)} convert(f32[512,1152]{1,0:T(8,128)S(1)} %shard_map.148) | non-fusion elementwise | flops 589824 | bytes 3538944 | tf_op jit(solution)/shard_map/convert_element_type | solution.py:425
Async XLA Ops:
  26.4 17.2 %collective-permute-start.2 = (f32[64,1024]{1,0:T(8,128)S(1)}, f32[64,1024]{1,0:T(8,128)S(1)}, u32[]{:S(2)}, u32[]{:S(2)}) collective-permute-start(f32[64,1024]{1,0:T(8,128)S(1)} %get-tuple-element.8.own), channel_id=1, source_target_pairs={{0,6},{1,7},{2,4},{3,5},{4,2},{5,3},{6,0},{7,1}} | collective-permute-start | bytes 786440 | tf_op jit(solution)/shard_map/ppermute | solution.py:410
  27.5 16.1 %collective-permute-start.1 = (f32[64,1024]{1,0:T(8,128)S(1)}, f32[64,1024]{1,0:T(8,128)S(1)}, u32[]{:S(2)}, u32[]{:S(2)}) collective-permute-start(f32[64,1024]{1,0:T(8,128)S(1)} %get-tuple-element.8.own), channel_id=1, source_target_pairs={{0,4},{1,5},{2,6},{3,7},{4,0},{5,1},{6,2},{7,3}} | collective-permute-start | bytes 786440 | tf_op jit(solution)/shard_map/ppermute | solution.py:410
  29.0 14.6 %collective-permute-start = (f32[64,1024]{1,0:T(8,128)S(1)}, f32[64,1024]{1,0:T(8,128)S(1)}, u32[]{:S(2)}, u32[]{:S(2)}) collective-permute-start(f32[64,1024]{1,0:T(8,128)S(1)} %get-tuple-element.8.own), channel_id=1, source_target_pairs={{0,2},{1,3},{2,0},{3,1},{4,6},{5,7},{6,4},{7,5}} | collective-permute-start | bytes 786440 | tf_op jit(solution)/shard_map/ppermute | solution.py:410
  36.7 6.9 %copy-start = (bf16[1024,1152]{1,0:T(8,128)(2,1)S(1)}, bf16[1024,1152]{1,0:T(8,128)(2,1)}, u32[]{:S(2)}) copy-start(bf16[1024,1152]{1,0:T(8,128)(2,1)} %wo_v.1) | copy-start | bytes 7077892
  36.7 6.9 %copy-start.1 = (bf16[512,1152]{1,0:T(8,128)(2,1)S(1)}, bf16[512,1152]{1,0:T(8,128)(2,1)}, u32[]{:S(2)}) copy-start(bf16[512,1152]{1,0:T(8,128)(2,1)} %x_v.1) | copy-start | bytes 3538948
  36.7 6.9 %copy-start.2 = (bf16[1152]{0:T(1024)(128)(2,1)S(1)}, bf16[1152]{0:T(1024)(128)(2,1)}, u32[]{:S(2)}) copy-start(bf16[1152]{0:T(1024)(128)(2,1)} %b_ref.1) | copy-start | bytes 6916

commit v12 on v11

--- a/solution.py
+++ b/solution.py
@@ -26,6 +26,7 @@
 QW = HEADS * HEAD_DIM
 PW = QW + 128
 GROUP = 8
+HALF = 32
 STEP = 64
 CHUNK = 64
 NCHUNK = BATCH // CHUNK
@@ -206,7 +207,7 @@
             for h in range(HEADS):
                 part[rows, h * HEAD_DIM:(h + 1) * HEAD_DIM] = o[h * GROUP:(h + 1) * GROUP, :]
 
-        starts = [al(base + g * GROUP, GROUP) for g in range(CHUNK // GROUP)]
+        starts = [al(base + g * GROUP, GROUP) for g in range(HALF // GROUP)]
         cs = [scores(r0) for r0 in starts]
         ps = [soften(r0, c) for r0, c in zip(starts, cs)]
         for r0, e in zip(starts, ps):
@@ -217,9 +218,9 @@
     return pl.ds(pl.multiple_of(c * CHUNK, CHUNK), CHUNK)
 
 
-def step_kernel(pos_hbm, freq_hbm, ns_hbm, sp_hbm, x_hbm, wq_hbm, wk_hbm, wv_hbm, k_hbm, v_hbm,
-                own, kbuf, vbuf, sp_out,
-                x_v, wq_v, wk_v, wv_v, n_v, q_v, kn_v, vn_v, p_col, js_col, cos_v, sin_v,
+def step_kernel(pos_hbm, freq_hbm, ns_hbm, sp_hbm, x_hbm, wq_hbm, wk_hbm, wv_hbm, wo_hbm, k_hbm, v_hbm,
+                own, kbuf, vbuf, sp_out, x_v, wo_v,
+                wq_v, wk_v, wv_v, n_v, q_v, kn_v, vn_v, p_col, js_col, cos_v, sin_v,
                 part, r0, r1, pos_row, freq_ref, ns_ref, w_sem, k_sem, v_sem, s0, s1):
     p = Places()
     barrier = pltpu.get_barrier_semaphore()
@@ -227,7 +228,7 @@
         pl.semaphore_signal(barrier, inc=1, device_id={'kv': peer}, device_id_type=pl.DeviceIdType.MESH)
     off = lax.axis_index('kv') * SLOTS
     weights = ((x_hbm, x_v), (wk_hbm, wk_v), (wv_hbm, wv_v), (wq_hbm, wq_v), (sp_hbm, sp_out),
-               (pos_hbm, pos_row), (freq_hbm, freq_ref), (ns_hbm, ns_ref))
+               (pos_hbm, pos_row), (freq_hbm, freq_ref), (ns_hbm, ns_ref), (wo_hbm, wo_v))
 
     def w_in(n):
         return pltpu.make_async_copy(weights[n][0], weights[n][1], w_sem.at[n])
@@ -285,9 +286,10 @@
     att = Attention(off, kbuf, vbuf, q_v, kn_v, vn_v, p_col, js_col, part)
 
     def attend(c):
-        @pl.when(c == NCHUNK // 2)
+        @pl.when(c == NCHUNK - 1)
         def _():
             w_in(4).start()
+            w_in(8).start()
 
         @pl.when(c % (ROWS // CHUNK) == 0)
         def _():
@@ -301,13 +303,14 @@
 
         for cp in kv_in(c):
             cp.wait()
-        att.rows(c * CHUNK)
+        att.rows(c * CHUNK + HALF * (1 - p.core))
 
         @pl.when(c == 0)
         def _():
             pl.semaphore_wait(barrier, 4)
 
         red.pair_copy(c).start()
+        att.rows(c * CHUNK + HALF * p.core)
 
     lags = ((0, attend), (1, red.pair_step), (6, red.chip_step))
 
@@ -319,6 +322,7 @@
                 body(i - lag)
 
     w_in(4).wait()
+    w_in(8).wait()
     p_all = pos_row[...]
     slot_ids = off + lax.broadcasted_iota(jnp.int32, (SLOTS, BATCH), 0)
     sp_out[...] = jnp.where(slot_ids == (p_all & 511), p_all, sp_out[...])
@@ -371,16 +375,17 @@
         return pltpu.with_memory_space_constraint(a, pltpu.HBM)
 
     def local_step(x_in, positions, k_cache, v_cache, slot_pos, norm_scale, w_q, w_k, w_v, w_o, b_o):
-        own, k_out, v_out, sp_t = pl.pallas_call(
+        own, k_out, v_out, sp_t, x_keep, wo_keep = pl.pallas_call(
             step_kernel,
             out_shape=(jax.ShapeDtypeStruct((BATCH // 8, QW), F32),
                        pltpu.VMEM((BATCH, SLOTS, HEAD_DIM), BF16),
                        pltpu.VMEM((BATCH, SLOTS, HEAD_DIM), BF16),
-                       pltpu.VMEM((SLOTS, BATCH), jnp.int32)),
-            in_specs=[hbm] * 10,
-            out_specs=(vmem,) * 4,
+                       pltpu.VMEM((SLOTS, BATCH), jnp.int32),
+                       pltpu.VMEM((BATCH, D_MODEL), BF16),
+                       pltpu.VMEM((QW, D_MODEL), BF16)),
+            in_specs=[hbm] * 11,
+            out_specs=(vmem,) * 6,
             scratch_shapes=[
-                pltpu.VMEM((BATCH, D_MODEL), BF16),
                 pltpu.VMEM((D_MODEL, QW), BF16),
                 pltpu.VMEM((D_MODEL, HEAD_DIM), BF16),
                 pltpu.VMEM((D_MODEL, HEAD_DIM), BF16),
@@ -398,15 +403,15 @@
                 pltpu.VMEM((1, BATCH), jnp.int32),
                 pltpu.VMEM((1, ROPE_DIM), F32),
                 pltpu.VMEM((D_MODEL,), BF16),
-                pltpu.SemaphoreType.DMA((8,)),
+                pltpu.SemaphoreType.DMA((9,)),
                 pltpu.SemaphoreType.DMA((NCHUNK,)),
                 pltpu.SemaphoreType.DMA((NCHUNK,)),
                 pltpu.SemaphoreType.DMA((2, NCHUNK)),
                 pltpu.SemaphoreType.DMA((2, 3 * NCHUNK)),
             ],
             cost_estimate=pl.CostEstimate(flops=30_000_000_000, bytes_accessed=40_000_000, transcendentals=200_000),
-            compiler_params=pltpu.CompilerParams(collective_id=0, has_side_effects=True, vmem_limit_bytes=20 * 1024 * 1024),
-        )(*[in_hbm(a) for a in (positions.reshape(1, BATCH), jnp.asarray(inv_freq_row()), norm_scale, slot_pos.T, x_in, w_q, w_k, w_v, k_cache, v_cache)])
+            compiler_params=pltpu.CompilerParams(collective_id=0, has_side_effects=True, vmem_limit_bytes=18 * 1024 * 1024),
+        )(*[in_hbm(a) for a in (positions.reshape(1, BATCH), jnp.asarray(inv_freq_row()), norm_scale, slot_pos.T, x_in, w_q, w_k, w_v, w_o, k_cache, v_cache)])
         far = [lax.ppermute(own, 'kv', [(i, i ^ m) for i in range(8)]) for m in (2, 4, 6)]
         x_out = pl.pallas_call(
             out_kernel,
@@ -420,8 +425,8 @@
                 pltpu.SemaphoreType.DMA((4,)),
             ],
             cost_estimate=pl.CostEstimate(flops=1_200_000_000, bytes_accessed=6_000_000, transcendentals=0),
-            compiler_params=pltpu.CompilerParams(collective_id=1, has_side_effects=True, vmem_limit_bytes=20 * 1024 * 1024),
-        )(own, *far, x_in, w_o, b_o)
+            compiler_params=pltpu.CompilerParams(collective_id=1, has_side_effects=True, vmem_limit_bytes=18 * 1024 * 1024),
+        )(own, *far, x_keep, wo_keep, b_o)
         return x_out.astype(BF16), k_out, v_out, sp_t.T
 
     return jax.shard_map(

time: 48.5 us -> 48.3 us (level)
  local copies, waits for them, and re-layouts: 13.7 us -> 13 us
  Pallas kernels: 29.4 us -> 29.9 us
    unnamed x9 -> x5, local copies, waits for them, and re-layouts: 13.7 us -> 13 us
  transfers between devices with their start and end apart: 3 -> 3, of which waited for: 0 -> 0; matrix products, arithmetic and copies ran while one was open for 28% -> 27% of each run, Pallas kernels for 0% -> 0%
where the time goes in v12:
time: 48.3 us; the launch traced here: 48.2 us
  Pallas kernels  29.9 us (62%)
  local copies, waits for them, and re-layouts  13 us (27%)
  starting transfers between devices  3.51 us (7%)
  other arithmetic  1.14 us (2%)
  between operations  0.67 us (1%)
    pallas_call x1, Pallas kernels, local_step(): pl.pallas_call(step_kernel, out_shape=(jax.ShapeDtypeStruct((BATCH // 8,...  26.2 us
    unnamed x5, local copies, waits for them, and re-layouts  13 us
    pallas_call x1, Pallas kernels, local_step(): pl.pallas_call(out_kernel, out_shape=jax.ShapeDtypeStruct((BATCH, D_MODEL...  3.65 us
    ppermute x3, starting transfers between devices, local_step(): lax.ppermute(own, 'kv', [(i, i ^ m) for i in range(8)])  3.51 us
    convert_element_type x1, other arithmetic, local_step(): return (x_out.astype(BF16), k_out, v_out, sp_t.T)  1.14 us
  transfers between devices with their start and end apart: 3, of which 0 were waited for; matrix products, arithmetic and copies ran while one was open for 27% of the time, Pallas kernels for 0%

profile of v12, /device:TPU:0, one launch (start us, length us, event | category | flops | bytes accessed | tf_op | source)
XLA Modules:
  0.0 48.2 jit_solution(6501657745251620164)
XLA Ops:
  0.6 26.2 %shard_map.147 = (f32[64,1024]{1,0:T(8,128)S(1)}, bf16[512,64,256]{2,1,0:T(8,128)(2,1)S(1)}, bf16[512,64,256]{2,1,0:T(8,128)(2,1)S(1)}, s32[64,512]{1,0:T(8,128)...) custom-call(s32[1,512]{1,0:T(1,128)} %bitcast.5, f32[1,128]{1,0:T(1,128)} %constant.2.clone.freq_hbm, ...), custom_call_target="tpu_custom_call" | custom-call | flops 30000001024 | bytes 40000000 | tf_op jit(solution)/shard_map/pallas_call | solution.py:378
  26.9 0.8 %collective-permute-start.2 = (f32[64,1024]{1,0:T(8,128)S(1)}, f32[64,1024]{1,0:T(8,128)S(1)}, u32[]{:S(2)}, u32[]{:S(2)}) collective-permute-start(f32[64,1024]{1,0:T(8,128)S(1)} %get-tuple-element.10.own), channel_id=1, source_target_pairs={{0,6},{1,7},{2,4},{3,5},{4,2},{5,3},{6,0},{7,1}} | collective-permute-start | bytes 786440 | tf_op jit(solution)/shard_map/ppermute | solution.py:415
  27.7 1.7 %collective-permute-start.1 = (f32[64,1024]{1,0:T(8,128)S(1)}, f32[64,1024]{1,0:T(8,128)S(1)}, u32[]{:S(2)}, u32[]{:S(2)}) collective-permute-start(f32[64,1024]{1,0:T(8,128)S(1)} %get-tuple-element.10.own), channel_id=1, source_target_pairs={{0,4},{1,5},{2,6},{3,7},{4,0},{5,1},{6,2},{7,3}} | collective-permute-start | bytes 786440 | tf_op jit(solution)/shard_map/ppermute | solution.py:415
  29.4 1.0 %collective-permute-start = (f32[64,1024]{1,0:T(8,128)S(1)}, f32[64,1024]{1,0:T(8,128)S(1)}, u32[]{:S(2)}, u32[]{:S(2)}) collective-permute-start(f32[64,1024]{1,0:T(8,128)S(1)} %get-tuple-element.10.own), channel_id=1, source_target_pairs={{0,2},{1,3},{2,0},{3,1},{4,6},{5,7},{6,4},{7,5}} | collective-permute-start | bytes 786440 | tf_op jit(solution)/shard_map/ppermute | solution.py:415
  30.4 0.7 %copy.21 = s32[512,64]{0,1:T(8,128)} copy(s32[512,64]{0,1:T(8,128)S(1)} %bitcast.3) | data formatting | bytes 262144
  31.0 6.2 %copy.19 = bf16[512,64,256]{2,1,0:T(8,128)(2,1)} copy(bf16[512,64,256]{2,1,0:T(8,128)(2,1)S(1)} %get-tuple-element.17) | data formatting | bytes 33554432
  37.2 0.0 copy-start
  37.2 6.2 %copy.20 = bf16[512,64,256]{2,1,0:T(8,128)(2,1)} copy(bf16[512,64,256]{2,1,0:T(8,128)(2,1)S(1)} %get-tuple-element.18) | data formatting | bytes 33554432
  43.4 0.0 collective-permute-done.2.from_d
  43.4 0.0 collective-permute-done.1.from_y
  43.4 0.0 collective-permute-done.from_x
  43.4 0.0 copy-done
  43.4 3.6 %shard_map.148 = f32[512,1152]{1,0:T(8,128)S(1)} custom-call(f32[64,1024]{1,0:T(8,128)S(1)} %get-tuple-element.10.own, f32[64,1024]{1,0:T(8,128)S(1)} %collective-permute-done.from_x, f32[64,1024]{1,0:T(8,128)S(1)} %collective-permute-done.1.from_y, f32[64,1024]{1,0:T(8,128)S(1)} %collective-permute-done.2.from_d, ...), custom_call_target="tpu_custom_call" | custom-call | flops 1200000000 | bytes 6000000 | tf_op jit(solution)/shard_map/pallas_call | solution.py:416
  47.0 1.1 %convert_element_type.3 = bf16[512,1152]{1,0:T(8,128)(2,1)} convert(f32[512,1152]{1,0:T(8,128)S(1)} %shard_map.148) | non-fusion elementwise | flops 589824 | bytes 3538944 | tf_op jit(solution)/shard_map/convert_element_type | solution.py:430
Async XLA Ops:
  26.9 16.5 %collective-permute-start.2 = (f32[64,1024]{1,0:T(8,128)S(1)}, f32[64,1024]{1,0:T(8,128)S(1)}, u32[]{:S(2)}, u32[]{:S(2)}) collective-permute-start(f32[64,1024]{1,0:T(8,128)S(1)} %get-tuple-element.10.own), channel_id=1, source_target_pairs={{0,6},{1,7},{2,4},{3,5},{4,2},{5,3},{6,0},{7,1}} | collective-permute-start | bytes 786440 | tf_op jit(solution)/shard_map/ppermute | solution.py:415
  27.7 15.7 %collective-permute-start.1 = (f32[64,1024]{1,0:T(8,128)S(1)}, f32[64,1024]{1,0:T(8,128)S(1)}, u32[]{:S(2)}, u32[]{:S(2)}) collective-permute-start(f32[64,1024]{1,0:T(8,128)S(1)} %get-tuple-element.10.own), channel_id=1, source_target_pairs={{0,4},{1,5},{2,6},{3,7},{4,0},{5,1},{6,2},{7,3}} | collective-permute-start | bytes 786440 | tf_op jit(solution)/shard_map/ppermute | solution.py:415
  29.4 14.0 %collective-permute-start = (f32[64,1024]{1,0:T(8,128)S(1)}, f32[64,1024]{1,0:T(8,128)S(1)}, u32[]{:S(2)}, u32[]{:S(2)}) collective-permute-start(f32[64,1024]{1,0:T(8,128)S(1)} %get-tuple-element.10.own), channel_id=1, source_target_pairs={{0,2},{1,3},{2,0},{3,1},{4,6},{5,7},{6,4},{7,5}} | collective-permute-start | bytes 786440 | tf_op jit(solution)/shard_map/ppermute | solution.py:415
  37.2 6.2 %copy-start = (bf16[1152]{0:T(1024)(128)(2,1)S(1)}, bf16[1152]{0:T(1024)(128)(2,1)}, u32[]{:S(2)}) copy-start(bf16[1152]{0:T(1024)(128)(2,1)} %b_ref.1) | copy-start | bytes 6916

commit v13 on v12

--- a/solution.py
+++ b/solution.py
@@ -151,7 +151,7 @@
         self.pick = [(self.sub // 2) == cc for cc in range(4)]
         self.iotas = [(lax.broadcasted_iota(jnp.int32, (16, HEAD_DIM), 0) + 16 * t).astype(F32).astype(BF16) for t in range(SLOTS // 16)]
 
-    def rows(self, base):
+    def rows(self, base, count):
         kbuf, vbuf, q_v, kn_v, vn_v, p_col, js_col, part = self.refs
         pick, iotas, lane, slot_c = self.pick, self.iotas, self.lane, self.slot_c
 
@@ -207,7 +207,7 @@
             for h in range(HEADS):
                 part[rows, h * HEAD_DIM:(h + 1) * HEAD_DIM] = o[h * GROUP:(h + 1) * GROUP, :]
 
-        starts = [al(base + g * GROUP, GROUP) for g in range(HALF // GROUP)]
+        starts = [al(base + g * GROUP, GROUP) for g in range(count // GROUP)]
         cs = [scores(r0) for r0 in starts]
         ps = [soften(r0, c) for r0, c in zip(starts, cs)]
         for r0, e in zip(starts, ps):
@@ -303,14 +303,23 @@
 
         for cp in kv_in(c):
             cp.wait()
-        att.rows(c * CHUNK + HALF * (1 - p.core))
+        @pl.when(c < NCHUNK - 1)
+        def _():
+            att.rows(c * CHUNK, CHUNK)
+
+        @pl.when(c == NCHUNK - 1)
+        def _():
+            att.rows(c * CHUNK + HALF * (1 - p.core), HALF)
 
         @pl.when(c == 0)
         def _():
             pl.semaphore_wait(barrier, 4)
 
         red.pair_copy(c).start()
-        att.rows(c * CHUNK + HALF * p.core)
+
+        @pl.when(c == NCHUNK - 1)
+        def _():
+            att.rows(c * CHUNK + HALF * p.core, HALF)
 
     lags = ((0, attend), (1, red.pair_step), (6, red.chip_step))
 
@@ -352,7 +361,7 @@
         xin = jnp.concatenate([x_v[pl.ds(r, 8), :].astype(F32) for r in rows], axis=0)
         y = xin + jnp.dot(o, wo_v[...], preferred_element_type=F32) + bias
         for t, r in enumerate(rows):
-            out_ref[pl.ds(r, 8), :] = y[8 * t:8 * t + 8, :]
+            out_ref[pl.ds(r, 8), :] = y[8 * t:8 * t + 8, :].astype(BF16)
 
     emit(refs, p.core)
     for n in range(4):
@@ -415,7 +424,7 @@
         far = [lax.ppermute(own, 'kv', [(i, i ^ m) for i in range(8)]) for m in (2, 4, 6)]
         x_out = pl.pallas_call(
             out_kernel,
-            out_shape=jax.ShapeDtypeStruct((BATCH, D_MODEL), F32),
+            out_shape=jax.ShapeDtypeStruct((BATCH, D_MODEL), BF16),
             in_specs=[vmem] * 7,
             out_specs=vmem,
             scratch_shapes=[
@@ -427,7 +436,7 @@
             cost_estimate=pl.CostEstimate(flops=1_200_000_000, bytes_accessed=6_000_000, transcendentals=0),
             compiler_params=pltpu.CompilerParams(collective_id=1, has_side_effects=True, vmem_limit_bytes=18 * 1024 * 1024),
         )(own, *far, x_keep, wo_keep, b_o)
-        return x_out.astype(BF16), k_out, v_out, sp_t.T
+        return x_out, k_out, v_out, sp_t.T
 
     return jax.shard_map(
         local_step,

time: 48.3 us -> 47.7 us (0.988)
  other arithmetic: 1.14 us -> 0 us
  local copies, waits for them, and re-layouts: 13 us -> 14 us
  Pallas kernels: 29.9 us -> 29.4 us
    convert_element_type x1 -> x0, other arithmetic: 1.14 us -> none  [local_step(): return (x_out.astype(BF16), k_out, v_out, sp_t.T)]
    unnamed x5 -> x6, local copies, waits for them, and re-layouts: 13 us -> 14 us
where the time goes in v13:
time: 47.7 us; the launch traced here: 47.6 us
  Pallas kernels  29.4 us (62%)
  local copies, waits for them, and re-layouts  14 us (29%)
  starting transfers between devices  3.51 us (7%)
  between operations  0.67 us (1%)
    pallas_call x1, Pallas kernels, local_step(): pl.pallas_call(step_kernel, out_shape=(jax.ShapeDtypeStruct((BATCH // 8,...  25.8 us
    unnamed x6, local copies, waits for them, and re-layouts  14 us
    pallas_call x1, Pallas kernels, local_step(): pl.pallas_call(out_kernel, out_shape=jax.ShapeDtypeStruct((BATCH, D_MODEL...  3.63 us
    ppermute x3, starting transfers between devices, local_step(): lax.ppermute(own, 'kv', [(i, i ^ m) for i in range(8)])  3.51 us
  transfers between devices with their start and end apart: 3, of which 0 were waited for; matrix products, arithmetic and copies ran while one was open for 27% of the time, Pallas kernels for 0%

profile of v13, /device:TPU:0, one launch (start us, length us, event | category | flops | bytes accessed | tf_op | source)
XLA Modules:
  0.0 47.6 jit_solution(2085918356018946892)
XLA Ops:
  0.6 25.8 %shard_map.147 = (f32[64,1024]{1,0:T(8,128)S(1)}, bf16[512,64,256]{2,1,0:T(8,128)(2,1)S(1)}, bf16[512,64,256]{2,1,0:T(8,128)(2,1)S(1)}, s32[64,512]{1,0:T(8,128)...) custom-call(s32[1,512]{1,0:T(1,128)} %bitcast.5, f32[1,128]{1,0:T(1,128)} %constant.2.clone.freq_hbm, ...), custom_call_target="tpu_custom_call" | custom-call | flops 30000001024 | bytes 40000000 | tf_op jit(solution)/shard_map/pallas_call | solution.py:387
  26.4 1.0 %collective-permute-start.2 = (f32[64,1024]{1,0:T(8,128)S(1)}, f32[64,1024]{1,0:T(8,128)S(1)}, u32[]{:S(2)}, u32[]{:S(2)}) collective-permute-start(f32[64,1024]{1,0:T(8,128)S(1)} %get-tuple-element.10.own), channel_id=1, source_target_pairs={{0,6},{1,7},{2,4},{3,5},{4,2},{5,3},{6,0},{7,1}} | collective-permute-start | bytes 786440 | tf_op jit(solution)/shard_map/ppermute | solution.py:424
  27.5 1.5 %collective-permute-start.1 = (f32[64,1024]{1,0:T(8,128)S(1)}, f32[64,1024]{1,0:T(8,128)S(1)}, u32[]{:S(2)}, u32[]{:S(2)}) collective-permute-start(f32[64,1024]{1,0:T(8,128)S(1)} %get-tuple-element.10.own), channel_id=1, source_target_pairs={{0,4},{1,5},{2,6},{3,7},{4,0},{5,1},{6,2},{7,3}} | collective-permute-start | bytes 786440 | tf_op jit(solution)/shard_map/ppermute | solution.py:424
  28.9 1.0 %collective-permute-start = (f32[64,1024]{1,0:T(8,128)S(1)}, f32[64,1024]{1,0:T(8,128)S(1)}, u32[]{:S(2)}, u32[]{:S(2)}) collective-permute-start(f32[64,1024]{1,0:T(8,128)S(1)} %get-tuple-element.10.own), channel_id=1, source_target_pairs={{0,2},{1,3},{2,0},{3,1},{4,6},{5,7},{6,4},{7,5}} | collective-permute-start | bytes 786440 | tf_op jit(solution)/shard_map/ppermute | solution.py:424
  29.9 0.7 %copy.22 = s32[512,64]{0,1:T(8,128)} copy(s32[512,64]{0,1:T(8,128)S(1)} %bitcast.3) | data formatting | bytes 262144
  30.6 6.2 %copy.20 = bf16[512,64,256]{2,1,0:T(8,128)(2,1)} copy(bf16[512,64,256]{2,1,0:T(8,128)(2,1)S(1)} %get-tuple-element.17) | data formatting | bytes 33554432
  36.7 0.0 copy-start
  36.7 6.2 %copy.21 = bf16[512,64,256]{2,1,0:T(8,128)(2,1)} copy(bf16[512,64,256]{2,1,0:T(8,128)(2,1)S(1)} %get-tuple-element.18) | data formatting | bytes 33554432
  42.9 0.0 collective-permute-done.2.from_d
  42.9 0.0 collective-permute-done.1.from_y
  42.9 0.0 collective-permute-done.from_x
  42.9 0.0 copy-done
  42.9 3.6 %shard_map.148 = bf16[512,1152]{1,0:T(8,128)(2,1)S(1)} custom-call(f32[64,1024]{1,0:T(8,128)S(1)} %get-tuple-element.10.own, f32[64,1024]{1,0:T(8,128)S(1)} %collective-permute-done.from_x, f32[64,1024]{1,0:T(8,128)S(1)} %collective-permute-done.1.from_y, f32[64,1024]{1,0:T(8,128)S(1)} %collective-permute-done.2.from_d, ...), custom_call_target="tpu_custom_call" | custom-call | flops 1200000000 | bytes 6000000 | tf_op jit(solution)/shard_map/pallas_call | solution.py:425
  46.6 1.0 %copy.23 = bf16[512,1152]{1,0:T(8,128)(2,1)} copy(bf16[512,1152]{1,0:T(8,128)(2,1)S(1)} %shard_map.148) | data formatting | bytes 2359296
Async XLA Ops:
  26.4 16.5 %collective-permute-start.2 = (f32[64,1024]{1,0:T(8,128)S(1)}, f32[64,1024]{1,0:T(8,128)S(1)}, u32[]{:S(2)}, u32[]{:S(2)}) collective-permute-start(f32[64,1024]{1,0:T(8,128)S(1)} %get-tuple-element.10.own), channel_id=1, source_target_pairs={{0,6},{1,7},{2,4},{3,5},{4,2},{5,3},{6,0},{7,1}} | collective-permute-start | bytes 786440 | tf_op jit(solution)/shard_map/ppermute | solution.py:424
  27.5 15.4 %collective-permute-start.1 = (f32[64,1024]{1,0:T(8,128)S(1)}, f32[64,1024]{1,0:T(8,128)S(1)}, u32[]{:S(2)}, u32[]{:S(2)}) collective-permute-start(f32[64,1024]{1,0:T(8,128)S(1)} %get-tuple-element.10.own), channel_id=1, source_target_pairs={{0,4},{1,5},{2,6},{3,7},{4,0},{5,1},{6,2},{7,3}} | collective-permute-start | bytes 786440 | tf_op jit(solution)/shard_map/ppermute | solution.py:424
  28.9 14.0 %collective-permute-start = (f32[64,1024]{1,0:T(8,128)S(1)}, f32[64,1024]{1,0:T(8,128)S(1)}, u32[]{:S(2)}, u32[]{:S(2)}) collective-permute-start(f32[64,1024]{1,0:T(8,128)S(1)} %get-tuple-element.10.own), channel_id=1, source_target_pairs={{0,2},{1,3},{2,0},{3,1},{4,6},{5,7},{6,4},{7,5}} | collective-permute-start | bytes 786440 | tf_op jit(solution)/shard_map/ppermute | solution.py:424
  36.7 6.2 %copy-start = (bf16[1152]{0:T(1024)(128)(2,1)S(1)}, bf16[1152]{0:T(1024)(128)(2,1)}, u32[]{:S(2)}) copy-start(bf16[1152]{0:T(1024)(128)(2,1)} %b_ref.1) | copy-start | bytes 6916

commit v14 on v13

--- a/solution.py
+++ b/solution.py
@@ -30,7 +30,7 @@
 STEP = 64
 CHUNK = 64
 NCHUNK = BATCH // CHUNK
-ROWS = 512
+ROWS = 256
 
 
 def sin_cos(theta):
@@ -355,18 +355,20 @@
         copy(n).start()
     bias = b_ref[...].astype(F32).reshape(1, D_MODEL)
 
-    def emit(blocks, core):
-        rows = [al(t * CHUNK + p.eighth(n, core)) for n in range(4) for t in range(NCHUNK)]
+    def emit(blocks, chips, core):
+        rows = [al(t * CHUNK + p.eighth(n, core)) for n in chips for t in range(NCHUNK)]
         o = jnp.concatenate([t[...].astype(BF16) for t in blocks], axis=0)
         xin = jnp.concatenate([x_v[pl.ds(r, 8), :].astype(F32) for r in rows], axis=0)
         y = xin + jnp.dot(o, wo_v[...], preferred_element_type=F32) + bias
         for t, r in enumerate(rows):
             out_ref[pl.ds(r, 8), :] = y[8 * t:8 * t + 8, :].astype(BF16)
 
-    emit(refs, p.core)
-    for n in range(4):
-        copy(n).wait_recv()
-    emit([g.at[n] for n in range(4)], 1 - p.core)
+    emit(refs, range(4), p.core)
+    for first in (0, 2):
+        pair = (first, first + 1)
+        for n in pair:
+            copy(n).wait_recv()
+        emit([g.at[n] for n in pair], pair, 1 - p.core)
     for n in range(4):
         copy(n).wait_send()
 

time: 47.7 us -> 47 us (0.985)
  Pallas kernels: 29.4 us -> 28.7 us
  transfers between devices with their start and end apart: 3 -> 3, of which waited for: 0 -> 0; matrix products, arithmetic and copies ran while one was open for 27% -> 28% of each run, Pallas kernels for 0% -> 0%
where the time goes in v14:
time: 47 us; the launch traced here: 46.9 us
  Pallas kernels  28.7 us (61%)
  local copies, waits for them, and re-layouts  14 us (30%)
  starting transfers between devices  3.51 us (7%)
  between operations  0.67 us (1%)
    pallas_call x1, Pallas kernels, local_step(): pl.pallas_call(step_kernel, out_shape=(jax.ShapeDtypeStruct((BATCH // 8,...  25.4 us
    unnamed x6, local copies, waits for them, and re-layouts  14 us
    ppermute x3, starting transfers between devices, local_step(): lax.ppermute(own, 'kv', [(i, i ^ m) for i in range(8)])  3.51 us
    pallas_call x1, Pallas kernels, local_step(): pl.pallas_call(out_kernel, out_shape=jax.ShapeDtypeStruct((BATCH, D_MODEL...  3.3 us
  transfers between devices with their start and end apart: 3, of which 0 were waited for; matrix products, arithmetic and copies ran while one was open for 28% of the time, Pallas kernels for 0%

profile of v14, /device:TPU:0, one launch (start us, length us, event | category | flops | bytes accessed | tf_op | source)
XLA Modules:
  0.0 46.9 jit_solution(17557724224196180249)
XLA Ops:
  0.6 25.4 %shard_map.147 = (f32[64,1024]{1,0:T(8,128)S(1)}, bf16[512,64,256]{2,1,0:T(8,128)(2,1)S(1)}, bf16[512,64,256]{2,1,0:T(8,128)(2,1)S(1)}, s32[64,512]{1,0:T(8,128)...) custom-call(s32[1,512]{1,0:T(1,128)} %bitcast.5, f32[1,128]{1,0:T(1,128)} %constant.2.clone.freq_hbm, ...), custom_call_target="tpu_custom_call" | custom-call | flops 30000001024 | bytes 40000000 | tf_op jit(solution)/shard_map/pallas_call | solution.py:389
  26.1 1.0 %collective-permute-start.2 = (f32[64,1024]{1,0:T(8,128)S(1)}, f32[64,1024]{1,0:T(8,128)S(1)}, u32[]{:S(2)}, u32[]{:S(2)}) collective-permute-start(f32[64,1024]{1,0:T(8,128)S(1)} %get-tuple-element.10.own), channel_id=1, source_target_pairs={{0,6},{1,7},{2,4},{3,5},{4,2},{5,3},{6,0},{7,1}} | collective-permute-start | bytes 786440 | tf_op jit(solution)/shard_map/ppermute | solution.py:426
  27.1 1.5 %collective-permute-start.1 = (f32[64,1024]{1,0:T(8,128)S(1)}, f32[64,1024]{1,0:T(8,128)S(1)}, u32[]{:S(2)}, u32[]{:S(2)}) collective-permute-start(f32[64,1024]{1,0:T(8,128)S(1)} %get-tuple-element.10.own), channel_id=1, source_target_pairs={{0,4},{1,5},{2,6},{3,7},{4,0},{5,1},{6,2},{7,3}} | collective-permute-start | bytes 786440 | tf_op jit(solution)/shard_map/ppermute | solution.py:426
  28.6 1.0 %collective-permute-start = (f32[64,1024]{1,0:T(8,128)S(1)}, f32[64,1024]{1,0:T(8,128)S(1)}, u32[]{:S(2)}, u32[]{:S(2)}) collective-permute-start(f32[64,1024]{1,0:T(8,128)S(1)} %get-tuple-element.10.own), channel_id=1, source_target_pairs={{0,2},{1,3},{2,0},{3,1},{4,6},{5,7},{6,4},{7,5}} | collective-permute-start | bytes 786440 | tf_op jit(solution)/shard_map/ppermute | solution.py:426
  29.6 0.7 %copy.22 = s32[512,64]{0,1:T(8,128)} copy(s32[512,64]{0,1:T(8,128)S(1)} %bitcast.3) | data formatting | bytes 262144
  30.2 6.2 %copy.20 = bf16[512,64,256]{2,1,0:T(8,128)(2,1)} copy(bf16[512,64,256]{2,1,0:T(8,128)(2,1)S(1)} %get-tuple-element.17) | data formatting | bytes 33554432
  36.4 0.0 copy-start
  36.4 6.2 %copy.21 = bf16[512,64,256]{2,1,0:T(8,128)(2,1)} copy(bf16[512,64,256]{2,1,0:T(8,128)(2,1)S(1)} %get-tuple-element.18) | data formatting | bytes 33554432
  42.5 0.0 collective-permute-done.2.from_d
  42.5 0.0 collective-permute-done.1.from_y
  42.5 0.0 collective-permute-done.from_x
  42.6 0.0 copy-done
  42.6 3.3 %shard_map.148 = bf16[512,1152]{1,0:T(8,128)(2,1)S(1)} custom-call(f32[64,1024]{1,0:T(8,128)S(1)} %get-tuple-element.10.own, f32[64,1024]{1,0:T(8,128)S(1)} %collective-permute-done.from_x, f32[64,1024]{1,0:T(8,128)S(1)} %collective-permute-done.1.from_y, f32[64,1024]{1,0:T(8,128)S(1)} %collective-permute-done.2.from_d, ...), custom_call_target="tpu_custom_call" | custom-call | flops 1200000000 | bytes 6000000 | tf_op jit(solution)/shard_map/pallas_call | solution.py:427
  45.9 1.0 %copy.23 = bf16[512,1152]{1,0:T(8,128)(2,1)} copy(bf16[512,1152]{1,0:T(8,128)(2,1)S(1)} %shard_map.148) | data formatting | bytes 2359296
Async XLA Ops:
  26.1 16.5 %collective-permute-start.2 = (f32[64,1024]{1,0:T(8,128)S(1)}, f32[64,1024]{1,0:T(8,128)S(1)}, u32[]{:S(2)}, u32[]{:S(2)}) collective-permute-start(f32[64,1024]{1,0:T(8,128)S(1)} %get-tuple-element.10.own), channel_id=1, source_target_pairs={{0,6},{1,7},{2,4},{3,5},{4,2},{5,3},{6,0},{7,1}} | collective-permute-start | bytes 786440 | tf_op jit(solution)/shard_map/ppermute | solution.py:426
  27.1 15.4 %collective-permute-start.1 = (f32[64,1024]{1,0:T(8,128)S(1)}, f32[64,1024]{1,0:T(8,128)S(1)}, u32[]{:S(2)}, u32[]{:S(2)}) collective-permute-start(f32[64,1024]{1,0:T(8,128)S(1)} %get-tuple-element.10.own), channel_id=1, source_target_pairs={{0,4},{1,5},{2,6},{3,7},{4,0},{5,1},{6,2},{7,3}} | collective-permute-start | bytes 786440 | tf_op jit(solution)/shard_map/ppermute | solution.py:426
  28.6 14.0 %collective-permute-start = (f32[64,1024]{1,0:T(8,128)S(1)}, f32[64,1024]{1,0:T(8,128)S(1)}, u32[]{:S(2)}, u32[]{:S(2)}) collective-permute-start(f32[64,1024]{1,0:T(8,128)S(1)} %get-tuple-element.10.own), channel_id=1, source_target_pairs={{0,2},{1,3},{2,0},{3,1},{4,6},{5,7},{6,4},{7,5}} | collective-permute-start | bytes 786440 | tf_op jit(solution)/shard_map/ppermute | solution.py:426
  36.4 6.2 %copy-start = (bf16[1152]{0:T(1024)(128)(2,1)S(1)}, bf16[1152]{0:T(1024)(128)(2,1)}, u32[]{:S(2)}) copy-start(bf16[1152]{0:T(1024)(128)(2,1)} %b_ref.1) | copy-start | bytes 6916

commit v15 on v14

--- a/solution.py
+++ b/solution.py
@@ -286,11 +286,6 @@
     att = Attention(off, kbuf, vbuf, q_v, kn_v, vn_v, p_col, js_col, part)
 
     def attend(c):
-        @pl.when(c == NCHUNK - 1)
-        def _():
-            w_in(4).start()
-            w_in(8).start()
-
         @pl.when(c % (ROWS // CHUNK) == 0)
         def _():
             rows = pl.ds(al(c * CHUNK, ROWS), ROWS)
@@ -303,6 +298,11 @@
 
         for cp in kv_in(c):
             cp.wait()
+
+        @pl.when(c == NCHUNK - 1)
+        def _():
+            w_in(4).start()
+            w_in(8).start()
         @pl.when(c < NCHUNK - 1)
         def _():
             att.rows(c * CHUNK, CHUNK)

time: 47 us -> 47 us (level)
  no operation moved by 1% of the time
where the time goes in v15:
time: 47 us; the launch traced here: 46.9 us
  Pallas kernels  28.7 us (61%)
  local copies, waits for them, and re-layouts  14 us (30%)
  starting transfers between devices  3.51 us (7%)
  between operations  0.67 us (1%)
    pallas_call x1, Pallas kernels, local_step(): pl.pallas_call(step_kernel, out_shape=(jax.ShapeDtypeStruct((BATCH // 8,...  25.4 us
    unnamed x6, local copies, waits for them, and re-layouts  14 us
    ppermute x3, starting transfers between devices, local_step(): lax.ppermute(own, 'kv', [(i, i ^ m) for i in range(8)])  3.51 us
    pallas_call x1, Pallas kernels, local_step(): pl.pallas_call(out_kernel, out_shape=jax.ShapeDtypeStruct((BATCH, D_MODEL...  3.29 us
  transfers between devices with their start and end apart: 3, of which 0 were waited for; matrix products, arithmetic and copies ran while one was open for 28% of the time, Pallas kernels for 0%

profile of v15, /device:TPU:0, one launch (start us, length us, event | category | flops | bytes accessed | tf_op | source)
XLA Modules:
  0.0 46.9 jit_solution(2437176138758915702)
XLA Ops:
  0.6 25.4 %shard_map.147 = (f32[64,1024]{1,0:T(8,128)S(1)}, bf16[512,64,256]{2,1,0:T(8,128)(2,1)S(1)}, bf16[512,64,256]{2,1,0:T(8,128)(2,1)S(1)}, s32[64,512]{1,0:T(8,128)...) custom-call(s32[1,512]{1,0:T(1,128)} %bitcast.5, f32[1,128]{1,0:T(1,128)} %constant.2.clone.freq_hbm, ...), custom_call_target="tpu_custom_call" | custom-call | flops 30000001024 | bytes 40000000 | tf_op jit(solution)/shard_map/pallas_call | solution.py:389
  26.0 1.0 %collective-permute-start.2 = (f32[64,1024]{1,0:T(8,128)S(1)}, f32[64,1024]{1,0:T(8,128)S(1)}, u32[]{:S(2)}, u32[]{:S(2)}) collective-permute-start(f32[64,1024]{1,0:T(8,128)S(1)} %get-tuple-element.10.own), channel_id=1, source_target_pairs={{0,6},{1,7},{2,4},{3,5},{4,2},{5,3},{6,0},{7,1}} | collective-permute-start | bytes 786440 | tf_op jit(solution)/shard_map/ppermute | solution.py:426
  27.1 1.5 %collective-permute-start.1 = (f32[64,1024]{1,0:T(8,128)S(1)}, f32[64,1024]{1,0:T(8,128)S(1)}, u32[]{:S(2)}, u32[]{:S(2)}) collective-permute-start(f32[64,1024]{1,0:T(8,128)S(1)} %get-tuple-element.10.own), channel_id=1, source_target_pairs={{0,4},{1,5},{2,6},{3,7},{4,0},{5,1},{6,2},{7,3}} | collective-permute-start | bytes 786440 | tf_op jit(solution)/shard_map/ppermute | solution.py:426
  28.6 1.0 %collective-permute-start = (f32[64,1024]{1,0:T(8,128)S(1)}, f32[64,1024]{1,0:T(8,128)S(1)}, u32[]{:S(2)}, u32[]{:S(2)}) collective-permute-start(f32[64,1024]{1,0:T(8,128)S(1)} %get-tuple-element.10.own), channel_id=1, source_target_pairs={{0,2},{1,3},{2,0},{3,1},{4,6},{5,7},{6,4},{7,5}} | collective-permute-start | bytes 786440 | tf_op jit(solution)/shard_map/ppermute | solution.py:426
  29.6 0.7 %copy.22 = s32[512,64]{0,1:T(8,128)} copy(s32[512,64]{0,1:T(8,128)S(1)} %bitcast.3) | data formatting | bytes 262144
  30.2 6.2 %copy.20 = bf16[512,64,256]{2,1,0:T(8,128)(2,1)} copy(bf16[512,64,256]{2,1,0:T(8,128)(2,1)S(1)} %get-tuple-element.17) | data formatting | bytes 33554432
  36.4 0.0 copy-start
  36.4 6.2 %copy.21 = bf16[512,64,256]{2,1,0:T(8,128)(2,1)} copy(bf16[512,64,256]{2,1,0:T(8,128)(2,1)S(1)} %get-tuple-element.18) | data formatting | bytes 33554432
  42.5 0.0 collective-permute-done.2.from_d
  42.5 0.0 collective-permute-done.1.from_y
  42.5 0.0 collective-permute-done.from_x
  42.5 0.0 copy-done
  42.6 3.3 %shard_map.148 = bf16[512,1152]{1,0:T(8,128)(2,1)S(1)} custom-call(f32[64,1024]{1,0:T(8,128)S(1)} %get-tuple-element.10.own, f32[64,1024]{1,0:T(8,128)S(1)} %collective-permute-done.from_x, f32[64,1024]{1,0:T(8,128)S(1)} %collective-permute-done.1.from_y, f32[64,1024]{1,0:T(8,128)S(1)} %collective-permute-done.2.from_d, ...), custom_call_target="tpu_custom_call" | custom-call | flops 1200000000 | bytes 6000000 | tf_op jit(solution)/shard_map/pallas_call | solution.py:427
  45.9 1.0 %copy.23 = bf16[512,1152]{1,0:T(8,128)(2,1)} copy(bf16[512,1152]{1,0:T(8,128)(2,1)S(1)} %shard_map.148) | data formatting | bytes 2359296
Async XLA Ops:
  26.0 16.5 %collective-permute-start.2 = (f32[64,1024]{1,0:T(8,128)S(1)}, f32[64,1024]{1,0:T(8,128)S(1)}, u32[]{:S(2)}, u32[]{:S(2)}) collective-permute-start(f32[64,1024]{1,0:T(8,128)S(1)} %get-tuple-element.10.own), channel_id=1, source_target_pairs={{0,6},{1,7},{2,4},{3,5},{4,2},{5,3},{6,0},{7,1}} | collective-permute-start | bytes 786440 | tf_op jit(solution)/shard_map/ppermute | solution.py:426
  27.1 15.4 %collective-permute-start.1 = (f32[64,1024]{1,0:T(8,128)S(1)}, f32[64,1024]{1,0:T(8,128)S(1)}, u32[]{:S(2)}, u32[]{:S(2)}) collective-permute-start(f32[64,1024]{1,0:T(8,128)S(1)} %get-tuple-element.10.own), channel_id=1, source_target_pairs={{0,4},{1,5},{2,6},{3,7},{4,0},{5,1},{6,2},{7,3}} | collective-permute-start | bytes 786440 | tf_op jit(solution)/shard_map/ppermute | solution.py:426
  28.6 13.9 %collective-permute-start = (f32[64,1024]{1,0:T(8,128)S(1)}, f32[64,1024]{1,0:T(8,128)S(1)}, u32[]{:S(2)}, u32[]{:S(2)}) collective-permute-start(f32[64,1024]{1,0:T(8,128)S(1)} %get-tuple-element.10.own), channel_id=1, source_target_pairs={{0,2},{1,3},{2,0},{3,1},{4,6},{5,7},{6,4},{7,5}} | collective-permute-start | bytes 786440 | tf_op jit(solution)/shard_map/ppermute | solution.py:426
  36.4 6.2 %copy-start = (bf16[1152]{0:T(1024)(128)(2,1)S(1)}, bf16[1152]{0:T(1024)(128)(2,1)}, u32[]{:S(2)}) copy-start(bf16[1152]{0:T(1024)(128)(2,1)} %b_ref.1) | copy-start | bytes 6916
